TPU v7x, 32 devices: a whole 2x2x4 slice. The times are simulated.
32 devices in a mesh: gx: 4 (over y, core), gy: 2 (over x), gz: 4 (over z).
Axes of the slice: x: 2, y: 2, z: 4, core: 2. Of those that a mesh axis runs over, the one named last changes fastest.
Arguments:
- old_basis: float32 [4, 32, 32, 512], P(None, 'gx', 'gy', 'gz'), may hold values from -4 to 4, as said below
- previous: float32 [4, 32, 32, 512], P(None, 'gx', 'gy', 'gz'), as said below
- incoming: float32 [4, 32, 32, 512], P(None, 'gx', 'gy', 'gz'), may hold values from -6 to 6
- coefficient: float32 [32, 32, 512], P('gx', 'gy', 'gz'), may hold values from 0.5 to 4
Outputs:
- orthonormal: float32 [4, 32, 32, 512], P(None, 'gx', 'gy', 'gz')
- projection: float32 [4, 4], replicated
- triangle: float32 [4, 4], replicated
- preconditioned: float32 [4, 32, 32, 512], P(None, 'gx', 'gy', 'gz')
- operated: float32 [4, 32, 32, 512], P(None, 'gx', 'gy', 'gz')
Inputs may be any that keep to these rules, and one draw needn't show every extreme that they name: `old_basis`: entries of order one; the basis vectors are independent, so every Gram matrix formed from them is well conditioned. `previous`: entries of order one; each vector has a part outside the span of old_basis of norm of order one under the inner product.
All inputs are finite; a program needn't handle non-finite values.
Results may differ from a plain program's by a relative error of at most 0.0003.
Values sent between devices are 32-bit elements; how exact they have to be, the bound alone decides.
No kernel may reach another device: no remote copies, remote signals or barrier semaphores. Data moves between devices by JAX's collectives and lax.ppermute only.
A program may use at most 64 MiB of HBM per device.

v0:
```python
import jax
import jax.numpy as jnp
from jax import lax
from jax.sharding import PartitionSpec as P

LEVELS = 6
COARSE_SWEEPS = 4


OMEGA = 0.8
HIGH = lax.Precision.HIGHEST


def with_halo(shard, sides, width):
    for axis, dim in sides:
        count, length = (lax.axis_size(axis), shard.shape[dim])
        up = [(i, (i + 1) % count) for i in range(count - 1)]
        down = [(j, i) for i, j in up]
        last = lax.slice_in_dim(shard, length - width, length, axis=dim)
        leading = lax.slice_in_dim(shard, 0, width, axis=dim)
        before = lax.ppermute(last, axis, up)
        after = lax.ppermute(leading, axis, down)
        shard = jnp.concatenate([before, shard, after], axis=dim)
    return shard


def stencil(extended, coeffs, factor):
    center = extended[:, 1:-1, 1:-1, 1:-1]
    total = extended[:, 2:, 1:-1, 1:-1] + extended[:, :-2, 1:-1, 1:-1]
    total = total + extended[:, 1:-1, 2:, 1:-1] + extended[:, 1:-1, :-2, 1:-1]
    total = total + extended[:, 1:-1, 1:-1, 2:] + extended[:, 1:-1, 1:-1, :-2]
    return factor * coeffs * (6.0 * center - total)


def zero_margin(field):
    return jnp.pad(field, ((0, 0), (1, 1), (1, 1), (1, 1)))


def with_faces(field):
    return with_halo(field, (("gx", 1), ("gy", 2), ("gz", 3)), 1)


def restrict(field):
    depth, size_a, size_b, size_c = field.shape
    return field.reshape(depth, size_a // 2, 2, size_b // 2, 2, size_c // 2, 2).mean(axis=(2, 4, 6))


def prolong(field):
    return jnp.repeat(jnp.repeat(jnp.repeat(field, 2, axis=1), 2, axis=2), 2, axis=3)


def whole_cycle(source, coeff_list, level):
    coeffs = coeff_list[level]
    factor = 0.25**level
    diagonal = 6.0 * factor * coeffs
    iterate = OMEGA * source / diagonal
    if level == LEVELS - 1:
        for sweep in range(COARSE_SWEEPS - 1):
            iterate = (
                iterate
                + OMEGA * (source - stencil(zero_margin(iterate), coeffs, factor)) / diagonal
            )
        return iterate
    iterate = iterate + OMEGA * (source - stencil(zero_margin(iterate), coeffs, factor)) / diagonal
    residue = source - stencil(zero_margin(iterate), coeffs, factor)
    iterate = iterate + prolong(whole_cycle(restrict(residue), coeff_list, level + 1))
    iterate = iterate + OMEGA * (source - stencil(zero_margin(iterate), coeffs, factor)) / diagonal
    return iterate


def agglomerate(source, coeffs, start_level):
    vectors = source.shape[0]
    stacked = jnp.concatenate([source, coeffs[None]], axis=0)
    depth, size_a, size_b, size_c = stacked.shape
    flattened = stacked.reshape(depth, size_a * size_b * size_c)
    gathered = lax.all_gather(flattened, ("gx", "gy", "gz"), axis=1, tiled=True)
    count_x, count_y, count_z = (lax.axis_size("gx"), lax.axis_size("gy"), lax.axis_size("gz"))
    gathered = gathered.reshape(depth, count_x, count_y, count_z, size_a, size_b, size_c)
    gathered = gathered.transpose(0, 1, 4, 2, 5, 3, 6).reshape(
        depth, count_x * size_a, count_y * size_b, count_z * size_c
    )
    coarse_list = [gathered[vectors]]
    for level in range(LEVELS - 1 - start_level):
        coarse_list.append(restrict(coarse_list[-1][None])[0])
    solution = whole_cycle(gathered[:vectors], [None] * start_level + coarse_list, start_level)
    starts = (
        jnp.zeros((), jnp.int32),
        lax.axis_index("gx") * size_a,
        lax.axis_index("gy") * size_b,
        lax.axis_index("gz") * size_c,
    )
    return lax.dynamic_slice(solution, starts, (vectors, size_a, size_b, size_c))


def local_cycle(source, coeff_list, level, start_level):
    coeffs = coeff_list[level]
    if level == start_level:
        return agglomerate(source, coeffs, start_level)
    factor = 0.25**level
    diagonal = 6.0 * factor * coeffs
    vectors = source.shape[0]
    stacked = jnp.concatenate([source, coeffs[None]], axis=0)
    widened = with_halo(stacked, (("gx", 1), ("gy", 2), ("gz", 3)), 2)
    source_wide = widened[:vectors]
    coeff_wide = widened[vectors]
    safe_wide = jnp.where(coeff_wide > 0.0, coeff_wide, 1.0)
    sweep_one = OMEGA * source_wide / (6.0 * factor * safe_wide)
    inner_coeff = coeff_wide[1:-1, 1:-1, 1:-1]
    inner_safe = safe_wide[1:-1, 1:-1, 1:-1]
    sweep_two = sweep_one[:, 1:-1, 1:-1, 1:-1] + OMEGA * (
        source_wide[:, 1:-1, 1:-1, 1:-1] - stencil(sweep_one, inner_coeff, factor)
    ) / (6.0 * factor * inner_safe)
    iterate = sweep_two[:, 1:-1, 1:-1, 1:-1]
    residue = source - stencil(sweep_two, coeffs, factor)
    iterate = iterate + prolong(local_cycle(restrict(residue), coeff_list, level + 1, start_level))
    iterate = iterate + OMEGA * (source - stencil(with_faces(iterate), coeffs, factor)) / diagonal
    return iterate


def triangular_inverse(lower):
    order = lower.shape[0]
    identity = jnp.eye(order, dtype=lower.dtype)
    inverse = jnp.zeros_like(lower)
    for row in range(order):
        values = identity[row] - jnp.dot(lower[row, :row], inverse[:row], precision=HIGH)
        inverse = inverse.at[row].set(values / lower[row, row])
    return inverse


def per_device(old_basis, previous, incoming, coefficient):
    local_cells = old_basis.shape[1] * old_basis.shape[2] * old_basis.shape[3]
    total_cells = float(
        local_cells * lax.axis_size("gx") * lax.axis_size("gy") * lax.axis_size("gz")
    )
    basis_local = jnp.einsum("mxyz,jxyz->mj", old_basis, previous, precision=HIGH)
    projection = lax.psum(basis_local, ("gx", "gy", "gz")) / total_cells
    remainder = previous - jnp.einsum("mxyz,mj->jxyz", old_basis, projection, precision=HIGH)
    gram_local = jnp.einsum("ixyz,jxyz->ij", remainder, remainder, precision=HIGH)
    gram = lax.psum(gram_local, ("gx", "gy", "gz")) / total_cells
    start_level = LEVELS - 3
    coeff_list = [coefficient]
    for level in range(start_level):
        coeff_list.append(restrict(coeff_list[-1][None])[0])
    preconditioned = local_cycle(incoming, coeff_list, 0, start_level)
    operated = stencil(with_faces(preconditioned), coefficient, 1.0)
    lower = jnp.linalg.cholesky(gram)
    inverse = triangular_inverse(lower)
    orthonormal = jnp.einsum("ji,ixyz->jxyz", inverse, remainder, precision=HIGH)
    return (orthonormal, projection, lower.T, preconditioned, operated)


def solution(mesh):
    in_specs = (
        P(None, "gx", "gy", "gz"),
        P(None, "gx", "gy", "gz"),
        P(None, "gx", "gy", "gz"),
        P("gx", "gy", "gz"),
    )
    out_specs = (
        P(None, "gx", "gy", "gz"),
        P(),
        P(),
        P(None, "gx", "gy", "gz"),
        P(None, "gx", "gy", "gz"),
    )
    return jax.shard_map(
        per_device, mesh=mesh, in_specs=in_specs, out_specs=out_specs, check_vma=False
    )
```

profile of v0, /device:TPU:0, one launch (start us, length us, event | category | flops | bytes accessed | tf_op | source)
XLA Modules:
  0.0 369.1 jit_solution(2257460580880497571)
XLA Ops:
  5.3 4.0 %collective-permute-done.1 = f32[5,2,16,128]{3,2,1,0:T(8,128)S(1)} collective-permute-done((f32[5,2,16,128]{3,2,1,0:T(8,128)S(1)}, f32[5,2,16,128]{3,2,1,0:T(8,128)S(1)}, u32[]{:S(2)}, u32[]{:S(2)}) %collective-permute-start.1) | collective-permute-done | bytes 81952 | tf_op jit(solution)/shard_map/ppermute | solution.py:22
  17.5 5.5 %reshape_broadcast_in_dim.3 = f32[4,2,8,2,64,2]{5,4,3,2,1,0:T(8,128)} reshape(f32[8,16,128]{2,1,0:T(8,128)S(1)} %copy-done.1) | data formatting | bytes 131072 | tf_op jit(solution)/shard_map/reshape;broadcast_in_dim | solution.py:45
  31.8 44.3 %psum.14 = f32[4,4]{0,1:T(4,128)S(1)} all-reduce(f32[4,4]{0,1:T(4,128)S(1)} %convolution_bitcast_fusion.1), channel_id=1, replica_groups=mesh['gx'=4,'gy'=2,'gz'=4] {'gx','gy','gz'}, use_global_device_ids=true, to_apply=%region_0.0 | all-reduce | flops 16 | bytes 128 | tf_op jit(solution)/shard_map/psum | solution.py:136
  80.6 4.7 %copy.690 = f32[4,8,16,128]{0,3,2,1:T(8,128)} copy(f32[4,8,16,128]{3,2,1,0:T(8,128)S(1)} %fusion.35) | data formatting | bytes 524288 | tf_op jit(solution)/shard_map/sub | solution.py:114
  85.4 8.7 %reduce_sum.102 = f32[4,4,8,64]{0,3,2,1:T(8,128)S(1)} reduce(f32[4,4,2,8,2,64,2]{0,6,5,4,3,2,1:T(2,128)} %bitcast.130, f32[]{:T(128)} %constant.248.clone.1), dimensions={2,4,6}, to_apply=%region_4.0 | reduce | flops 57344 | bytes 294916 | tf_op jit(solution)/shard_map/reduce_sum | solution.py:45
  105.2 4.2 %collective-permute-done.9 = f32[5,8,2,64]{3,1,2,0:T(8,128)S(1)} collective-permute-done((f32[5,8,2,64]{3,1,2,0:T(8,128)S(1)}, f32[5,8,2,64]{3,1,2,0:T(8,128)S(1)}, u32[]{:S(2)}, u32[]{:S(2)}) %collective-permute-start.9) | collective-permute-done | bytes 20512 | tf_op jit(solution)/shard_map/ppermute | solution.py:22
  118.9 4.7 %collective-permute-done.11 = f32[5,8,12,2]{3,1,2,0:T(8,128)S(1)} collective-permute-done((f32[5,8,12,2]{3,1,2,0:T(8,128)S(1)}, f32[5,8,12,2]{3,1,2,0:T(8,128)S(1)}, u32[]{:S(2)}, u32[]{:S(2)}) %collective-permute-start.11) | collective-permute-done | bytes 3872 | tf_op jit(solution)/shard_map/ppermute | solution.py:22
  129.5 39.5 %psum.15 = f32[4,4]{0,1:T(4,128)S(1)} all-reduce(f32[4,4]{0,1:T(4,128)S(1)} %convolution_bitcast_fusion), channel_id=1, replica_groups=mesh['gx'=4,'gy'=2,'gz'=4] {'gx','gy','gz'}, use_global_device_ids=true, to_apply=%region_1.0 | all-reduce | flops 16 | bytes 128 | tf_op jit(solution)/shard_map/psum | solution.py:139
  169.0 4.2 %collective-permute-start.14 = (f32[5,6,2,32]{3,2,1,0:T(2,128)S(1)}, f32[5,6,2,32]{3,2,1,0:T(2,128)S(1)}, u32[]{:S(2)}, u32[]{:S(2)}) collective-permute-start(f32[5,6,2,32]{3,2,1,0:T(2,128)S(1)} %get-tuple-element.158), channel_id=1, source_target_pairs={{0,4},{1,5},{2,6},{3,7},{8,12},{9,13},{10,14},{11,15},{16,20},{17,... | collective-permute-start | bytes 23048 | tf_op jit(solution)/shard_map/ppermute | solution.py:21
  174.7 4.2 %collective-permute-done.15 = f32[5,6,2,32]{3,2,1,0:T(2,128)S(1)} collective-permute-done((f32[5,6,2,32]{3,2,1,0:T(2,128)S(1)}, f32[5,6,2,32]{3,2,1,0:T(2,128)S(1)}, u32[]{:S(2)}, u32[]{:S(2)}) %collective-permute-start.15) | collective-permute-done | bytes 7712 | tf_op jit(solution)/shard_map/ppermute | solution.py:22
  184.0 4.4 %collective-permute-done.17 = f32[5,6,8,2]{3,2,1,0:T(8,128)S(1)} collective-permute-done((f32[5,6,8,2]{3,2,1,0:T(8,128)S(1)}, f32[5,6,8,2]{3,2,1,0:T(8,128)S(1)}, u32[]{:S(2)}, u32[]{:S(2)}) %collective-permute-start.17) | collective-permute-done | bytes 1952 | tf_op jit(solution)/shard_map/ppermute | solution.py:22
  189.3 65.0 %all-gather = f32[32,32,5]{1,2,0:T(8,128)S(1)} all-gather(f32[1,32,5]{1,2,0:T(8,128)S(1)} %maximum_bitcast_fusion), channel_id=1, replica_groups=mesh['gx'=4,'gy'=2,'gz'=4] {'gx','gy','gz'}, dimensions={0}, use_global_device_ids=true | all-gather | bytes 21120 | tf_op jit(solution)/shard_map/all_gather | solution.py:76
  268.2 4.2 %collective-permute-done.20 = f32[4,4,1,32]{3,2,1,0:T(1,128)S(1)} collective-permute-done((f32[4,4,1,32]{3,2,1,0:T(1,128)S(1)}, f32[4,4,1,32]{3,2,1,0:T(1,128)S(1)}, u32[]{:S(2)}, u32[]{:S(2)}) %collective-permute-start.20) | collective-permute-done | bytes 2080 | tf_op jit(solution)/shard_map/ppermute | solution.py:22
  273.8 4.5 %collective-permute-start.23 = (f32[4,4,6,1]{3,1,2,0:T(4,128)S(1)}, f32[4,4,6,1]{3,1,2,0:T(4,128)S(1)}, u32[]{:S(2)}, u32[]{:S(2)}) collective-permute-start(f32[4,4,6,1]{3,1,2,0:T(4,128)S(1)} %get-tuple-element.163), channel_id=1, source_target_pairs={{0,1},{1,2},{2,3},{4,5},{5,6},{6,7},{8,9},{9,10},{10,11},{12,13},{... | collective-permute-start | bytes 1160 | tf_op jit(solution)/shard_map/ppermute | solution.py:21
  289.8 4.2 %collective-permute-done.26 = f32[4,6,1,64]{3,0,2,1:T(4,128)S(1)} collective-permute-done((f32[4,6,1,64]{3,0,2,1:T(4,128)S(1)}, f32[4,6,1,64]{3,0,2,1:T(4,128)S(1)}, u32[]{:S(2)}, u32[]{:S(2)}) %collective-permute-start.26) | collective-permute-done | bytes 6176 | tf_op jit(solution)/shard_map/ppermute | solution.py:22
  295.5 4.9 %collective-permute-start.29 = (f32[4,6,10,1]{3,0,2,1:T(4,128)S(1)}, f32[4,6,10,1]{3,0,2,1:T(4,128)S(1)}, u32[]{:S(2)}, u32[]{:S(2)}) collective-permute-start(f32[4,6,10,1]{3,0,2,1:T(4,128)S(1)} %get-tuple-element.147), channel_id=1, source_target_pairs={{0,1},{1,2},{2,3},{4,5},{5,6},{6,7},{8,9},{9,10},{10,11},{12,13},{... | collective-permute-start | bytes 2888 | tf_op jit(solution)/shard_map/ppermute | solution.py:21
  309.8 3.9 %collective-permute-start.31 = (f32[4,1,16,128]{3,2,1,0:T(8,128)S(1)}, f32[4,1,16,128]{3,2,1,0:T(8,128)S(1)}, u32[]{:S(2)}, u32[]{:S(2)}) collective-permute-start(f32[4,1,16,128]{3,2,1,0:T(8,128)S(1)} %get-tuple-element.128), channel_id=1, source_target_pairs={{0,8},{8,16},{16,24},{1,9},{9,17},{17,25},{2,10},{10,18},{18,26},{... | collective-permute-start | bytes 98312 | tf_op jit(solution)/shard_map/ppermute | solution.py:21
  319.8 4.1 %collective-permute-done.32 = f32[4,10,1,128]{3,0,2,1:T(4,128)S(1)} collective-permute-done((f32[4,10,1,128]{3,0,2,1:T(4,128)S(1)}, f32[4,10,1,128]{3,0,2,1:T(4,128)S(1)}, u32[]{:S(2)}, u32[]{:S(2)}) %collective-permute-start.32) | collective-permute-done | bytes 20512 | tf_op jit(solution)/shard_map/ppermute | solution.py:22
  325.5 4.7 %collective-permute-start.35 = (f32[4,10,18,1]{3,0,2,1:T(4,128)S(1)}, f32[4,10,18,1]{3,0,2,1:T(4,128)S(1)}, u32[]{:S(2)}, u32[]{:S(2)}) collective-permute-start(f32[4,10,18,1]{3,0,2,1:T(4,128)S(1)} %get-tuple-element.117), channel_id=1, source_target_pairs={{0,1},{1,2},{2,3},{4,5},{5,6},{6,7},{8,9},{9,10},{10,11},{12,13},{... | collective-permute-start | bytes 8648 | tf_op jit(solution)/shard_map/ppermute | solution.py:21
  331.1 4.2 %collective-permute-done.34 = f32[4,10,18,1]{3,0,2,1:T(4,128)S(1)} collective-permute-done((f32[4,10,18,1]{3,0,2,1:T(4,128)S(1)}, f32[4,10,18,1]{3,0,2,1:T(4,128)S(1)}, u32[]{:S(2)}, u32[]{:S(2)}) %collective-permute-start.34) | collective-permute-done | bytes 2912 | tf_op jit(solution)/shard_map/ppermute | solution.py:22
  339.0 4.8 %collective-permute-start.37 = (f32[4,1,16,128]{3,2,1,0:T(8,128)S(1)}, f32[4,1,16,128]{3,2,1,0:T(8,128)S(1)}, u32[]{:S(2)}, u32[]{:S(2)}) collective-permute-start(f32[4,1,16,128]{3,2,1,0:T(8,128)S(1)} %get-tuple-element.126), channel_id=1, source_target_pairs={{0,8},{8,16},{16,24},{1,9},{9,17},{17,25},{2,10},{10,18},{18,26},{... | collective-permute-start | bytes 98312 | tf_op jit(solution)/shard_map/ppermute | solution.py:21
  348.6 4.1 %collective-permute-done.38 = f32[4,10,1,128]{3,0,2,1:T(4,128)S(1)} collective-permute-done((f32[4,10,1,128]{3,0,2,1:T(4,128)S(1)}, f32[4,10,1,128]{3,0,2,1:T(4,128)S(1)}, u32[]{:S(2)}, u32[]{:S(2)}) %collective-permute-start.38) | collective-permute-done | bytes 20512 | tf_op jit(solution)/shard_map/ppermute | solution.py:22
  354.3 4.7 %collective-permute-start.41 = (f32[4,10,18,1]{3,0,2,1:T(4,128)S(1)}, f32[4,10,18,1]{3,0,2,1:T(4,128)S(1)}, u32[]{:S(2)}, u32[]{:S(2)}) collective-permute-start(f32[4,10,18,1]{3,0,2,1:T(4,128)S(1)} %get-tuple-element.113), channel_id=1, source_target_pairs={{0,1},{1,2},{2,3},{4,5},{5,6},{6,7},{8,9},{9,10},{10,11},{12,13},{... | collective-permute-start | bytes 8648 | tf_op jit(solution)/shard_map/ppermute | solution.py:21
  361.2 4.8 %collective-permute-done.40 = f32[4,10,18,1]{3,0,2,1:T(4,128)S(1)} collective-permute-done((f32[4,10,18,1]{3,0,2,1:T(4,128)S(1)}, f32[4,10,18,1]{3,0,2,1:T(4,128)S(1)}, u32[]{:S(2)}, u32[]{:S(2)}) %collective-permute-start.40) | collective-permute-done | bytes 2912 | tf_op jit(solution)/shard_map/ppermute | solution.py:22
  (279 shorter events, 120.4 us)
Async XLA Ops:
  10.4 15.3 %collective-permute-start.2 = (f32[5,12,2,128]{3,2,1,0:T(2,128)S(1)}, f32[5,12,2,128]{3,2,1,0:T(2,128)S(1)}, u32[]{:S(2)}, u32[]{:S(2)}) collective-permute-start(f32[5,12,2,128]{3,2,1,0:T(2,128)S(1)} %get-tuple-element.108), channel_id=1, source_target_pairs={{0,4},{1,5},{2,6},{3,7},{8,12},{9,13},{10,14},{11,15},{16,20},{17,... | collective-permute-start | bytes 184328 | tf_op jit(solution)/shard_map/ppermute | solution.py:21
  13.8 11.9 %collective-permute-start.3 = (f32[5,12,2,128]{3,2,1,0:T(2,128)S(1)}, f32[5,12,2,128]{3,2,1,0:T(2,128)S(1)}, u32[]{:S(2)}, u32[]{:S(2)}) collective-permute-start(f32[5,12,2,128]{3,2,1,0:T(2,128)S(1)} %get-tuple-element.109), channel_id=1, source_target_pairs={{4,0},{5,1},{6,2},{7,3},{12,8},{13,9},{14,10},{15,11},{20,16},{21,... | collective-permute-start | bytes 184328 | tf_op jit(solution)/shard_map/ppermute | solution.py:22
  26.5 49.6 %collective-permute-start.4 = (f32[5,12,20,2]{2,3,1,0:T(2,128)S(1)}, f32[5,12,20,2]{2,3,1,0:T(2,128)S(1)}, u32[]{:S(2)}, u32[]{:S(2)}) collective-permute-start(f32[5,12,20,2]{2,3,1,0:T(2,128)S(1)} %copy.766), channel_id=1, source_target_pairs={{0,1},{1,2},{2,3},{4,5},{5,6},{6,7},{8,9},{9,10},{10,11},{12,13},{... | collective-permute-start | bytes 28808 | tf_op jit(solution)/shard_map/ppermute | solution.py:21
  30.5 46.1 %collective-permute-start.5 = (f32[5,12,20,2]{2,3,1,0:T(2,128)S(1)}, f32[5,12,20,2]{2,3,1,0:T(2,128)S(1)}, u32[]{:S(2)}, u32[]{:S(2)}) collective-permute-start(f32[5,12,20,2]{2,3,1,0:T(2,128)S(1)} %copy.767), channel_id=1, source_target_pairs={{1,0},{2,1},{3,2},{5,4},{6,5},{7,6},{9,8},{10,9},{11,10},{13,12},{... | collective-permute-start | bytes 28808 | tf_op jit(solution)/shard_map/ppermute | solution.py:22
  103.5 5.9 %collective-permute-start.9 = (f32[5,8,2,64]{3,1,2,0:T(8,128)S(1)}, f32[5,8,2,64]{3,1,2,0:T(8,128)S(1)}, u32[]{:S(2)}, u32[]{:S(2)}) collective-permute-start(f32[5,8,2,64]{3,1,2,0:T(8,128)S(1)} %copy.839), channel_id=1, source_target_pairs={{4,0},{5,1},{6,2},{7,3},{12,8},{13,9},{14,10},{15,11},{20,16},{21,... | collective-permute-start | bytes 61448 | tf_op jit(solution)/shard_map/ppermute | solution.py:22
  109.5 9.4 %collective-permute-start.10 = (f32[5,8,12,2]{3,1,2,0:T(8,128)S(1)}, f32[5,8,12,2]{3,1,2,0:T(8,128)S(1)}, u32[]{:S(2)}, u32[]{:S(2)}) collective-permute-start(f32[5,8,12,2]{3,1,2,0:T(8,128)S(1)} %get-tuple-element.130), channel_id=1, source_target_pairs={{0,1},{1,2},{2,3},{4,5},{5,6},{6,7},{8,9},{9,10},{10,11},{12,13},{... | collective-permute-start | bytes 11528 | tf_op jit(solution)/shard_map/ppermute | solution.py:21
  112.9 10.7 %collective-permute-start.11 = (f32[5,8,12,2]{3,1,2,0:T(8,128)S(1)}, f32[5,8,12,2]{3,1,2,0:T(8,128)S(1)}, u32[]{:S(2)}, u32[]{:S(2)}) collective-permute-start(f32[5,8,12,2]{3,1,2,0:T(8,128)S(1)} %get-tuple-element.131), channel_id=1, source_target_pairs={{1,0},{2,1},{3,2},{5,4},{6,5},{7,6},{9,8},{10,9},{11,10},{13,12},{... | collective-permute-start | bytes 11528 | tf_op jit(solution)/shard_map/ppermute | solution.py:22
  126.1 42.8 %collective-permute-start.12 = (f32[5,2,4,32]{3,2,1,0:T(4,128)S(1)}, f32[5,2,4,32]{3,2,1,0:T(4,128)S(1)}, u32[]{:S(2)}, u32[]{:S(2)}) collective-permute-start(f32[5,2,4,32]{3,2,1,0:T(4,128)S(1)} %pad_maximum_fusion.50), channel_id=1, source_target_pairs={{0,8},{8,16},{16,24},{1,9},{9,17},{17,25},{2,10},{10,18},{18,26},{... | collective-permute-start | bytes 15368 | tf_op jit(solution)/shard_map/ppermute | solution.py:21
  128.2 40.8 %collective-permute-start.13 = (f32[5,2,4,32]{3,2,1,0:T(4,128)S(1)}, f32[5,2,4,32]{3,2,1,0:T(4,128)S(1)}, u32[]{:S(2)}, u32[]{:S(2)}) collective-permute-start(f32[5,2,4,32]{3,2,1,0:T(4,128)S(1)} %pad_maximum_fusion.50), channel_id=1, source_target_pairs={{8,0},{16,8},{24,16},{9,1},{17,9},{25,17},{10,2},{18,10},{26,18},{... | collective-permute-start | bytes 15368 | tf_op jit(solution)/shard_map/ppermute | solution.py:22
  169.0 5.7 %collective-permute-start.14 = (f32[5,6,2,32]{3,2,1,0:T(2,128)S(1)}, f32[5,6,2,32]{3,2,1,0:T(2,128)S(1)}, u32[]{:S(2)}, u32[]{:S(2)}) collective-permute-start(f32[5,6,2,32]{3,2,1,0:T(2,128)S(1)} %get-tuple-element.158), channel_id=1, source_target_pairs={{0,4},{1,5},{2,6},{3,7},{8,12},{9,13},{10,14},{11,15},{16,20},{17,... | collective-permute-start | bytes 23048 | tf_op jit(solution)/shard_map/ppermute | solution.py:21
  173.2 5.8 %collective-permute-start.15 = (f32[5,6,2,32]{3,2,1,0:T(2,128)S(1)}, f32[5,6,2,32]{3,2,1,0:T(2,128)S(1)}, u32[]{:S(2)}, u32[]{:S(2)}) collective-permute-start(f32[5,6,2,32]{3,2,1,0:T(2,128)S(1)} %get-tuple-element.159), channel_id=1, source_target_pairs={{4,0},{5,1},{6,2},{7,3},{12,8},{13,9},{14,10},{15,11},{20,16},{21,... | collective-permute-start | bytes 23048 | tf_op jit(solution)/shard_map/ppermute | solution.py:22
  181.6 6.8 %collective-permute-start.17 = (f32[5,6,8,2]{3,2,1,0:T(8,128)S(1)}, f32[5,6,8,2]{3,2,1,0:T(8,128)S(1)}, u32[]{:S(2)}, u32[]{:S(2)}) collective-permute-start(f32[5,6,8,2]{3,2,1,0:T(8,128)S(1)} %get-tuple-element.151), channel_id=1, source_target_pairs={{1,0},{2,1},{3,2},{5,4},{6,5},{7,6},{9,8},{10,9},{11,10},{13,12},{... | collective-permute-start | bytes 5768 | tf_op jit(solution)/shard_map/ppermute | solution.py:22
  272.5 6.5 %collective-permute-start.22 = (f32[4,4,6,1]{3,1,2,0:T(4,128)S(1)}, f32[4,4,6,1]{3,1,2,0:T(4,128)S(1)}, u32[]{:S(2)}, u32[]{:S(2)}) collective-permute-start(f32[4,4,6,1]{3,1,2,0:T(4,128)S(1)} %get-tuple-element.162), channel_id=1, source_target_pairs={{1,0},{2,1},{3,2},{5,4},{6,5},{7,6},{9,8},{10,9},{11,10},{13,12},{... | collective-permute-start | bytes 1160 | tf_op jit(solution)/shard_map/ppermute | solution.py:22
  273.8 6.3 %collective-permute-start.23 = (f32[4,4,6,1]{3,1,2,0:T(4,128)S(1)}, f32[4,4,6,1]{3,1,2,0:T(4,128)S(1)}, u32[]{:S(2)}, u32[]{:S(2)}) collective-permute-start(f32[4,4,6,1]{3,1,2,0:T(4,128)S(1)} %get-tuple-element.163), channel_id=1, source_target_pairs={{0,1},{1,2},{2,3},{4,5},{5,6},{6,7},{8,9},{9,10},{10,11},{12,13},{... | collective-permute-start | bytes 1160 | tf_op jit(solution)/shard_map/ppermute | solution.py:21
  294.2 7.1 %collective-permute-start.28 = (f32[4,6,10,1]{3,0,2,1:T(4,128)S(1)}, f32[4,6,10,1]{3,0,2,1:T(4,128)S(1)}, u32[]{:S(2)}, u32[]{:S(2)}) collective-permute-start(f32[4,6,10,1]{3,0,2,1:T(4,128)S(1)} %get-tuple-element.146), channel_id=1, source_target_pairs={{1,0},{2,1},{3,2},{5,4},{6,5},{7,6},{9,8},{10,9},{11,10},{13,12},{... | collective-permute-start | bytes 2888 | tf_op jit(solution)/shard_map/ppermute | solution.py:22
  295.5 7.6 %collective-permute-start.29 = (f32[4,6,10,1]{3,0,2,1:T(4,128)S(1)}, f32[4,6,10,1]{3,0,2,1:T(4,128)S(1)}, u32[]{:S(2)}, u32[]{:S(2)}) collective-permute-start(f32[4,6,10,1]{3,0,2,1:T(4,128)S(1)} %get-tuple-element.147), channel_id=1, source_target_pairs={{0,1},{1,2},{2,3},{4,5},{5,6},{6,7},{8,9},{9,10},{10,11},{12,13},{... | collective-permute-start | bytes 2888 | tf_op jit(solution)/shard_map/ppermute | solution.py:21
  308.5 7.2 %collective-permute-start.30 = (f32[4,1,16,128]{3,2,1,0:T(8,128)S(1)}, f32[4,1,16,128]{3,2,1,0:T(8,128)S(1)}, u32[]{:S(2)}, u32[]{:S(2)}) collective-permute-start(f32[4,1,16,128]{3,2,1,0:T(8,128)S(1)} %get-tuple-element.129), channel_id=1, source_target_pairs={{8,0},{16,8},{24,16},{9,1},{17,9},{25,17},{10,2},{18,10},{26,18},{... | collective-permute-start | bytes 98312 | tf_op jit(solution)/shard_map/ppermute | solution.py:22
  309.8 5.9 %collective-permute-start.31 = (f32[4,1,16,128]{3,2,1,0:T(8,128)S(1)}, f32[4,1,16,128]{3,2,1,0:T(8,128)S(1)}, u32[]{:S(2)}, u32[]{:S(2)}) collective-permute-start(f32[4,1,16,128]{3,2,1,0:T(8,128)S(1)} %get-tuple-element.128), channel_id=1, source_target_pairs={{0,8},{8,16},{16,24},{1,9},{9,17},{17,25},{2,10},{10,18},{18,26},{... | collective-permute-start | bytes 98312 | tf_op jit(solution)/shard_map/ppermute | solution.py:21
  318.3 5.7 %collective-permute-start.32 = (f32[4,10,1,128]{3,0,2,1:T(4,128)S(1)}, f32[4,10,1,128]{3,0,2,1:T(4,128)S(1)}, u32[]{:S(2)}, u32[]{:S(2)}) collective-permute-start(f32[4,10,1,128]{3,0,2,1:T(4,128)S(1)} %copy.742), channel_id=1, source_target_pairs={{4,0},{5,1},{6,2},{7,3},{12,8},{13,9},{14,10},{15,11},{20,16},{21,... | collective-permute-start | bytes 61448 | tf_op jit(solution)/shard_map/ppermute | solution.py:22
  324.2 11.1 %collective-permute-start.34 = (f32[4,10,18,1]{3,0,2,1:T(4,128)S(1)}, f32[4,10,18,1]{3,0,2,1:T(4,128)S(1)}, u32[]{:S(2)}, u32[]{:S(2)}) collective-permute-start(f32[4,10,18,1]{3,0,2,1:T(4,128)S(1)} %get-tuple-element.116), channel_id=1, source_target_pairs={{1,0},{2,1},{3,2},{5,4},{6,5},{7,6},{9,8},{10,9},{11,10},{13,12},{... | collective-permute-start | bytes 8648 | tf_op jit(solution)/shard_map/ppermute | solution.py:22
  325.5 11.5 %collective-permute-start.35 = (f32[4,10,18,1]{3,0,2,1:T(4,128)S(1)}, f32[4,10,18,1]{3,0,2,1:T(4,128)S(1)}, u32[]{:S(2)}, u32[]{:S(2)}) collective-permute-start(f32[4,10,18,1]{3,0,2,1:T(4,128)S(1)} %get-tuple-element.117), channel_id=1, source_target_pairs={{0,1},{1,2},{2,3},{4,5},{5,6},{6,7},{8,9},{9,10},{10,11},{12,13},{... | collective-permute-start | bytes 8648 | tf_op jit(solution)/shard_map/ppermute | solution.py:21
  337.7 6.7 %collective-permute-start.36 = (f32[4,1,16,128]{3,2,1,0:T(8,128)S(1)}, f32[4,1,16,128]{3,2,1,0:T(8,128)S(1)}, u32[]{:S(2)}, u32[]{:S(2)}) collective-permute-start(f32[4,1,16,128]{3,2,1,0:T(8,128)S(1)} %get-tuple-element.127), channel_id=1, source_target_pairs={{8,0},{16,8},{24,16},{9,1},{17,9},{25,17},{10,2},{18,10},{26,18},{... | collective-permute-start | bytes 98312 | tf_op jit(solution)/shard_map/ppermute | solution.py:22
  353.0 13.0 %collective-permute-start.40 = (f32[4,10,18,1]{3,0,2,1:T(4,128)S(1)}, f32[4,10,18,1]{3,0,2,1:T(4,128)S(1)}, u32[]{:S(2)}, u32[]{:S(2)}) collective-permute-start(f32[4,10,18,1]{3,0,2,1:T(4,128)S(1)} %get-tuple-element.112), channel_id=1, source_target_pairs={{1,0},{2,1},{3,2},{5,4},{6,5},{7,6},{9,8},{10,9},{11,10},{13,12},{... | collective-permute-start | bytes 8648 | tf_op jit(solution)/shard_map/ppermute | solution.py:22
  354.3 13.4 %collective-permute-start.41 = (f32[4,10,18,1]{3,0,2,1:T(4,128)S(1)}, f32[4,10,18,1]{3,0,2,1:T(4,128)S(1)}, u32[]{:S(2)}, u32[]{:S(2)}) collective-permute-start(f32[4,10,18,1]{3,0,2,1:T(4,128)S(1)} %get-tuple-element.113), channel_id=1, source_target_pairs={{0,1},{1,2},{2,3},{4,5},{5,6},{6,7},{8,9},{9,10},{10,11},{12,13},{... | collective-permute-start | bytes 8648 | tf_op jit(solution)/shard_map/ppermute | solution.py:21
  (25 other events, 168.0 us)
where the time goes:
time: 371 us; the launch traced here: 369 us
  blocking collectives  149 us (40%)
  starting transfers between devices  93.5 us (25%)
  waiting for transfers between devices  62.6 us (17%)
  other arithmetic  29.1 us (8%)
  local copies, waits for them, and re-layouts  26.4 us (7%)
  matrix products  6.55 us (2%)
    ppermute x21, starting transfers between devices, with_halo(): before = lax.ppermute(last, axis, up)  66.2 us
    all_gather x1, blocking collectives, agglomerate(): gathered = lax.all_gather(flattened, ('gx', 'gy', 'gz'), axis=1, tiled=True)  65 us
    ppermute x21, waiting for transfers between devices, with_halo(): after = lax.ppermute(leading, axis, down)  50.6 us
    psum x1, blocking collectives, per_device(): projection = lax.psum(basis_local, ('gx', 'gy', 'gz')) / total_cells  44.3 us
    psum x1, blocking collectives, per_device(): gram = lax.psum(gram_local, ('gx', 'gy', 'gz')) / total_cells  39.5 us
    ppermute x21, starting transfers between devices, with_halo(): after = lax.ppermute(leading, axis, down)  27.3 us
    reduce_sum x14, other arithmetic, restrict(): field.reshape(depth, size_a // 2, 2, size_b // 2, 2, size_c // 2, 2)  13 us
    ppermute x21, waiting for transfers between devices, with_halo(): before = lax.ppermute(last, axis, up)  12 us
  transfers between devices with their start and end apart: 42, of which 24 were waited for; matrix products, arithmetic and copies ran while one was open for 7% of the time, Pallas kernels for 0%

commit v1 on v0

v1 whole, which is shorter than its diff:
```python
import functools

import jax
import jax.numpy as jnp
from jax import lax
from jax.experimental import pallas as pl
from jax.experimental.pallas import tpu as pltpu
from jax.sharding import PartitionSpec as P

LEVELS = 6
COARSE_SWEEPS = 4
OMEGA = 0.8
KEEP = 1.0 - OMEGA
SIXTH = OMEGA / 6.0
PRE_G = OMEGA * (2.0 - OMEGA)
PRE_N = OMEGA * OMEGA / 6.0
AXES = ("gx", "gy", "gz")
HIGH = lax.Precision.HIGHEST
H = 3
NN = (((1,), (0,)), ((), ()))
NT = (((1,), (1,)), ((), ()))
TN = (((0,), (0,)), ((), ()))
VM = pl.BlockSpec(memory_space=pltpu.VMEM)


def dot(a, b, dims=NN):
    return lax.dot_general(a, b, dims, precision=HIGH, preferred_element_type=jnp.float32)


def iota(shape, dim):
    return lax.broadcasted_iota(jnp.int32, shape, dim)


def onehot(cond, scale=1.0):
    return jnp.where(cond, jnp.float32(scale), jnp.float32(0.0))


def roll(a, shift, axis):
    size = a.shape[axis]
    shift = shift % size
    return a if shift == 0 else pltpu.roll(a, shift, axis)


class Place:
    def __init__(self, counts):
        self.counts = counts
        self.at = tuple(lax.axis_index(a) for a in AXES)
        self.me = self.linear(self.at)

    def linear(self, p):
        nx, ny, nz = self.counts
        return (p[0] * ny + p[1]) * nz + p[2]

    def lo(self, axis):
        return self.at[axis] > 0

    def hi(self, axis):
        return self.at[axis] < self.counts[axis] - 1

    def has(self, d):
        ok = None
        for axis in range(3):
            if d[axis]:
                one = self.hi(axis) if d[axis] > 0 else self.lo(axis)
                ok = one if ok is None else jnp.logical_and(ok, one)
        return ok

    def slot(self, d):
        there = self.linear(tuple(p + s for p, s in zip(self.at, d)))
        return jnp.where(self.has(d), there, self.me)


def f32(flag):
    return jnp.where(flag, jnp.float32(1.0), jnp.float32(0.0))


def keep(flag, a):
    return jnp.where(flag, a, jnp.zeros_like(a))


def fill_slots(ref, count, value, rows):
    if count <= 64:
        for t in range(count):
            ref[t, 0:rows] = value
    else:
        def body(t, carry):
            ref[t, 0:rows] = value
            return carry
        lax.fori_loop(0, count, body, 0)


def first_kernel(counts, merge_y, inc, c, *refs):
    if merge_y:
        g, xlo, xhi, ymsg, slots, c2p = refs
    else:
        g, xlo, xhi, ylo, yhi, slots, c2p = refs
    V, X, Y, Z = inc.shape
    place = Place(counts)
    for x in range(X):
        scale = 1.0 / (6.0 * c[x])
        for v in range(V):
            value = inc[v, x] * scale
            g[v, x] = value
            if x < H:
                xlo[v, x] = value
            if x >= X - H:
                xhi[v, x - (X - H)] = value
    sub = iota((8, Z), 0)

    def packed(v, j, start, own):
        return jnp.where(own, g[v, 2 * j, pl.ds(start, 8)], roll(g[v, 2 * j + 1, pl.ds(start, 8)], 4, 0))

    for v in range(V):
        for j in range(X // 2):
            if merge_y:
                up = place.at[1] == 0
                start = pl.multiple_of(jnp.where(up, Y - 8, 0), 8)
                own = (sub + jnp.where(up, 0, 4)) % 8 >= 4
                ymsg[v, j] = packed(v, j, start, own)
            else:
                yhi[v, j] = packed(v, j, Y - 8, sub >= 4)
                ylo[v, j] = packed(v, j, 0, sub < 4)
    ny2, nz2 = Y // 4, Z // 4
    total = None
    for y in range(ny2):
        sums = []
        for x in range(X // 4):
            quad = c[4 * x] + c[4 * x + 1] + c[4 * x + 2] + c[4 * x + 3]
            sums.append(jnp.sum(quad[4 * y : 4 * y + 4], axis=0, keepdims=True))
        rows = jnp.where(sub % 2 == 0, sums[0], sums[1])
        li, lo = iota((Z, Z), 0), iota((Z, Z), 1)
        part = dot(rows, onehot(lo == y * nz2 + li // 4, 1.0 / 64.0))
        total = part if total is None else total + part
    c2p[...] = total
    row, lane = iota((32, Z), 0), iota((32, Z), 1)
    layer = row % 4
    wanted = jnp.where(row < 16, Z - H, 0) + layer
    faces = None
    for v in range(V):
        pick = onehot((lane == wanted) & (layer < H) & ((row % 16) // 4 == v))
        part = dot(pick, g[v].reshape(X * Y, Z), NT)
        faces = part if faces is None else faces + part
    row = iota((16, Z), 0)
    c2_rows = jnp.where(row == 3, total[0:1], jnp.where(row == 7, total[1:2], jnp.zeros((16, Z), jnp.float32)))
    special = (row == 3) | (row == 7)
    up_faces = jnp.where(special, c2_rows, faces[0:16])
    down_faces = jnp.where(special, c2_rows, faces[16:32])
    count = counts[0] * counts[1] * counts[2]
    fill_slots(slots, count, c2_rows[0:8], 8)
    slots[place.me] = c2_rows
    for dx in (-1, 0, 1):
        for dy in (-1, 0, 1):
            slots[place.slot((dx, dy, 1))] = up_faces
            slots[place.slot((dx, dy, -1))] = down_faces
            if dx and dy:
                t = place.slot((dx, dy, 0))
                for cell, (a, b) in enumerate(((0, 0), (0, 1), (1, 0))):
                    x = X - 1 - a if dx > 0 else a
                    y = Y - 1 - b if dy > 0 else b
                    for v in range(V):
                        slots[t, v * 4 + cell] = g[v, x, y]


def spread(cur, below, above, zl, zr):
    return below + above + roll(cur, 1, 0) + roll(cur, -1, 0) + zl + zr


def fine_sum(ref, v, i, V, lane):
    cur = ref[v, i]
    zl, zr = roll(cur, 1, 1), roll(cur, -1, 1)
    if v < V:
        rim = ref[V, i]
        last = lane.shape[1] - 1
        zl = jnp.where(lane == 0, roll(rim, -(16 * v + 2), 1), zl)
        zr = jnp.where(lane == last, roll(rim, last - (16 * v + 10), 1), zr)
    return spread(cur, ref[v, i - 1], ref[v, i + 1], zl, zr)


def fine_masks(place, Y, Z):
    R = Y + 8
    row = iota((R, Z), 0)
    ym = onehot(row < Y) + onehot((row >= Y) & (row < Y + H)) * f32(place.hi(1))
    ym = ym + onehot(row >= R - H) * f32(place.lo(1))
    lane = iota((R, Z), 1)
    k = lane % 8
    outside_lo = ((lane // 8) % 2 == 0) & (k < H)
    outside_hi = ((lane // 8) % 2 == 1) & (k >= 2)
    zm = jnp.where(outside_lo, f32(place.lo(2)), jnp.where(outside_hi, f32(place.hi(2)), jnp.float32(1.0)))
    return ym, ym * zm


def x_flag(place, i, X):
    if i < H:
        return f32(place.lo(0))
    if i >= H + X:
        return f32(place.hi(0))
    return None


def scaled(flag, mask):
    return mask if flag is None else mask * flag


def second_kernel(counts, g, c, xl, xh, yl, yh, slots, gram, G, S, p1, slots1, c1, Q, QC):
    V, X, Y, Z = g.shape
    R = Y + 8
    place = Place(counts)
    sub = iota((8, Z), 0)
    zero8 = jnp.zeros((8, Z), jnp.float32)
    zero_y = jnp.zeros((Y, Z), jnp.float32)
    has_yl, has_yh, has_xl, has_xh = place.lo(1), place.hi(1), place.lo(0), place.hi(0)
    m_hi = jnp.logical_and(sub < H, has_yh)
    m_lo = jnp.logical_and(sub >= 8 - H, has_yl)
    for v in range(V):
        for x in range(X):
            G[v, H + x, 0:Y] = g[v, x]
            hi, lo = yh[v, x // 2], yl[v, x // 2]
            if x % 2:
                hi, lo = roll(hi, 4, 0), roll(lo, 4, 0)
            G[v, H + x, Y:R] = jnp.where(m_hi, hi, jnp.where(m_lo, lo, zero8))
        for i in range(H):
            G[v, i, 0:Y] = keep(has_xl, xl[v, i])
            G[v, i, Y:R] = zero8
            G[v, H + X + i, 0:Y] = keep(has_xh, xh[v, i])
            G[v, H + X + i, Y:R] = zero8
    for dx in (-1, 1):
        for dy in (-1, 1):
            ok, t = place.has((dx, dy, 0)), place.slot((dx, dy, 0))
            for cell, (a, b) in enumerate(((0, 0), (0, 1), (1, 0))):
                i = H + X + a if dx > 0 else H - 1 - a
                r = Y + b if dy > 0 else R - 1 - b
                for v in range(V):
                    G[v, i, r] = keep(ok, slots[t, v * 4 + cell])
    row, lane32 = iota((32, Z), 0), iota((32, Z), 1)
    target = jnp.where(row < 16, 0, 10) + 16 * ((row % 16) // 4) + row % 4
    place_lanes = onehot((lane32 == target) & (row % 4 < H))

    def layers(dx, dy, lanes):
        below, above = (dx, dy, -1), (dx, dy, 1)
        low = keep(place.has(below), slots[place.slot(below)])
        high = keep(place.has(above), slots[place.slot(above)])
        both = jnp.concatenate([low, high], axis=0)
        return dot(both[:, lanes], place_lanes, TN)

    everything = slice(0, X * Y)
    for i in (0, H + X + H - 1):
        G[V, i] = jnp.zeros((R, Z), jnp.float32)
    mid = layers(0, 0, everything)
    up = layers(0, 1, everything)
    down = layers(0, -1, everything)
    for x in range(X):
        G[V, H + x, 0:Y] = mid[x * Y : (x + 1) * Y]
        tile = jnp.where(sub < 2, up[x * Y : x * Y + 8], zero8)
        G[V, H + x, Y:R] = jnp.where(sub >= 6, down[(x + 1) * Y - 8 : (x + 1) * Y], tile)
    for dx in (-1, 1):
        first = slice(0, 2 * Y) if dx > 0 else slice((X - 2) * Y, X * Y)
        side = layers(dx, 0, first)
        base = H + X if dx > 0 else H - 2
        for a in range(2):
            G[V, base + a, 0:Y] = side[a * Y : (a + 1) * Y]
            G[V, base + a, Y:R] = zero8
        near = slice(0, Y) if dx > 0 else slice((X - 1) * Y, X * Y)
        up = layers(dx, 1, near)
        down = layers(dx, -1, near)
        tile = jnp.where(sub < 2, up[0:8], zero8)
        G[V, H + X if dx > 0 else H - 1, Y:R] = jnp.where(sub >= 6, down[Y - 8 : Y], tile)
    lane = iota((R, Z), 1)
    for i in range(1, 2 * H + X - 1):
        rim = G[V, i]
        for v in range(V):
            body = G[v, i]
            rim = jnp.where((lane == 16 * v + 3) | (lane == 16 * v + 4), roll(body, 16 * v + 3, 1), rim)
            rim = jnp.where((lane == 16 * v + 8) | (lane == 16 * v + 9), roll(body, 16 * v + 10, 1), rim)
        G[V, i] = rim
    ym, zm = fine_masks(place, Y, Z)
    for i in range(1, 2 * H + X - 1):
        flag = x_flag(place, i, X)
        for v in range(V + 1):
            mask = scaled(flag, ym if v < V else zm)
            S[v, i] = mask * (PRE_G * G[v, i] + PRE_N * fine_sum(G, v, i, V, lane))
    for x in range(X // 2):
        for v in range(V):
            total = None
            for i in (2 * x, 2 * x + 1):
                inner = 6.0 * (G[v, H + i] - S[v, H + i]) + fine_sum(S, v, H + i, V, lane)
                part = c[i] * inner[0:Y]
                total = part if total is None else total + part
            Q[pl.ds((v * (X // 2) + x) * Y, Y)] = total
        QC[pl.ds(x * Y, Y)] = c[2 * x] + c[2 * x + 1]
    li, lo = iota((Z, Z), 0), iota((Z, Z), 1)
    halve = onehot(lo == li // 2, 0.125)
    n, nc = V * X * Y // 4, X * Y // 4
    b1 = dot(Q[pl.ds(0, n, stride=2)] + Q[pl.ds(1, n, stride=2)], halve)
    cc = dot(QC[pl.ds(0, nc, stride=2)] + QC[pl.ds(1, nc, stride=2)], halve)
    c1[...] = cc.reshape(X // 2, Y // 2, Z)
    scale = 1.0 / (1.5 * jnp.where(iota((nc, Z), 1) < Z // 2, cc, jnp.float32(1.0)))
    U = jnp.concatenate([b1[v * nc : (v + 1) * nc] * scale for v in range(V)], axis=0)
    per = nc
    for vp in range(V // 2):
        both = U[2 * vp * per : (2 * vp + 1) * per] + roll(U[(2 * vp + 1) * per : (2 * vp + 2) * per], Z // 2, 1)
        p1[vp] = both.reshape(X // 2, Y // 2, Z)
    half = Z // 2
    row, lane8 = iota((8, Z), 0), iota((8, Z), 1)
    wanted = jnp.where(row < H, row, half - 2 * H + row)
    faces = dot(onehot((lane8 == wanted) & (row < 2 * H)), U, NT)
    gram_row = gram[0:1]
    base = jnp.where(row == 6, gram_row, zero8)
    faces = jnp.where(row < 6, faces, base)
    fill_slots(slots1, counts[0] * counts[1] * counts[2], base, 8)
    X1, Y1 = X // 2, Y // 2
    for dx in (-1, 0, 1):
        for dy in (-1, 0, 1):
            slots1[place.slot((dx, dy, 1))] = faces
            slots1[place.slot((dx, dy, -1))] = faces
            if dx and dy:
                t = place.slot((dx, dy, 0))
                for vp in range(V // 2):
                    slots1[t, vp] = p1[vp, X1 - 1 if dx > 0 else 0, Y1 - 1 if dy > 0 else 0]


EDGE = ((0, 0), (0, 1), (1, 0))


def edge_steps(merge_y):
    return [(dx, dy) for dx in (1, -1) for dy in ((0,) if merge_y else (1, -1))]


def coarse_masks(place, R, Z):
    half = Z // 2
    row, lane = iota((R, Z), 0), iota((R, Z), 1)
    y = R // 2
    mask = onehot(row < y) + onehot((row >= y) & (row < y + H)) * f32(place.hi(1))
    mask = mask + onehot(row >= R - H) * f32(place.lo(1))
    lanes = onehot(lane < half) + onehot((lane >= half) & (lane < half + H)) * f32(place.hi(2))
    lanes = lanes + onehot(lane >= Z - H) * f32(place.lo(2))
    return mask * lanes


def level1_sum(get, i):
    cur = get(i)
    return spread(cur, get(i - 1), get(i + 1), roll(cur, 1, 1), roll(cur, -1, 1))


def third_kernel(counts, merge_y, p1, c1, xl, xh, yl, yh, slots, c2p, G1, S1, slots2, *refs):
    edges, Q = refs[:-1], refs[-1]
    VP, X, Y, Z = p1.shape
    V, R, half = 2 * VP, 2 * Y, Z // 2
    place = Place(counts)
    row, lane = iota((Y, Z), 0), iota((Y, Z), 1)
    zero = jnp.zeros((Y, Z), jnp.float32)

    def unpack(tile, v):
        return jnp.where(lane < half, roll(tile, half, 1) if v % 2 else tile, zero)

    r16, l16 = iota((16, Z), 0), iota((16, Z), 1)
    target = jnp.where(r16 < 8, Z - 2 * H + r16, half + r16 - 8)
    used = ((r16 >= H) & (r16 < 2 * H)) | ((r16 >= 8) & (r16 < 8 + H))
    place_lanes = onehot((l16 == target) & used)

    def layers(dx, dy):
        below, above = (dx, dy, -1), (dx, dy, 1)
        low = keep(place.has(below), slots[place.slot(below)])
        high = keep(place.has(above), slots[place.slot(above)])
        return dot(jnp.concatenate([low, high], axis=0), place_lanes, TN)

    mid, up, down = layers(0, 0), layers(0, 1), layers(0, -1)
    m_hi = jnp.logical_and(row < H, place.hi(1))
    m_lo = jnp.logical_and(row >= Y - H, place.lo(1))

    def tile_of(d, v, x):
        k = (v * X + x) * Y
        return d[k : k + Y]

    for v in range(V):
        for x in range(X):
            G1[v, H + x, 0:Y] = unpack(p1[v // 2, x], v) + tile_of(mid, v, x)
            hi = unpack(yh[v // 2, x], v) + tile_of(up, v, x)
            lo = unpack(yl[v // 2, x], v) + tile_of(down, v, x)
            G1[v, H + x, Y:R] = jnp.where(m_hi, hi, jnp.where(m_lo, lo, zero))
    for dx in (-1, 1):
        side, up, down = layers(dx, 0), layers(dx, 1), layers(dx, -1)
        src = xh if dx > 0 else xl
        ok = place.hi(0) if dx > 0 else place.lo(0)
        for v in range(V):
            for a in range(H):
                x = a if dx > 0 else X - 1 - a
                i = H + X + a if dx > 0 else H - 1 - a
                G1[v, i, 0:Y] = keep(ok, unpack(src[v // 2, x], v) + tile_of(side, v, x))
                tile = zero
                if a < 2:
                    tile = jnp.where(m_hi, tile_of(up, v, x), jnp.where(m_lo, tile_of(down, v, x), zero))
                G1[v, i, Y:R] = tile
        for dy in (-1, 1):
            ok, t = place.has((dx, dy, 0)), place.slot((dx, dy, 0))
            i = H + X if dx > 0 else H - 1
            r = Y if dy > 0 else R - 1
            for v in range(V):
                line = slots[t, pl.ds(v // 2, 1)]
                line = roll(line, half, 1) if v % 2 else line
                line = jnp.where(lane[0:1] < half, line, jnp.zeros((1, Z), jnp.float32))
                G1[v, i, pl.ds(r, 1)] = G1[v, i, pl.ds(r, 1)] + keep(ok, line)
    mask = coarse_masks(place, R, Z)
    for i in range(1, 2 * H + X - 1):
        m = scaled(x_flag(place, i, X), mask)
        for v in range(V):
            get = lambda j: G1[v, j]
            S1[v, i] = m * (PRE_G * G1[v, i] + PRE_N * level1_sum(get, i))
    for ref, (dx, dy) in zip(edges, edge_steps(merge_y)):
        for cell, (a, b) in enumerate(EDGE):
            i = H + X - 1 - a if dx > 0 else H + a
            if dy == 0:
                y = jnp.where(place.at[1] == 0, Y - 1 - b, b)
            else:
                y = Y - 1 - b if dy > 0 else b
            for vp in range(VP):
                one, two = S1[2 * vp, i, pl.ds(y, 1)], S1[2 * vp + 1, i, pl.ds(y, 1)]
                ref[pl.ds(cell * VP + vp, 1)] = jnp.where(lane[0:1] < half, one, roll(two, half, 1))
                if cell:
                    ref[pl.ds((2 + cell) * VP + vp, 1)] = p1[vp, i - H, pl.ds(y, 1)]
    for x in range(X // 2):
        for v in range(V):
            total = None
            for i in (2 * x, 2 * x + 1):
                get = lambda j: S1[v, j]
                inner = 6.0 * (G1[v, H + i] - S1[v, H + i]) + level1_sum(get, H + i)
                part = c1[i] * inner[0:Y]
                total = part if total is None else total + part
            Q[pl.ds((v * (X // 2) + x) * Y, Y)] = total
    li, lo = iota((Z, Z), 0), iota((Z, Z), 1)
    rows = V * X // 2
    msg = None
    for y in range(Y // 2):
        pair = Q[pl.ds(2 * y, rows, stride=Y)] + Q[pl.ds(2 * y + 1, rows, stride=Y)]
        part = dot(pair, onehot((lo == y * (half // 2) + li // 2) & (li < half), 0.25 * 0.125))
        msg = part if msg is None else msg + part
    msg = msg / (6.0 * 0.0625 * c2p[...])
    fill_slots(slots2, counts[0] * counts[1] * counts[2], msg, 8)


def coarse_kernel(counts, parts_y, slots0, slots2, out, W, pre):
    nx, ny, nz = counts
    Z = 128
    place = Place(counts)
    width = Z // parts_y
    row, lane = iota((8, Z), 0), iota((8, Z), 1)
    odd = row % 2 == 1
    zero = jnp.zeros((8, Z), jnp.float32)

    def assemble(tile):
        grid = []
        for y in range(ny):
            for j in range(parts_y):
                line = []
                for x in range(nx):
                    acc = zero
                    for z in range(nz):
                        moved = roll(tile[(x * ny + y) * nz + z], width * (z - j), 1)
                        acc = jnp.where(lane // width == z, moved, acc)
                    line.append(acc)
                grid.append(line)
        return grid

    count = nx * ny * nz
    g2 = assemble([slots2[t] for t in range(count)])
    c2 = assemble([jnp.where(odd, slots0[t, pl.ds(7, 1)], slots0[t, pl.ds(3, 1)]) for t in range(count)])

    def at(v, y, x):
        inside = 0 <= y < len(v) and 0 <= x < len(v[0])
        return v[y][x] if inside else None

    def add(*terms):
        total = None
        for term in terms:
            if term is not None:
                total = term if total is None else total + term
        return total

    def neighbours(v, level, length):
        rows = [[roll(t, -1, 0) for t in line] for line in v] if level == 2 else None
        back = [[roll(t, 1, 0) for t in line] for line in v] if level == 2 else None
        result = []
        for y in range(len(v)):
            line = []
            for x in range(len(v[0])):
                t = v[y][x]
                zs = jnp.where(lane == 0, zero, roll(t, 1, 1)) + jnp.where(lane == length - 1, zero, roll(t, -1, 1))
                ys = add(zs, at(v, y - 1, x), at(v, y + 1, x))
                if level == 2:
                    xs = jnp.where(odd, add(back[y][x], at(back, y, x + 1)), add(rows[y][x], at(rows, y, x - 1)))
                    line.append(ys + xs)
                else:
                    line.append(add(ys, at(v, y, x - 1), at(v, y, x + 1)))
            result.append(line)
        return result

    def combine(fn, *grids):
        return [[fn(*ts) for ts in zip(*lines)] for lines in zip(*grids)]

    li, lo = iota((Z, Z), 0), iota((Z, Z), 1)
    halve = onehot(lo == li // 2, 0.125)
    double = onehot(li == lo // 2)

    def lanes(grid, matrix):
        flat = [t for line in grid for t in line]
        moved = dot(jnp.concatenate(flat, axis=0) if len(flat) > 1 else flat[0], matrix)
        w = len(grid[0])
        return [[moved[(y * w + x) * 8 : (y * w + x + 1) * 8] for x in range(w)] for y in range(len(grid))]

    def shrink(v, level):
        v = [[a + b for a, b in zip(v[2 * y], v[2 * y + 1])] for y in range(len(v) // 2)]
        if level == 2:
            v = combine(lambda t: t + jnp.where(odd, roll(t, 1, 0), roll(t, -1, 0)), v)
        else:
            v = [[line[2 * x] + line[2 * x + 1] for x in range(len(line) // 2)] for line in v]
        return lanes(v, halve)

    def grow(v, level):
        v = lanes(v, double)
        v = [line for line in v for _ in range(2)]
        return v if level == 2 else [[t for t in line for _ in range(2)] for line in v]

    def sweep(v, g, level, length):
        return combine(lambda a, b, s: KEEP * a + OMEGA * b + SIXTH * s, v, g, neighbours(v, level, length))

    def cycle(g, cs, level, length):
        last = level == LEVELS - 1
        if last:
            v = combine(lambda b: OMEGA * b, g)
            for _ in range(COARSE_SWEEPS - 1):
                v = sweep(v, g, level, length)
            return v
        v = combine(lambda b, s: PRE_G * b + PRE_N * s, g, neighbours(g, level, length))
        if level > 2:
            v = combine(lambda t: jnp.where(lane < length, t, zero), v)
        factor = 0.25**level
        r = combine(
            lambda c, b, a, s: (factor * c) * (6.0 * (b - a) + s), cs, g, v, neighbours(v, level, length)
        )
        down = shrink(r, level)
        c_down = shrink(cs, level)
        inner = lane < length // 2
        d = 6.0 * 0.25 ** (level + 1)
        g_down = combine(lambda b, c: jnp.where(inner, b / (d * jnp.where(inner, c, 1.0)), zero), down, c_down)
        e = grow(cycle(g_down, c_down, level + 1, length // 2), level)
        v = combine(lambda a, b: a + b, v, e)
        v = sweep(v, g, level, length)
        return combine(lambda t: jnp.where(lane < length, t, zero), v) if level > 2 else v

    v = cycle(g2, c2, 2, width * nz)
    for y in range(len(v)):
        for x in range(nx):
            W[y, x] = v[y][x]
    pre[...] = jnp.zeros_like(pre)
    ix, iy, iz = place.at
    for xw in range(4):
        x = ix + (xw + 1) // 2 - 1
        x_ok = jnp.logical_and(x >= 0, x < nx)
        x = jnp.clip(x, 0, nx - 1)
        for j in range(-1, parts_y + 1):
            y = iy * parts_y + j
            ok = jnp.logical_and(x_ok, jnp.logical_and(y >= 0, y < ny * parts_y))
            y = jnp.clip(y, 0, ny * parts_y - 1)
            for vec in range(4):
                pre[vec, xw, pl.ds(j % 8, 1)] = keep(ok, W[y, x, pl.ds(vec * 2 + (xw + 1) % 2, 1)])
    z1 = jnp.where(lo < 96, lo, lo - Z)
    window = onehot(li == iz * width + jnp.floor_divide(z1 + 2, 2) - 1)
    moved = dot(pre[...].reshape(4 * 4 * 8, Z), window)
    out[...] = moved.reshape(4, 4, 8, Z)


def last_kernel(counts, merge_y, e2, G1, S1, G, S, c, *refs):
    edges, (pre, op, E1, C1, E0, C0) = refs[:-6], refs[-6:]
    V, X1, Y1, Z = e2.shape[0], S1.shape[1] - 2 * H, S1.shape[2] // 2, S1.shape[3]
    X, Y = 2 * X1, 2 * Y1
    R1, R = 2 * Y1, Y + 8
    place = Place(counts)
    for v in range(V):
        for x in range(X1):
            k = (v * X1 + x) * R1
            tile = e2[v, x]
            E1[pl.ds(k, 8, stride=2)] = tile
            E1[pl.ds(k + 1, 8, stride=2)] = tile
    for v in range(V):
        for i in range(1, 2 * H + X1 - 1):
            C1[v, i] = S1[v, i] + E1[pl.ds((v * X1 + (i - 1) // 2) * R1, R1)]
    half = Z // 2
    lane = iota((1, Z), 1)
    for ref, (sx, sy) in zip(edges, edge_steps(merge_y)):
        dx = -sx
        for dy in (-1, 1) if sy == 0 else (-sy,):
            ok = place.has((dx, dy, 0))
            for cell, (a, b) in enumerate(EDGE):
                i = H + X1 + a if dx > 0 else H - 1 - a
                r = Y1 + b if dy > 0 else R1 - 1 - b
                for v in range(V):
                    line = ref[pl.ds(cell * (V // 2) + v // 2, 1)]
                    line = roll(line, half, 1) if v % 2 else line
                    line = line + E1[pl.ds((v * X1 + (i - 1) // 2) * R1 + r, 1)]
                    use = jnp.logical_and(lane < half, ok)
                    C1[v, i, pl.ds(r, 1)] = jnp.where(use, line, C1[v, i, pl.ds(r, 1)])
                    if cell:
                        line = ref[pl.ds((2 + cell) * (V // 2) + v // 2, 1)]
                        line = roll(line, half, 1) if v % 2 else line
                        ii, rr = i, r
                        if a:
                            rr = Y1 - 1 if dy > 0 else 0
                        else:
                            ii = H + X1 - 1 if dx > 0 else H
                        line = jnp.where(use, PRE_N * line, jnp.zeros_like(line))
                        C1[v, ii, pl.ds(rr, 1)] = C1[v, ii, pl.ds(rr, 1)] + line
    mask = coarse_masks(place, R1, Z)
    n = X1 + 2
    fine = []
    for v in range(V):
        tiles = []
        for i in range(H - 1, H + X1 + 1):
            m = scaled(x_flag(place, i, X1), mask)
            get = lambda j: C1[v, j]
            tiles.append(m * (KEEP * C1[v, i] + OMEGA * G1[v, i] + SIXTH * level1_sum(get, i)))
        fine.append(jnp.concatenate(tiles, axis=0))
    li, lo = iota((Z, Z), 0), iota((Z, Z), 1)
    double = onehot(li == lo // 2)
    k = lo % 8
    low_side = (lo // 8) % 2 == 0
    source = jnp.where(low_side, jnp.where(k < H, Z - 1, 0), jnp.where(k < 2, half - 1, half))
    rim = None
    for v in range(V):
        part = dot(fine[v], onehot((li == source) & (lo // 16 == v)))
        rim = part if rim is None else rim + part
    sub = iota((8, Z), 0)
    zero8 = jnp.zeros((8, Z), jnp.float32)
    for v in range(V + 1):
        wide = dot(fine[v], double) if v < V else rim
        for i in range(n):
            base = (v * n + i) * R
            tile = wide[i * R1 : i * R1 + Y1]
            edge = wide[i * R1 + Y1 : (i + 1) * R1]
            E0[pl.ds(base, 8, stride=2)] = tile
            E0[pl.ds(base + 1, 8, stride=2)] = tile
            E0[pl.ds(base + Y, 8)] = jnp.where(sub < 2, edge[0:1], jnp.where(sub >= 6, edge[7:8], zero8))
    for v in range(V + 1):
        for i in range(1, 2 * H + X - 1):
            C0[v, i] = S[v, i] + E0[pl.ds((v * n + (i - 1) // 2) * R, R)]
    ym, zm = fine_masks(place, Y, Z)
    lane = iota((R, Z), 1)
    for i in range(H - 1, H + X + 1):
        flag = x_flag(place, i, X)
        for v in range(V + 1):
            m = scaled(flag, ym if v < V else zm)
            value = m * (KEEP * C0[v, i] + OMEGA * G[v, i] + SIXTH * fine_sum(C0, v, i, V, lane))
            E0[pl.ds((v * (X + 2) + i - H + 1) * R, R)] = value
            if v < V and H <= i < H + X:
                pre[v, i - H] = value[0:Y]

    class View:
        def __getitem__(self, key):
            v, i = key
            return E0[pl.ds((v * (X + 2) + i - H + 1) * R, R)]

    view = View()
    for x in range(X):
        for v in range(V):
            around = fine_sum(view, v, H + x, V, lane)
            op[v, x] = c[x] * (6.0 * view[v, H + x][0:Y] - around[0:Y])


def gram_kernel(old, prev, out):
    M, X, Y, Z = old.shape
    J = prev.shape[0]
    pairs = [(a, b) for a in range(M + J) for b in range(a, M + J)]
    sums = [None] * len(pairs)
    for x in range(X):
        for y in range(0, Y, 8):
            tiles = [old[m, x, y : y + 8] for m in range(M)] + [prev[j, x, y : y + 8] for j in range(J)]
            for p, (a, b) in enumerate(pairs):
                term = tiles[a] * tiles[b]
                sums[p] = term if sums[p] is None else sums[p] + term
    ones = jnp.ones((8, Z), jnp.float32)
    lane = iota((8, Z), 1)
    rows = jnp.concatenate([jnp.sum(s, axis=0, keepdims=True) for s in sums], axis=0)
    pad = jnp.zeros((Z - len(pairs), Z), jnp.float32)
    out[...] = dot(ones, jnp.concatenate([rows, pad], axis=0), NT)


def ortho_kernel(count, cells, old, prev, slots, orth, proj, tri):
    M, X, Y, Z = old.shape
    J = prev.shape[0]
    if count <= 64:
        total = slots[0, pl.ds(6, 1)]
        for t in range(1, count):
            total = total + slots[t, pl.ds(6, 1)]
    else:
        total = lax.fori_loop(0, count, lambda t, s: s + slots[t, pl.ds(6, 1)], jnp.zeros((1, Z), jnp.float32))
    total = jnp.broadcast_to(total, (8, Z)) / cells
    value = {}
    p = 0
    for a in range(M + J):
        for b in range(a, M + J):
            one = jnp.broadcast_to(total[:, p : p + 1], (8, Z))
            value[a, b] = value[b, a] = one
            p += 1
    P_ = [[value[m, M + j] for j in range(J)] for m in range(M)]
    gram = {}
    for i in range(J):
        for j in range(i + 1):
            s = value[M + i, M + j]
            for m in range(M):
                inner = None
                for k in range(M):
                    term = value[m, k] * P_[k][j]
                    inner = term if inner is None else inner + term
                s = s - P_[m][i] * (P_[m][j] - inner) - P_[m][j] * P_[m][i]
            gram[i, j] = s
    L = {}
    for i in range(J):
        for j in range(i + 1):
            s = gram[i, j]
            for k in range(j):
                s = s - L[i, k] * L[j, k]
            L[i, j] = jnp.sqrt(s) if i == j else s / L[j, j]
    inv = {}
    for i in range(J):
        for j in range(i + 1):
            s = jnp.ones((8, Z), jnp.float32) if i == j else None
            for k in range(j, i):
                term = L[i, k] * inv[k, j]
                s = -term if s is None else s - term
            inv[i, j] = s / L[i, i]
    row, col = iota((M, J), 0), iota((M, J), 1)
    proj_v, tri_v = jnp.zeros((M, J), jnp.float32), jnp.zeros((J, J), jnp.float32)
    for m in range(M):
        for j in range(J):
            here = (row == m) & (col == j)
            proj_v = jnp.where(here, P_[m][j][0:M, 0:J], proj_v)
            if j >= m:
                tri_v = jnp.where(here, L[j, m][0:J, 0:J], tri_v)
    proj[...] = proj_v
    tri[...] = tri_v
    mix = {}
    for j in range(J):
        for m in range(M):
            s = None
            for i in range(j + 1):
                term = inv[j, i] * P_[m][i]
                s = term if s is None else s + term
            mix[j, m] = s
    for x in range(X):
        for y in range(0, Y, 8):
            olds = [old[m, x, y : y + 8] for m in range(M)]
            rem = []
            for i in range(J):
                r = prev[i, x, y : y + 8]
                for m in range(M):
                    r = r - P_[m][i] * olds[m]
                rem.append(r)
            for j in range(J):
                s = None
                for i in range(j + 1):
                    term = inv[j, i] * rem[i]
                    s = term if s is None else s + term
                orth[j, x, y : y + 8] = s


def run(kernel, shapes, args, scratch=(), name=None):
    fn = pl.pallas_call(
        kernel,
        out_shape=[jax.ShapeDtypeStruct(s, jnp.float32) for s in shapes],
        in_specs=[VM] * len(args),
        out_specs=[VM] * len(shapes),
        scratch_shapes=[pltpu.VMEM(s, jnp.float32) for s in scratch],
        name=name,
    )
    return fn(*args)


def shift(value, axis, step):
    n = lax.axis_size(axis)
    return lax.ppermute(value, axis, [(i, (i + step) % n) for i in range(n)])


def diagonal(counts, value, dx, dy):
    nx, ny = counts[:2]
    step = dy if dy else 1
    pairs = [(x * ny + y, (x + dx) % nx * ny + (y + step) % ny) for x in range(nx) for y in range(ny)]
    return lax.ppermute(value, ("gx", "gy"), pairs)


def swap(slots):
    return lax.all_to_all(slots, AXES, split_axis=0, concat_axis=0, tiled=True)


def wide_coarse(counts, parts_y, slots0, slots2):
    nx, ny, nz = counts
    Z = slots2.shape[2]
    width = Z // parts_y

    def whole(t, lead):
        t = t.reshape(nx, ny, nz, lead * 2, Z)
        parts = []
        for j in range(parts_y):
            part = t[..., j * width : (j + 1) * width].transpose(3, 0, 1, 2, 4)
            parts.append(part.reshape(lead * 2, nx, ny, nz * width))
        t = jnp.stack(parts, axis=3).reshape(lead, 2, nx, ny * parts_y, nz * width)
        return t.transpose(0, 2, 1, 3, 4).reshape(lead, nx * 2, ny * parts_y, nz * width)

    g2 = whole(slots2, 4)
    c2 = whole(jnp.stack([slots0[:, 3], slots0[:, 7]], axis=1), 1)

    def around(v):
        p = jnp.pad(v, ((0, 0), (1, 1), (1, 1), (1, 1)))
        m = slice(1, -1)
        return (
            p[:, 2:, m, m] + p[:, :-2, m, m] + p[:, m, 2:, m] + p[:, m, :-2, m] + p[:, m, m, 2:] + p[:, m, m, :-2]
        )

    def pairs(e):
        return onehot(iota((e, 2 * e), 0) == iota((e, 2 * e), 1) // 2)

    def shrink(v):
        d, a, b, e = v.shape
        v = v.reshape(d, a // 2, 2, b, e).sum(axis=2)
        v = v[:, :, 0::2] + v[:, :, 1::2]
        return dot(v.reshape(-1, e), pairs(e // 2).T * 0.125).reshape(d, a // 2, b // 2, e // 2)

    def grow(v):
        d, a, b, e = v.shape
        v = dot(v.reshape(-1, e), pairs(e)).reshape(d, a, b, 2 * e)
        return jnp.repeat(jnp.repeat(v, 2, axis=1), 2, axis=2)

    def cycle(g, c, level):
        if level == LEVELS - 1:
            v = OMEGA * g
            for _ in range(COARSE_SWEEPS - 1):
                v = KEEP * v + OMEGA * g + SIXTH * around(v)
            return v
        v = PRE_G * g + PRE_N * around(g)
        r = 0.25**level * c * (6.0 * (g - v) + around(v))
        down = shrink(c)
        v = v + grow(cycle(shrink(r) / (6.0 * 0.25 ** (level + 1) * down), down, level + 1))
        return KEEP * v + OMEGA * g + SIXTH * around(v)

    e = jnp.pad(cycle(g2, c2, 2), ((0, 0), (1, 1), (1, 1), (1, 1)))
    ix, iy, iz = (lax.axis_index(a) for a in AXES)
    e = lax.dynamic_slice(
        e, (jnp.int32(0), ix * 2, iy * parts_y, iz * width), (4, 4, parts_y + 2, width + 2)
    )
    e = jnp.repeat(e, 2, axis=3)
    e = jnp.concatenate(
        [e[..., 2:], jnp.zeros(e.shape[:3] + (Z - 2 * width - 4,), e.dtype), e[..., :2]], axis=3
    )
    pad = jnp.zeros((4, 4, 8 - parts_y - 2, Z), e.dtype)
    return jnp.concatenate([e[:, :, 1:], pad, e[:, :, :1]], axis=2)


def per_device(counts, old, prev, inc, c):
    V, X, Y, Z = inc.shape
    count = counts[0] * counts[1] * counts[2]
    merge_y = counts[1] == 2
    R = Y + 8
    X1, Y1 = X // 2, Y // 2
    y_shape = (V, X // 2, 8, Z)
    shapes = [(V, X, Y, Z), (V, H, Y, Z), (V, H, Y, Z), y_shape]
    shapes += [] if merge_y else [y_shape]
    shapes += [(count, 16, Z), (8, Z)]
    outs = run(functools.partial(first_kernel, counts, merge_y), shapes, (inc, c), name="first")
    g, xlo, xhi = outs[:3]
    slots0, c2p = outs[-2:]
    slots0 = swap(slots0)
    xl, xh = shift(xhi, "gx", 1), shift(xlo, "gx", -1)
    if merge_y:
        yl = yh = shift(outs[3], "gy", 1)
    else:
        yl, yh = shift(outs[4], "gy", 1), shift(outs[3], "gy", -1)
    (gram,) = run(gram_kernel, [(8, Z)], (old, prev), name="gram")
    ext0, ext1 = (V + 1, X + 2 * H, R, Z), (V, X1 + 2 * H, 2 * Y1, Z)
    G, S, p1, slots1, c1 = run(
        functools.partial(second_kernel, counts),
        [ext0, ext0, (V // 2, X1, Y1, Z), (count, 8, Z), (X1, Y1, Z)],
        (g, c, xl, xh, yl, yh, slots0, gram),
        [(V * X1 * Y, Z), (X1 * Y, Z)],
        name="second",
    )
    slots1 = swap(slots1)
    xl, xh = shift(p1, "gx", 1), shift(p1, "gx", -1)
    if merge_y:
        yl = yh = shift(p1, "gy", 1)
    else:
        yl, yh = shift(p1, "gy", 1), shift(p1, "gy", -1)
    steps = edge_steps(merge_y)
    G1, S1, slots2, *edges = run(
        functools.partial(third_kernel, counts, merge_y),
        [ext1, ext1, (count, 8, Z)] + [(16, Z)] * len(steps),
        (p1, c1, xl, xh, yl, yh, slots1, c2p),
        [(V * X1 // 2 * Y1, Z)],
        name="third",
    )
    slots2 = swap(slots2)
    edges = [diagonal(counts, e, dx, dy) for e, (dx, dy) in zip(edges, steps)]
    orth, proj, tri = run(
        functools.partial(ortho_kernel, count, float(count * X * Y * Z)),
        [(V, X, Y, Z), (4, 4), (4, 4)],
        (old, prev, slots1),
        name="ortho",
    )
    parts_y = Y // 4
    if counts[2] * (Z // parts_y) == Z and count <= 64:
        (e2,) = run(
            functools.partial(coarse_kernel, counts, parts_y),
            [(V, 4, 8, Z)],
            (slots0, slots2),
            [(counts[1] * parts_y, counts[0], 8, Z), (V, 4, 8, Z)],
            name="coarse",
        )
    else:
        e2 = wide_coarse(counts, parts_y, slots0, slots2)
    pre, op = run(
        functools.partial(last_kernel, counts, merge_y),
        [(V, X, Y, Z), (V, X, Y, Z)],
        (e2, G1, S1, G, S, c, *edges),
        [(V * X1 * 2 * Y1, Z), ext1, ((V + 1) * (X + 2) * R, Z), ext0],
        name="last",
    )
    return orth, proj, tri, pre, op


def solution(mesh):
    block = P(None, *AXES)
    counts = tuple(mesh.shape[a] for a in AXES)
    return jax.shard_map(
        functools.partial(per_device, counts),
        mesh=mesh,
        in_specs=(block, block, block, P(*AXES)),
        out_specs=(block, P(), P(), block, block),
        check_vma=False,
    )
```

time: 371 us -> 61.7 us (0.17)
  blocking collectives: 149 us -> 0 us
  starting transfers between devices: 93.5 us -> 23.5 us
  waiting for transfers between devices: 62.6 us -> 12.6 us
  other arithmetic: 29.1 us -> 0 us
  local copies, waits for them, and re-layouts: 26.4 us -> 2.63 us
  Pallas kernels: 0 us -> 21.7 us
  matrix products: 6.55 us -> 0 us
    ppermute x42 -> x8, starting transfers between devices: 93.5 us -> 9.7 us  [the longest x6 7 us: shift(): return lax.ppermute(value, axis, [(i, (i + step) % n) for i in range(n)])]
    psum x2 -> x0, blocking collectives: 83.8 us -> none  [the longest x1 44.3 us: per_device(): projection = lax.psum(basis_local, ('gx', 'gy', 'gz')) / total_cells]
    all_gather x1 -> x0, blocking collectives: 65 us -> none  [agglomerate(): gathered = lax.all_gather(flattened, ('gx', 'gy', 'gz'), axis=1, tiled=True)]
    ppermute x42 -> x8, waiting for transfers between devices: 62.6 us -> 3.31 us  [the longest x6 3.3 us: shift(): return lax.ppermute(value, axis, [(i, (i + step) % n) for i in range(n)])]
    pallas_call x0 -> x7, Pallas kernels: none -> 21.7 us  [run(): return fn(*args)]
    all_to_all x0 -> x3, starting transfers between devices: none -> 13.8 us  [swap(): return lax.all_to_all(slots, AXES, split_axis=0, concat_axis=0, tiled=True)]
    reduce_sum x14 -> x0, other arithmetic: 13 us -> none  [restrict(): field.reshape(depth, size_a // 2, 2, size_b // 2, 2, size_c // 2, 2)]
    all_to_all x0 -> x3, waiting for transfers between devices: none -> 9.31 us  [swap(): return lax.all_to_all(slots, AXES, split_axis=0, concat_axis=0, tiled=True)]
  transfers between devices with their start and end apart: 42 -> 11, of which waited for: 24 -> 5; matrix products, arithmetic and copies ran while one was open for 7% -> 0% of each run, Pallas kernels for 0% -> 14%
where the time goes in v1:
time: 61.7 us; the launch traced here: 61.2 us
  starting transfers between devices  23.5 us (38%)
  Pallas kernels  21.7 us (35%)
  waiting for transfers between devices  12.6 us (20%)
  local copies, waits for them, and re-layouts  2.63 us (4%)
  between operations  0.74 us (1%)
    pallas_call x7, Pallas kernels, run(): return fn(*args)  21.7 us
    all_to_all x3, starting transfers between devices, swap(): return lax.all_to_all(slots, AXES, split_axis=0, concat_axis=0, tiled=True)  13.8 us
    all_to_all x3, waiting for transfers between devices, swap(): return lax.all_to_all(slots, AXES, split_axis=0, concat_axis=0, tiled=True)  9.31 us
    ppermute x6, starting transfers between devices, shift(): return lax.ppermute(value, axis, [(i, (i + step) % n) for i in range(n)])  7 us
    ppermute x6, waiting for transfers between devices, shift(): return lax.ppermute(value, axis, [(i, (i + step) % n) for i in range(n)])  3.3 us
    ppermute x2, starting transfers between devices, diagonal(): return lax.ppermute(value, ('gx', 'gy'), pairs)  2.7 us
    unnamed x34, local copies, waits for them, and re-layouts  2.63 us
  transfers between devices with their start and end apart: 11, of which 5 were waited for; matrix products, arithmetic and copies ran while one was open for 0% of the time, Pallas kernels for 14%

profile of v1, /device:TPU:0, one launch (start us, length us, event | category | flops | bytes accessed | tf_op | source)
XLA Modules:
  0.0 61.2 jit_solution(7334920521004464713)
XLA Ops:
  0.6 2.4 %first.1 = (f32[4,8,16,128]{3,2,1,0:T(8,128)}, f32[4,3,16,128]{3,2,1,0:T(8,128)}, f32[4,3,16,128]{3,2,1,0:T(8,128)}, f32[4,4,8,128]{3,2,1,0:T(8,128)}, f32[32,16,128]{2,1,0:T(8,128)}, /*index=5*/f32[8,128]{1,0:T(8,128)}) custom-call(f32[4,8,16,128]{3,2,1,0:T(8,128)} %inc.1, f32[8,16,128]{2,1,0:T(8,128)} %c.5), custom_call_target="tpu_custom_call" | custom-call | tf_op jit(solution)/shard_map/first/pallas_call | solution.py:773
  3.1 7.3 %all-to-all-start = ((f32[32,16,128]{2,1,0:T(8,128)}), f32[32,16,128]{2,1,0:T(8,128)S(1)}, u32[]{:S(2)}, u32[]{:S(2)}) async-start(f32[32,16,128]{2,1,0:T(8,128)} %get-tuple-element.30), calls=%async_computation | async-start | bytes 524288 | tf_op jit(solution)/shard_map/all_to_all | solution.py:789
  10.7 1.5 %collective-permute-start.1 = (f32[4,3,16,128]{3,2,1,0:T(8,128)S(1)}, f32[4,3,16,128]{3,2,1,0:T(8,128)S(1)}, u32[]{:S(2)}, u32[]{:S(2)}) collective-permute-start(f32[4,3,16,128]{3,2,1,0:T(8,128)S(1)} %copy-done.12), channel_id=1, source_target_pairs={{0,24},{8,0},{16,8},{24,16},{1,25},{9,1},{17,9},{25,17},{2,26},{10... | collective-permute-start | bytes 294920 | tf_op jit(solution)/shard_map/ppermute | solution.py:778
  12.2 1.8 %collective-permute-start.2 = (f32[4,4,8,128]{3,2,1,0:T(8,128)S(1)}, f32[4,4,8,128]{3,2,1,0:T(8,128)S(1)}, u32[]{:S(2)}, u32[]{:S(2)}) collective-permute-start(f32[4,4,8,128]{3,2,1,0:T(8,128)S(1)} %copy-done.14), channel_id=1, source_target_pairs={{0,4},{4,0},{1,5},{5,1},{2,6},{6,2},{3,7},{7,3},{8,12},{12,8},{9,1... | collective-permute-start | bytes 196616 | tf_op jit(solution)/shard_map/ppermute | solution.py:778
  14.0 1.9 %gram.1 = f32[8,128]{1,0:T(8,128)} custom-call(f32[4,8,16,128]{3,2,1,0:T(8,128)} %old.3, f32[4,8,16,128]{3,2,1,0:T(8,128)} %prev.3), custom_call_target="tpu_custom_call" | custom-call | tf_op jit(solution)/shard_map/gram/pallas_call | solution.py:773
  15.9 1.0 %collective-permute-done.2.yl.yh = f32[4,4,8,128]{3,2,1,0:T(8,128)S(1)} collective-permute-done((f32[4,4,8,128]{3,2,1,0:T(8,128)S(1)}, f32[4,4,8,128]{3,2,1,0:T(8,128)S(1)}, u32[]{:S(2)}, u32[]{:S(2)}) %collective-permute-start.2) | collective-permute-done | bytes 65568 | tf_op jit(solution)/shard_map/ppermute | solution.py:778
  17.0 4.2 %all-to-all-done.slots.slots0 = f32[32,16,128]{2,1,0:T(8,128)S(1)} async-done(((f32[32,16,128]{2,1,0:T(8,128)}), f32[32,16,128]{2,1,0:T(8,128)S(1)}, u32[]{:S(2)}, u32[]{:S(2)}) %all-to-all-start) | async-done | bytes 262176 | tf_op jit(solution)/shard_map/all_to_all | solution.py:789
  21.2 0.7 %copy-done = f32[32,16,128]{2,1,0:T(8,128)} copy-done((f32[32,16,128]{2,1,0:T(8,128)}, f32[32,16,128]{2,1,0:T(8,128)S(1)}, u32[]{:S(2)}) %copy-start) | copy-done | bytes 262168
  21.9 4.2 %second.1 = (f32[5,14,24,128]{3,2,1,0:T(8,128)}, f32[5,14,24,128]{3,2,1,0:T(8,128)}, f32[2,4,8,128]{3,2,1,0:T(8,128)}, f32[32,8,128]{2,1,0:T(8,128)}, f32[4,8,128]{2,1,0:T(8,128)}) custom-call(f32[4,8,16,128]{3,2,1,0:T(8,128)} %get-tuple-element.26.g, f32[8,16,128]{2,1,0:T(8,128)} %c.5, f32[4,3,16,128]{3,2,1,0:T(8,128)} %copy-done.5, ...), custom_call_target="tpu_custom_call" | custom-call | tf_op jit(solution)/shard_map/second/pallas_call | solution.py:773
  26.1 2.7 %all-to-all-start.1 = ((f32[32,8,128]{2,1,0:T(8,128)}), f32[32,8,128]{2,1,0:T(8,128)S(1)}, u32[]{:S(2)}, u32[]{:S(2)}) async-start(f32[32,8,128]{2,1,0:T(8,128)} %get-tuple-element.31), calls=%async_computation.1 | async-start | bytes 262144 | tf_op jit(solution)/shard_map/all_to_all | solution.py:789
  29.0 1.6 %collective-permute-start.4 = (f32[2,4,8,128]{3,2,1,0:T(8,128)S(1)}, f32[2,4,8,128]{3,2,1,0:T(8,128)S(1)}, u32[]{:S(2)}, u32[]{:S(2)}) collective-permute-start(f32[2,4,8,128]{3,2,1,0:T(8,128)S(1)} %copy-done.7), channel_id=1, source_target_pairs={{0,24},{8,0},{16,8},{24,16},{1,25},{9,1},{17,9},{25,17},{2,26},{10... | collective-permute-start | bytes 98312 | tf_op jit(solution)/shard_map/ppermute | solution.py:778
  30.6 1.6 %collective-permute-start.5 = (f32[2,4,8,128]{3,2,1,0:T(8,128)S(1)}, f32[2,4,8,128]{3,2,1,0:T(8,128)S(1)}, u32[]{:S(2)}, u32[]{:S(2)}) collective-permute-start(f32[2,4,8,128]{3,2,1,0:T(8,128)S(1)} %copy-done.7), channel_id=1, source_target_pairs={{0,4},{4,0},{1,5},{5,1},{2,6},{6,2},{3,7},{7,3},{8,12},{12,8},{9,1... | collective-permute-start | bytes 98312 | tf_op jit(solution)/shard_map/ppermute | solution.py:778
  32.3 2.2 %collective-permute-done.5.yl.yh = f32[2,4,8,128]{3,2,1,0:T(8,128)S(1)} collective-permute-done((f32[2,4,8,128]{3,2,1,0:T(8,128)S(1)}, f32[2,4,8,128]{3,2,1,0:T(8,128)S(1)}, u32[]{:S(2)}, u32[]{:S(2)}) %collective-permute-start.5) | collective-permute-done | bytes 32800 | tf_op jit(solution)/shard_map/ppermute | solution.py:778
  34.5 2.1 %all-to-all-done.1.slots = f32[32,8,128]{2,1,0:T(8,128)S(1)} async-done(((f32[32,8,128]{2,1,0:T(8,128)}), f32[32,8,128]{2,1,0:T(8,128)S(1)}, u32[]{:S(2)}, u32[]{:S(2)}) %all-to-all-start.1) | async-done | bytes 131104 | tf_op jit(solution)/shard_map/all_to_all | solution.py:789
  36.6 0.6 %copy-done.1 = f32[32,8,128]{2,1,0:T(8,128)} copy-done((f32[32,8,128]{2,1,0:T(8,128)}, f32[32,8,128]{2,1,0:T(8,128)S(1)}, u32[]{:S(2)}) %copy-start.1) | copy-done | bytes 131096
  37.2 2.9 %third.1 = (f32[4,10,16,128]{3,2,1,0:T(8,128)}, f32[4,10,16,128]{3,2,1,0:T(8,128)}, f32[32,8,128]{2,1,0:T(8,128)}, f32[16,128]{1,0:T(8,128)}, f32[16,128]{1,0:T(8,128)}) custom-call(f32[2,4,8,128]{3,2,1,0:T(8,128)} %get-tuple-element.35.p1, f32[4,8,128]{2,1,0:T(8,128)} %get-tuple-element.36.c1, f32[2,4,8,128]{3,2,1,0:T(8,128)} %copy-done.8, ...), custom_call_target="tpu_custom_call" | custom-call | tf_op jit(solution)/shard_map/third/pallas_call | solution.py:773
  40.1 3.8 %all-to-all-start.2 = ((f32[32,8,128]{2,1,0:T(8,128)}), f32[32,8,128]{2,1,0:T(8,128)S(1)}, u32[]{:S(2)}, u32[]{:S(2)}) async-start(f32[32,8,128]{2,1,0:T(8,128)} %get-tuple-element.38), calls=%async_computation.2 | async-start | bytes 262144 | tf_op jit(solution)/shard_map/all_to_all | solution.py:789
  43.9 1.5 %collective-permute-start.6 = (f32[16,128]{1,0:T(8,128)S(1)}, f32[16,128]{1,0:T(8,128)S(1)}, u32[]{:S(2)}, u32[]{:S(2)}) collective-permute-start(f32[16,128]{1,0:T(8,128)S(1)} %copy-done.16), channel_id=1, source_target_pairs={{0,12},{4,8},{8,20},{12,16},{16,28},{20,24},{24,4},{28,0},{1,13},{... | collective-permute-start | bytes 24584 | tf_op jit(solution)/shard_map/ppermute | solution.py:785
  45.5 1.2 %collective-permute-start.7 = (f32[16,128]{1,0:T(8,128)S(1)}, f32[16,128]{1,0:T(8,128)S(1)}, u32[]{:S(2)}, u32[]{:S(2)}) collective-permute-start(f32[16,128]{1,0:T(8,128)S(1)} %copy-done.15), channel_id=1, source_target_pairs={{0,28},{4,24},{8,4},{12,0},{16,12},{20,8},{24,20},{28,16},{1,29},{... | collective-permute-start | bytes 24584 | tf_op jit(solution)/shard_map/ppermute | solution.py:785
  46.6 2.0 %ortho.1 = (f32[4,8,16,128]{3,2,1,0:T(8,128)}, f32[4,4]{1,0:T(4,128)}, f32[4,4]{1,0:T(4,128)}) custom-call(f32[4,8,16,128]{3,2,1,0:T(8,128)} %old.3, f32[4,8,16,128]{3,2,1,0:T(8,128)} %prev.3, f32[32,8,128]{2,1,0:T(8,128)} %copy-done.1), custom_call_target="tpu_custom_call" | custom-call | tf_op jit(solution)/shard_map/ortho/pallas_call | solution.py:773
  48.7 3.0 %all-to-all-done.2.slots2 = f32[32,8,128]{2,1,0:T(8,128)S(1)} async-done(((f32[32,8,128]{2,1,0:T(8,128)}), f32[32,8,128]{2,1,0:T(8,128)S(1)}, u32[]{:S(2)}, u32[]{:S(2)}) %all-to-all-start.2) | async-done | bytes 131104 | tf_op jit(solution)/shard_map/all_to_all | solution.py:789
  51.7 0.7 %copy-done.2 = f32[32,8,128]{2,1,0:T(8,128)} copy-done((f32[32,8,128]{2,1,0:T(8,128)}, f32[32,8,128]{2,1,0:T(8,128)S(1)}, u32[]{:S(2)}) %copy-start.2) | copy-done | bytes 131096
  52.4 4.4 %coarse.1.e2 = f32[4,4,8,128]{3,2,1,0:T(8,128)} custom-call(f32[32,16,128]{2,1,0:T(8,128)} %copy-done, f32[32,8,128]{2,1,0:T(8,128)} %copy-done.2), custom_call_target="tpu_custom_call" | custom-call | tf_op jit(solution)/shard_map/coarse/pallas_call | solution.py:773
  57.4 3.8 %last.1 = (f32[4,8,16,128]{3,2,1,0:T(8,128)}, f32[4,8,16,128]{3,2,1,0:T(8,128)}) custom-call(f32[4,4,8,128]{3,2,1,0:T(8,128)} %coarse.1.e2, f32[4,10,16,128]{3,2,1,0:T(8,128)} %get-tuple-element.39.G1, f32[4,10,16,128]{3,2,1,0:T(8,128)} %get-tuple-element.40.S1, f32[5,14,24,128]{3,2,1,0:T(8,128)} %get-tuple-element.41.G, ...), custom_call_target="tpu_custom_call" | custom-call | tf_op jit(solution)/shard_map/last/pallas_call | solution.py:773
  (39 shorter events, 1.2 us)
Async XLA Ops:
  3.1 7.4 %copy-start.13 = (f32[4,3,16,128]{3,2,1,0:T(8,128)S(1)}, f32[4,3,16,128]{3,2,1,0:T(8,128)}, u32[]{:S(2)}) copy-start(f32[4,3,16,128]{3,2,1,0:T(8,128)} %get-tuple-element.27) | copy-start | bytes 294916
  3.1 7.7 %copy-start.12 = (f32[4,3,16,128]{3,2,1,0:T(8,128)S(1)}, f32[4,3,16,128]{3,2,1,0:T(8,128)}, u32[]{:S(2)}) copy-start(f32[4,3,16,128]{3,2,1,0:T(8,128)} %get-tuple-element.28) | copy-start | bytes 294916
  3.1 9.2 %copy-start.14 = (f32[4,4,8,128]{3,2,1,0:T(8,128)S(1)}, f32[4,4,8,128]{3,2,1,0:T(8,128)}, u32[]{:S(2)}) copy-start(f32[4,4,8,128]{3,2,1,0:T(8,128)} %get-tuple-element.29) | copy-start | bytes 196612
  3.1 18.1 %all-to-all-start = ((f32[32,16,128]{2,1,0:T(8,128)}), f32[32,16,128]{2,1,0:T(8,128)S(1)}, u32[]{:S(2)}, u32[]{:S(2)}) async-start(f32[32,16,128]{2,1,0:T(8,128)} %get-tuple-element.30), calls=%async_computation | async-start | bytes 524288 | tf_op jit(solution)/shard_map/all_to_all | solution.py:789
  10.4 6.5 %collective-permute-start = (f32[4,3,16,128]{3,2,1,0:T(8,128)S(1)}, f32[4,3,16,128]{3,2,1,0:T(8,128)S(1)}, u32[]{:S(2)}, u32[]{:S(2)}) collective-permute-start(f32[4,3,16,128]{3,2,1,0:T(8,128)S(1)} %copy-done.13), channel_id=1, source_target_pairs={{0,8},{8,16},{16,24},{24,0},{1,9},{9,17},{17,25},{25,1},{2,10},{10... | collective-permute-start | bytes 294920 | tf_op jit(solution)/shard_map/ppermute | solution.py:778
  10.7 6.2 %collective-permute-start.1 = (f32[4,3,16,128]{3,2,1,0:T(8,128)S(1)}, f32[4,3,16,128]{3,2,1,0:T(8,128)S(1)}, u32[]{:S(2)}, u32[]{:S(2)}) collective-permute-start(f32[4,3,16,128]{3,2,1,0:T(8,128)S(1)} %copy-done.12), channel_id=1, source_target_pairs={{0,24},{8,0},{16,8},{24,16},{1,25},{9,1},{17,9},{25,17},{2,26},{10... | collective-permute-start | bytes 294920 | tf_op jit(solution)/shard_map/ppermute | solution.py:778
  12.2 4.7 %collective-permute-start.2 = (f32[4,4,8,128]{3,2,1,0:T(8,128)S(1)}, f32[4,4,8,128]{3,2,1,0:T(8,128)S(1)}, u32[]{:S(2)}, u32[]{:S(2)}) collective-permute-start(f32[4,4,8,128]{3,2,1,0:T(8,128)S(1)} %copy-done.14), channel_id=1, source_target_pairs={{0,4},{4,0},{1,5},{5,1},{2,6},{6,2},{3,7},{7,3},{8,12},{12,8},{9,1... | collective-permute-start | bytes 196616 | tf_op jit(solution)/shard_map/ppermute | solution.py:778
  16.9 4.2 %copy-start.3 = (f32[4,4,8,128]{3,2,1,0:T(8,128)}, f32[4,4,8,128]{3,2,1,0:T(8,128)S(1)}, u32[]{:S(2)}) copy-start(f32[4,4,8,128]{3,2,1,0:T(8,128)S(1)} %collective-permute-done.2.yl.yh) | copy-start | bytes 196612
  16.9 4.2 %copy-start.5 = (f32[4,3,16,128]{3,2,1,0:T(8,128)}, f32[4,3,16,128]{3,2,1,0:T(8,128)S(1)}, u32[]{:S(2)}) copy-start(f32[4,3,16,128]{3,2,1,0:T(8,128)S(1)} %collective-permute-done.xl) | copy-start | bytes 294916
  16.9 4.2 %copy-start.6 = (f32[4,3,16,128]{3,2,1,0:T(8,128)}, f32[4,3,16,128]{3,2,1,0:T(8,128)S(1)}, u32[]{:S(2)}) copy-start(f32[4,3,16,128]{3,2,1,0:T(8,128)S(1)} %collective-permute-done.1.xh) | copy-start | bytes 294916
  21.2 0.7 %copy-start = (f32[32,16,128]{2,1,0:T(8,128)}, f32[32,16,128]{2,1,0:T(8,128)S(1)}, u32[]{:S(2)}) copy-start(f32[32,16,128]{2,1,0:T(8,128)S(1)} %all-to-all-done.slots.slots0) | copy-start | bytes 786436
  26.1 2.7 %copy-start.7 = (f32[2,4,8,128]{3,2,1,0:T(8,128)S(1)}, f32[2,4,8,128]{3,2,1,0:T(8,128)}, u32[]{:S(2)}) copy-start(f32[2,4,8,128]{3,2,1,0:T(8,128)} %get-tuple-element.35.p1) | copy-start | bytes 98308
  26.1 10.5 %all-to-all-start.1 = ((f32[32,8,128]{2,1,0:T(8,128)}), f32[32,8,128]{2,1,0:T(8,128)S(1)}, u32[]{:S(2)}, u32[]{:S(2)}) async-start(f32[32,8,128]{2,1,0:T(8,128)} %get-tuple-element.31), calls=%async_computation.1 | async-start | bytes 262144 | tf_op jit(solution)/shard_map/all_to_all | solution.py:789
  28.8 3.5 %collective-permute-start.3 = (f32[2,4,8,128]{3,2,1,0:T(8,128)S(1)}, f32[2,4,8,128]{3,2,1,0:T(8,128)S(1)}, u32[]{:S(2)}, u32[]{:S(2)}) collective-permute-start(f32[2,4,8,128]{3,2,1,0:T(8,128)S(1)} %copy-done.7), channel_id=1, source_target_pairs={{0,8},{8,16},{16,24},{24,0},{1,9},{9,17},{17,25},{25,1},{2,10},{10... | collective-permute-start | bytes 98312 | tf_op jit(solution)/shard_map/ppermute | solution.py:778
  29.0 3.3 %collective-permute-start.4 = (f32[2,4,8,128]{3,2,1,0:T(8,128)S(1)}, f32[2,4,8,128]{3,2,1,0:T(8,128)S(1)}, u32[]{:S(2)}, u32[]{:S(2)}) collective-permute-start(f32[2,4,8,128]{3,2,1,0:T(8,128)S(1)} %copy-done.7), channel_id=1, source_target_pairs={{0,24},{8,0},{16,8},{24,16},{1,25},{9,1},{17,9},{25,17},{2,26},{10... | collective-permute-start | bytes 98312 | tf_op jit(solution)/shard_map/ppermute | solution.py:778
  30.6 3.9 %collective-permute-start.5 = (f32[2,4,8,128]{3,2,1,0:T(8,128)S(1)}, f32[2,4,8,128]{3,2,1,0:T(8,128)S(1)}, u32[]{:S(2)}, u32[]{:S(2)}) collective-permute-start(f32[2,4,8,128]{3,2,1,0:T(8,128)S(1)} %copy-done.7), channel_id=1, source_target_pairs={{0,4},{4,0},{1,5},{5,1},{2,6},{6,2},{3,7},{7,3},{8,12},{12,8},{9,1... | collective-permute-start | bytes 98312 | tf_op jit(solution)/shard_map/ppermute | solution.py:778
  32.3 4.3 %copy-start.8 = (f32[2,4,8,128]{3,2,1,0:T(8,128)}, f32[2,4,8,128]{3,2,1,0:T(8,128)S(1)}, u32[]{:S(2)}) copy-start(f32[2,4,8,128]{3,2,1,0:T(8,128)S(1)} %collective-permute-done.3.xl) | copy-start | bytes 98308
  32.3 4.3 %copy-start.9 = (f32[2,4,8,128]{3,2,1,0:T(8,128)}, f32[2,4,8,128]{3,2,1,0:T(8,128)S(1)}, u32[]{:S(2)}) copy-start(f32[2,4,8,128]{3,2,1,0:T(8,128)S(1)} %collective-permute-done.4.xh) | copy-start | bytes 98308
  34.5 2.1 %copy-start.4 = (f32[2,4,8,128]{3,2,1,0:T(8,128)}, f32[2,4,8,128]{3,2,1,0:T(8,128)S(1)}, u32[]{:S(2)}) copy-start(f32[2,4,8,128]{3,2,1,0:T(8,128)S(1)} %collective-permute-done.5.yl.yh) | copy-start | bytes 98308
  40.1 3.8 %copy-start.16 = (f32[16,128]{1,0:T(8,128)S(1)}, f32[16,128]{1,0:T(8,128)}, u32[]{:S(2)}) copy-start(f32[16,128]{1,0:T(8,128)} %get-tuple-element.43) | copy-start | bytes 24580
  40.1 5.3 %copy-start.15 = (f32[16,128]{1,0:T(8,128)S(1)}, f32[16,128]{1,0:T(8,128)}, u32[]{:S(2)}) copy-start(f32[16,128]{1,0:T(8,128)} %get-tuple-element.44) | copy-start | bytes 24580
  40.1 11.6 %all-to-all-start.2 = ((f32[32,8,128]{2,1,0:T(8,128)}), f32[32,8,128]{2,1,0:T(8,128)S(1)}, u32[]{:S(2)}, u32[]{:S(2)}) async-start(f32[32,8,128]{2,1,0:T(8,128)} %get-tuple-element.38), calls=%async_computation.2 | async-start | bytes 262144 | tf_op jit(solution)/shard_map/all_to_all | solution.py:789
  43.9 12.8 %collective-permute-start.6 = (f32[16,128]{1,0:T(8,128)S(1)}, f32[16,128]{1,0:T(8,128)S(1)}, u32[]{:S(2)}, u32[]{:S(2)}) collective-permute-start(f32[16,128]{1,0:T(8,128)S(1)} %copy-done.16), channel_id=1, source_target_pairs={{0,12},{4,8},{8,20},{12,16},{16,28},{20,24},{24,4},{28,0},{1,13},{... | collective-permute-start | bytes 24584 | tf_op jit(solution)/shard_map/ppermute | solution.py:785
  45.5 11.3 %collective-permute-start.7 = (f32[16,128]{1,0:T(8,128)S(1)}, f32[16,128]{1,0:T(8,128)S(1)}, u32[]{:S(2)}, u32[]{:S(2)}) collective-permute-start(f32[16,128]{1,0:T(8,128)S(1)} %copy-done.15), channel_id=1, source_target_pairs={{0,28},{4,24},{8,4},{12,0},{16,12},{20,8},{24,20},{28,16},{1,29},{... | collective-permute-start | bytes 24584 | tf_op jit(solution)/shard_map/ppermute | solution.py:785
  (4 other events, 2.5 us)

commit v2 on v1

--- a/solution.py
+++ b/solution.py
@@ -21,6 +21,14 @@
 NT = (((1,), (1,)), ((), ()))
 TN = (((0,), (0,)), ((), ()))
 VM = pl.BlockSpec(memory_space=pltpu.VMEM)
+HB = pl.BlockSpec(memory_space=pltpu.HBM)
+EDGE = ((0, 0), (0, 1), (1, 0))
+EDGE1 = EDGE + ((1, 1), (0, 2), (2, 0))
+GRAM_ROW, C_ROW = 3, 4
+
+
+def edge_steps(merge_y):
+    return [(dx, dy) for dx in (1, -1) for dy in ((0,) if merge_y else (1, -1))]
 
 
 def dot(a, b, dims=NN):
@@ -89,23 +97,52 @@
         lax.fori_loop(0, count, body, 0)
 
 
-def first_kernel(counts, merge_y, inc, c, *refs):
+def first_kernel(counts, merge_y, inc_hbm, c_hbm, *refs):
     if merge_y:
-        g, xlo, xhi, ymsg, slots, c2p = refs
+        g, xlo, xhi, ymsg, slots, inc, c, sems = refs
     else:
-        g, xlo, xhi, ylo, yhi, slots, c2p = refs
+        g, xlo, xhi, ylo, yhi, slots, inc, c, sems = refs
     V, X, Y, Z = inc.shape
     place = Place(counts)
-    for x in range(X):
-        scale = 1.0 / (6.0 * c[x])
-        for v in range(V):
-            value = inc[v, x] * scale
+    copy_c = pltpu.make_async_copy(c_hbm, c, sems.at[V])
+    copies = [pltpu.make_async_copy(inc_hbm.at[v], inc.at[v], sems.at[v]) for v in range(V)]
+    copy_c.start()
+    for copy in copies:
+        copy.start()
+    sub = iota((8, Z), 0)
+    row, lane = iota((32, Z), 0), iota((32, Z), 1)
+    layer = (row % 16) // 4
+    wanted = jnp.where(row < 16, Z - H, 0) + layer
+    copy_c.wait()
+    scale = [1.0 / (6.0 * c[x]) for x in range(X)]
+    faces = None
+    for v in range(V):
+        copies[v].wait()
+        for x in range(X):
+            value = inc[v, x] * scale[x]
             g[v, x] = value
             if x < H:
                 xlo[v, x] = value
             if x >= X - H:
                 xhi[v, x - (X - H)] = value
-    sub = iota((8, Z), 0)
+        pick = onehot((lane == wanted) & (layer < H) & (row % 4 == v))
+        part = dot(pick, g[v].reshape(X * Y, Z), NT)
+        faces = part if faces is None else faces + part
+    up = [faces[4 * k : 4 * k + 4] for k in range(H)]
+    down = [faces[16 + 4 * k : 20 + 4 * k] for k in range(H)]
+    for dx in (-1, 0, 1):
+        for dy in (-1, 0, 1):
+            above, below = place.slot((dx, dy, 1)), place.slot((dx, dy, -1))
+            for k in range(H):
+                slots[above, k] = up[k]
+                slots[below, k] = down[k]
+            if dx and dy:
+                t = place.slot((dx, dy, 0))
+                for cell, (a, b) in enumerate(EDGE):
+                    x = X - 1 - a if dx > 0 else a
+                    y = Y - 1 - b if dy > 0 else b
+                    for v in range(V):
+                        slots[t, cell, pl.ds(v, 1)] = g[v, x, pl.ds(y, 1)]
 
     def packed(v, j, start, own):
         return jnp.where(own, g[v, 2 * j, pl.ds(start, 8)], roll(g[v, 2 * j + 1, pl.ds(start, 8)], 4, 0))
@@ -113,52 +150,13 @@
     for v in range(V):
         for j in range(X // 2):
             if merge_y:
-                up = place.at[1] == 0
-                start = pl.multiple_of(jnp.where(up, Y - 8, 0), 8)
-                own = (sub + jnp.where(up, 0, 4)) % 8 >= 4
+                first = place.at[1] == 0
+                start = pl.multiple_of(jnp.where(first, Y - 8, 0), 8)
+                own = (sub + jnp.where(first, 0, 4)) % 8 >= 4
                 ymsg[v, j] = packed(v, j, start, own)
             else:
                 yhi[v, j] = packed(v, j, Y - 8, sub >= 4)
                 ylo[v, j] = packed(v, j, 0, sub < 4)
-    ny2, nz2 = Y // 4, Z // 4
-    total = None
-    for y in range(ny2):
-        sums = []
-        for x in range(X // 4):
-            quad = c[4 * x] + c[4 * x + 1] + c[4 * x + 2] + c[4 * x + 3]
-            sums.append(jnp.sum(quad[4 * y : 4 * y + 4], axis=0, keepdims=True))
-        rows = jnp.where(sub % 2 == 0, sums[0], sums[1])
-        li, lo = iota((Z, Z), 0), iota((Z, Z), 1)
-        part = dot(rows, onehot(lo == y * nz2 + li // 4, 1.0 / 64.0))
-        total = part if total is None else total + part
-    c2p[...] = total
-    row, lane = iota((32, Z), 0), iota((32, Z), 1)
-    layer = row % 4
-    wanted = jnp.where(row < 16, Z - H, 0) + layer
-    faces = None
-    for v in range(V):
-        pick = onehot((lane == wanted) & (layer < H) & ((row % 16) // 4 == v))
-        part = dot(pick, g[v].reshape(X * Y, Z), NT)
-        faces = part if faces is None else faces + part
-    row = iota((16, Z), 0)
-    c2_rows = jnp.where(row == 3, total[0:1], jnp.where(row == 7, total[1:2], jnp.zeros((16, Z), jnp.float32)))
-    special = (row == 3) | (row == 7)
-    up_faces = jnp.where(special, c2_rows, faces[0:16])
-    down_faces = jnp.where(special, c2_rows, faces[16:32])
-    count = counts[0] * counts[1] * counts[2]
-    fill_slots(slots, count, c2_rows[0:8], 8)
-    slots[place.me] = c2_rows
-    for dx in (-1, 0, 1):
-        for dy in (-1, 0, 1):
-            slots[place.slot((dx, dy, 1))] = up_faces
-            slots[place.slot((dx, dy, -1))] = down_faces
-            if dx and dy:
-                t = place.slot((dx, dy, 0))
-                for cell, (a, b) in enumerate(((0, 0), (0, 1), (1, 0))):
-                    x = X - 1 - a if dx > 0 else a
-                    y = Y - 1 - b if dy > 0 else b
-                    for v in range(V):
-                        slots[t, v * 4 + cell] = g[v, x, y]
 
 
 def spread(cur, below, above, zl, zr):
@@ -201,7 +199,8 @@
     return mask if flag is None else mask * flag
 
 
-def second_kernel(counts, g, c, xl, xh, yl, yh, slots, gram, G, S, p1, slots1, c1, Q, QC):
+def second_kernel(counts, merge_y, g, c, xl, xh, yl, yh, slots, gram, c2p, G, S, p1, slots1, c1, *refs):
+    edges, (Q, QC) = refs[:-2], refs[-2:]
     V, X, Y, Z = g.shape
     R = Y + 8
     place = Place(counts)
@@ -226,21 +225,21 @@
     for dx in (-1, 1):
         for dy in (-1, 1):
             ok, t = place.has((dx, dy, 0)), place.slot((dx, dy, 0))
-            for cell, (a, b) in enumerate(((0, 0), (0, 1), (1, 0))):
+            for cell, (a, b) in enumerate(EDGE):
                 i = H + X + a if dx > 0 else H - 1 - a
                 r = Y + b if dy > 0 else R - 1 - b
                 for v in range(V):
-                    G[v, i, r] = keep(ok, slots[t, v * 4 + cell])
-    row, lane32 = iota((32, Z), 0), iota((32, Z), 1)
-    target = jnp.where(row < 16, 0, 10) + 16 * ((row % 16) // 4) + row % 4
-    place_lanes = onehot((lane32 == target) & (row % 4 < H))
+                    G[v, i, pl.ds(r, 1)] = keep(ok, slots[t, cell, pl.ds(v, 1)])
+    row, lane24 = iota((8 * H, Z), 0), iota((8 * H, Z), 1)
+    target = jnp.where(row < 4 * H, 0, 10 - H) + 16 * (row % 4) + row // 4
+    place_lanes = onehot(lane24 == target)
 
     def layers(dx, dy, lanes):
         below, above = (dx, dy, -1), (dx, dy, 1)
-        low = keep(place.has(below), slots[place.slot(below)])
-        high = keep(place.has(above), slots[place.slot(above)])
-        both = jnp.concatenate([low, high], axis=0)
-        return dot(both[:, lanes], place_lanes, TN)
+        low, high = place.slot(below), place.slot(above)
+        rows = [keep(place.has(below), slots[low, k]) for k in range(H)]
+        rows += [keep(place.has(above), slots[high, k]) for k in range(H)]
+        return dot(jnp.concatenate(rows, axis=0)[:, lanes], place_lanes, TN)
 
     everything = slice(0, X * Y)
     for i in (0, H + X + H - 1):
@@ -300,29 +299,28 @@
         both = U[2 * vp * per : (2 * vp + 1) * per] + roll(U[(2 * vp + 1) * per : (2 * vp + 2) * per], Z // 2, 1)
         p1[vp] = both.reshape(X // 2, Y // 2, Z)
     half = Z // 2
-    row, lane8 = iota((8, Z), 0), iota((8, Z), 1)
-    wanted = jnp.where(row < H, row, half - 2 * H + row)
-    faces = dot(onehot((lane8 == wanted) & (row < 2 * H)), U, NT)
-    gram_row = gram[0:1]
-    base = jnp.where(row == 6, gram_row, zero8)
-    faces = jnp.where(row < 6, faces, base)
+    row, lane16 = iota((16, Z), 0), iota((16, Z), 1)
+    wanted = jnp.where(row < 8, half - H, 0) + row % 8
+    faces = dot(onehot((lane16 == wanted) & (row % 8 < H)), U, NT)
+    row = iota((8, Z), 0)
+    base = jnp.where(row == GRAM_ROW, gram[0:1], zero8)
+    base = jnp.where(row == C_ROW, c2p[0:1], jnp.where(row == C_ROW + 1, c2p[1:2], base))
     fill_slots(slots1, counts[0] * counts[1] * counts[2], base, 8)
-    X1, Y1 = X // 2, Y // 2
+    up, down = jnp.where(row < H, faces[0:8], base), jnp.where(row < H, faces[8:16], base)
     for dx in (-1, 0, 1):
         for dy in (-1, 0, 1):
-            slots1[place.slot((dx, dy, 1))] = faces
-            slots1[place.slot((dx, dy, -1))] = faces
-            if dx and dy:
-                t = place.slot((dx, dy, 0))
-                for vp in range(V // 2):
-                    slots1[t, vp] = p1[vp, X1 - 1 if dx > 0 else 0, Y1 - 1 if dy > 0 else 0]
-
-
-EDGE = ((0, 0), (0, 1), (1, 0))
-
-
-def edge_steps(merge_y):
-    return [(dx, dy) for dx in (1, -1) for dy in ((0,) if merge_y else (1, -1))]
+            slots1[place.slot((dx, dy, 1))] = up
+            slots1[place.slot((dx, dy, -1))] = down
+    X1, Y1 = X // 2, Y // 2
+    for ref, (dx, dy) in zip(edges, edge_steps(merge_y)):
+        for cell, (a, b) in enumerate(EDGE1):
+            x = X1 - 1 - a if dx > 0 else a
+            if dy == 0:
+                y = jnp.where(place.at[1] == 0, Y1 - 1 - b, b)
+            else:
+                y = Y1 - 1 - b if dy > 0 else b
+            for vp in range(V // 2):
+                ref[pl.ds(cell * (V // 2) + vp, 1)] = p1[vp, x, pl.ds(y, 1)]
 
 
 def coarse_masks(place, R, Z):
@@ -341,8 +339,8 @@
     return spread(cur, get(i - 1), get(i + 1), roll(cur, 1, 1), roll(cur, -1, 1))
 
 
-def third_kernel(counts, merge_y, p1, c1, xl, xh, yl, yh, slots, c2p, G1, S1, slots2, *refs):
-    edges, Q = refs[:-1], refs[-1]
+def third_kernel(counts, merge_y, p1, c1, xl, xh, yl, yh, slots, c2p, *refs):
+    edges, (G1, S1, slots2, Q) = refs[:-4], refs[-4:]
     VP, X, Y, Z = p1.shape
     V, R, half = 2 * VP, 2 * Y, Z // 2
     place = Place(counts)
@@ -353,9 +351,8 @@
         return jnp.where(lane < half, roll(tile, half, 1) if v % 2 else tile, zero)
 
     r16, l16 = iota((16, Z), 0), iota((16, Z), 1)
-    target = jnp.where(r16 < 8, Z - 2 * H + r16, half + r16 - 8)
-    used = ((r16 >= H) & (r16 < 2 * H)) | ((r16 >= 8) & (r16 < 8 + H))
-    place_lanes = onehot((l16 == target) & used)
+    target = jnp.where(r16 < 8, Z - H, half) + r16 % 8
+    place_lanes = onehot((l16 == target) & (r16 % 8 < H))
 
     def layers(dx, dy):
         below, above = (dx, dy, -1), (dx, dy, 1)
@@ -390,33 +387,25 @@
                 if a < 2:
                     tile = jnp.where(m_hi, tile_of(up, v, x), jnp.where(m_lo, tile_of(down, v, x), zero))
                 G1[v, i, Y:R] = tile
-        for dy in (-1, 1):
-            ok, t = place.has((dx, dy, 0)), place.slot((dx, dy, 0))
-            i = H + X if dx > 0 else H - 1
-            r = Y if dy > 0 else R - 1
-            for v in range(V):
-                line = slots[t, pl.ds(v // 2, 1)]
-                line = roll(line, half, 1) if v % 2 else line
-                line = jnp.where(lane[0:1] < half, line, jnp.zeros((1, Z), jnp.float32))
-                G1[v, i, pl.ds(r, 1)] = G1[v, i, pl.ds(r, 1)] + keep(ok, line)
+    for ref, (sx, sy) in zip(edges, edge_steps(merge_y)):
+        dx = -sx
+        for dy in (-1, 1) if sy == 0 else (-sy,):
+            ok = place.has((dx, dy, 0))
+            for cell, (a, b) in enumerate(EDGE1):
+                i = H + X + a if dx > 0 else H - 1 - a
+                r = Y + b if dy > 0 else R - 1 - b
+                for v in range(V):
+                    line = ref[pl.ds(cell * VP + v // 2, 1)]
+                    line = roll(line, half, 1) if v % 2 else line
+                    use = jnp.logical_and(lane[0:1] < half, ok)
+                    line = jnp.where(use, line, jnp.zeros((1, Z), jnp.float32))
+                    G1[v, i, pl.ds(r, 1)] = G1[v, i, pl.ds(r, 1)] + line
     mask = coarse_masks(place, R, Z)
     for i in range(1, 2 * H + X - 1):
         m = scaled(x_flag(place, i, X), mask)
         for v in range(V):
             get = lambda j: G1[v, j]
             S1[v, i] = m * (PRE_G * G1[v, i] + PRE_N * level1_sum(get, i))
-    for ref, (dx, dy) in zip(edges, edge_steps(merge_y)):
-        for cell, (a, b) in enumerate(EDGE):
-            i = H + X - 1 - a if dx > 0 else H + a
-            if dy == 0:
-                y = jnp.where(place.at[1] == 0, Y - 1 - b, b)
-            else:
-                y = Y - 1 - b if dy > 0 else b
-            for vp in range(VP):
-                one, two = S1[2 * vp, i, pl.ds(y, 1)], S1[2 * vp + 1, i, pl.ds(y, 1)]
-                ref[pl.ds(cell * VP + vp, 1)] = jnp.where(lane[0:1] < half, one, roll(two, half, 1))
-                if cell:
-                    ref[pl.ds((2 + cell) * VP + vp, 1)] = p1[vp, i - H, pl.ds(y, 1)]
     for x in range(X // 2):
         for v in range(V):
             total = None
@@ -437,116 +426,125 @@
     fill_slots(slots2, counts[0] * counts[1] * counts[2], msg, 8)
 
 
-def coarse_kernel(counts, parts_y, slots0, slots2, out, W, pre):
+def grid_of(count_y, count_x, fn):
+    return [[fn(y, x) for x in range(count_x)] for y in range(count_y)]
+
+
+def assemble(counts, parts_y, tile, lane):
     nx, ny, nz = counts
-    Z = 128
+    width = lane.shape[1] // parts_y
+
+    def one(y, x):
+        y, j = y // parts_y, y % parts_y
+        acc = roll(tile[(x * ny + y) * nz], -width * j, 1)
+        for z in range(1, nz):
+            acc = jnp.where(lane // width == z, roll(tile[(x * ny + y) * nz + z], width * (z - j), 1), acc)
+        return acc
+
+    return grid_of(ny * parts_y, nx, one)
+
+
+def combine(fn, *grids):
+    return [[fn(*ts) for ts in zip(*lines)] for lines in zip(*grids)]
+
+
+def add(*terms):
+    total = None
+    for term in terms:
+        if term is not None:
+            total = term if total is None else total + term
+    return total
+
+
+def shrink_tiles(v, level, odd, lane):
+    step = 2 ** (level - 2)
+    v = [[a + b for a, b in zip(v[2 * y], v[2 * y + 1])] for y in range(len(v) // 2)]
+    if level == 2:
+        v = combine(lambda t: t + jnp.where(odd, roll(t, 1, 0), roll(t, -1, 0)), v)
+    else:
+        v = [[line[2 * x] + line[2 * x + 1] for x in range(len(line) // 2)] for line in v]
+    upper = (lane // step) % 2 == 1
+    return combine(lambda t: 0.125 * (t + jnp.where(upper, roll(t, step, 1), roll(t, -step, 1))), v)
+
+
+def weights_kernel(counts, parts_y, slots1, *outs):
+    lane = iota((8, outs[0].shape[-1]), 1)
+    odd = iota(lane.shape, 0) % 2 == 1
+    count = counts[0] * counts[1] * counts[2]
+    rows = [jnp.where(odd, slots1[t, pl.ds(C_ROW + 1, 1)], slots1[t, pl.ds(C_ROW, 1)]) for t in range(count)]
+    c = assemble(counts, parts_y, rows, lane)
+    level = 2
+    refs = list(outs)
+    while True:
+        ref = refs.pop(0)
+        for y in range(len(c)):
+            for x in range(len(c[0])):
+                ref[y, x] = (0.25**level) * c[y][x]
+                if level > 2:
+                    inverse[y, x] = 1.0 / ((6.0 * 0.25**level) * c[y][x])
+        if level == LEVELS - 1:
+            return
+        c = shrink_tiles(c, level, odd, lane)
+        level += 1
+        inverse = refs.pop(0)
+
+
+def coarse_kernel(counts, parts_y, slots2, *refs):
+    *weights, out, W, pre = refs
+    nx, ny, nz = counts
+    Z = slots2.shape[2]
     place = Place(counts)
     width = Z // parts_y
-    row, lane = iota((8, Z), 0), iota((8, Z), 1)
-    odd = row % 2 == 1
+    lane = iota((8, Z), 1)
+    odd = iota((8, Z), 0) % 2 == 1
     zero = jnp.zeros((8, Z), jnp.float32)
-
-    def assemble(tile):
-        grid = []
-        for y in range(ny):
-            for j in range(parts_y):
-                line = []
-                for x in range(nx):
-                    acc = zero
-                    for z in range(nz):
-                        moved = roll(tile[(x * ny + y) * nz + z], width * (z - j), 1)
-                        acc = jnp.where(lane // width == z, moved, acc)
-                    line.append(acc)
-                grid.append(line)
-        return grid
-
-    count = nx * ny * nz
-    g2 = assemble([slots2[t] for t in range(count)])
-    c2 = assemble([jnp.where(odd, slots0[t, pl.ds(7, 1)], slots0[t, pl.ds(3, 1)]) for t in range(count)])
+    inverse = {3 + i: weights[1 + 2 * i] for i in range(LEVELS - 3)}
+    scale = {2: weights[0], **{3 + i: weights[2 + 2 * i] for i in range(LEVELS - 3)}}
 
     def at(v, y, x):
         inside = 0 <= y < len(v) and 0 <= x < len(v[0])
         return v[y][x] if inside else None
 
-    def add(*terms):
-        total = None
-        for term in terms:
-            if term is not None:
-                total = term if total is None else total + term
-        return total
-
-    def neighbours(v, level, length):
-        rows = [[roll(t, -1, 0) for t in line] for line in v] if level == 2 else None
+    def neighbours(v, level):
+        step = 2 ** (level - 2)
+        ahead = [[roll(t, -1, 0) for t in line] for line in v] if level == 2 else None
         back = [[roll(t, 1, 0) for t in line] for line in v] if level == 2 else None
-        result = []
-        for y in range(len(v)):
-            line = []
-            for x in range(len(v[0])):
-                t = v[y][x]
-                zs = jnp.where(lane == 0, zero, roll(t, 1, 1)) + jnp.where(lane == length - 1, zero, roll(t, -1, 1))
-                ys = add(zs, at(v, y - 1, x), at(v, y + 1, x))
-                if level == 2:
-                    xs = jnp.where(odd, add(back[y][x], at(back, y, x + 1)), add(rows[y][x], at(rows, y, x - 1)))
-                    line.append(ys + xs)
-                else:
-                    line.append(add(ys, at(v, y, x - 1), at(v, y, x + 1)))
-            result.append(line)
-        return result
-
-    def combine(fn, *grids):
-        return [[fn(*ts) for ts in zip(*lines)] for lines in zip(*grids)]
-
-    li, lo = iota((Z, Z), 0), iota((Z, Z), 1)
-    halve = onehot(lo == li // 2, 0.125)
-    double = onehot(li == lo // 2)
-
-    def lanes(grid, matrix):
-        flat = [t for line in grid for t in line]
-        moved = dot(jnp.concatenate(flat, axis=0) if len(flat) > 1 else flat[0], matrix)
-        w = len(grid[0])
-        return [[moved[(y * w + x) * 8 : (y * w + x + 1) * 8] for x in range(w)] for y in range(len(grid))]
-
-    def shrink(v, level):
-        v = [[a + b for a, b in zip(v[2 * y], v[2 * y + 1])] for y in range(len(v) // 2)]
-        if level == 2:
-            v = combine(lambda t: t + jnp.where(odd, roll(t, 1, 0), roll(t, -1, 0)), v)
-        else:
-            v = [[line[2 * x] + line[2 * x + 1] for x in range(len(line) // 2)] for line in v]
-        return lanes(v, halve)
+
+        def one(y, x):
+            t = v[y][x]
+            zs = jnp.where(lane < step, zero, roll(t, step, 1)) + jnp.where(lane >= Z - step, zero, roll(t, -step, 1))
+            ys = add(zs, at(v, y - 1, x), at(v, y + 1, x))
+            if level > 2:
+                return add(ys, at(v, y, x - 1), at(v, y, x + 1))
+            return ys + jnp.where(
+                odd, add(back[y][x], at(back, y, x + 1)), add(ahead[y][x], at(ahead, y, x - 1))
+            )
+
+        return grid_of(len(v), len(v[0]), one)
 
     def grow(v, level):
-        v = lanes(v, double)
         v = [line for line in v for _ in range(2)]
         return v if level == 2 else [[t for t in line for _ in range(2)] for line in v]
 
-    def sweep(v, g, level, length):
-        return combine(lambda a, b, s: KEEP * a + OMEGA * b + SIXTH * s, v, g, neighbours(v, level, length))
-
-    def cycle(g, cs, level, length):
-        last = level == LEVELS - 1
-        if last:
+    def sweep(v, g, level):
+        return combine(lambda a, b, s: KEEP * a + OMEGA * b + SIXTH * s, v, g, neighbours(v, level))
+
+    def cycle(g, level):
+        if level == LEVELS - 1:
             v = combine(lambda b: OMEGA * b, g)
             for _ in range(COARSE_SWEEPS - 1):
-                v = sweep(v, g, level, length)
+                v = sweep(v, g, level)
             return v
-        v = combine(lambda b, s: PRE_G * b + PRE_N * s, g, neighbours(g, level, length))
-        if level > 2:
-            v = combine(lambda t: jnp.where(lane < length, t, zero), v)
-        factor = 0.25**level
-        r = combine(
-            lambda c, b, a, s: (factor * c) * (6.0 * (b - a) + s), cs, g, v, neighbours(v, level, length)
-        )
-        down = shrink(r, level)
-        c_down = shrink(cs, level)
-        inner = lane < length // 2
-        d = 6.0 * 0.25 ** (level + 1)
-        g_down = combine(lambda b, c: jnp.where(inner, b / (d * jnp.where(inner, c, 1.0)), zero), down, c_down)
-        e = grow(cycle(g_down, c_down, level + 1, length // 2), level)
-        v = combine(lambda a, b: a + b, v, e)
-        v = sweep(v, g, level, length)
-        return combine(lambda t: jnp.where(lane < length, t, zero), v) if level > 2 else v
-
-    v = cycle(g2, c2, 2, width * nz)
+        v = combine(lambda b, s: PRE_G * b + PRE_N * s, g, neighbours(g, level))
+        c = grid_of(len(g), len(g[0]), lambda y, x: scale[level][y, x])
+        r = combine(lambda c, b, a, s: c * (6.0 * (b - a) + s), c, g, v, neighbours(v, level))
+        down = shrink_tiles(r, level, odd, lane)
+        down = grid_of(len(down), len(down[0]), lambda y, x: down[y][x] * inverse[level + 1][y, x])
+        v = combine(lambda a, b: a + b, v, grow(cycle(down, level + 1), level))
+        return sweep(v, g, level)
+
+    count = nx * ny * nz
+    v = cycle(assemble(counts, parts_y, [slots2[t] for t in range(count)], lane), 2)
     for y in range(len(v)):
         for x in range(nx):
             W[y, x] = v[y][x]
@@ -562,14 +560,14 @@
             y = jnp.clip(y, 0, ny * parts_y - 1)
             for vec in range(4):
                 pre[vec, xw, pl.ds(j % 8, 1)] = keep(ok, W[y, x, pl.ds(vec * 2 + (xw + 1) % 2, 1)])
+    li, lo = iota((Z, Z), 0), iota((Z, Z), 1)
     z1 = jnp.where(lo < 96, lo, lo - Z)
     window = onehot(li == iz * width + jnp.floor_divide(z1 + 2, 2) - 1)
     moved = dot(pre[...].reshape(4 * 4 * 8, Z), window)
     out[...] = moved.reshape(4, 4, 8, Z)
 
 
-def last_kernel(counts, merge_y, e2, G1, S1, G, S, c, *refs):
-    edges, (pre, op, E1, C1, E0, C0) = refs[:-6], refs[-6:]
+def last_kernel(counts, e2, G1, S1, G, S, c, pre_hbm, op_hbm, E1, C1, E0, C0, pre, op, sems):
     V, X1, Y1, Z = e2.shape[0], S1.shape[1] - 2 * H, S1.shape[2] // 2, S1.shape[3]
     X, Y = 2 * X1, 2 * Y1
     R1, R = 2 * Y1, Y + 8
@@ -583,31 +581,6 @@
     for v in range(V):
         for i in range(1, 2 * H + X1 - 1):
             C1[v, i] = S1[v, i] + E1[pl.ds((v * X1 + (i - 1) // 2) * R1, R1)]
-    half = Z // 2
-    lane = iota((1, Z), 1)
-    for ref, (sx, sy) in zip(edges, edge_steps(merge_y)):
-        dx = -sx
-        for dy in (-1, 1) if sy == 0 else (-sy,):
-            ok = place.has((dx, dy, 0))
-            for cell, (a, b) in enumerate(EDGE):
-                i = H + X1 + a if dx > 0 else H - 1 - a
-                r = Y1 + b if dy > 0 else R1 - 1 - b
-                for v in range(V):
-                    line = ref[pl.ds(cell * (V // 2) + v // 2, 1)]
-                    line = roll(line, half, 1) if v % 2 else line
-                    line = line + E1[pl.ds((v * X1 + (i - 1) // 2) * R1 + r, 1)]
-                    use = jnp.logical_and(lane < half, ok)
-                    C1[v, i, pl.ds(r, 1)] = jnp.where(use, line, C1[v, i, pl.ds(r, 1)])
-                    if cell:
-                        line = ref[pl.ds((2 + cell) * (V // 2) + v // 2, 1)]
-                        line = roll(line, half, 1) if v % 2 else line
-                        ii, rr = i, r
-                        if a:
-                            rr = Y1 - 1 if dy > 0 else 0
-                        else:
-                            ii = H + X1 - 1 if dx > 0 else H
-                        line = jnp.where(use, PRE_N * line, jnp.zeros_like(line))
-                        C1[v, ii, pl.ds(rr, 1)] = C1[v, ii, pl.ds(rr, 1)] + line
     mask = coarse_masks(place, R1, Z)
     n = X1 + 2
     fine = []
@@ -620,6 +593,7 @@
         fine.append(jnp.concatenate(tiles, axis=0))
     li, lo = iota((Z, Z), 0), iota((Z, Z), 1)
     double = onehot(li == lo // 2)
+    half = Z // 2
     k = lo % 8
     low_side = (lo // 8) % 2 == 0
     source = jnp.where(low_side, jnp.where(k < H, Z - 1, 0), jnp.where(k < 2, half - 1, half))
@@ -651,6 +625,8 @@
             E0[pl.ds((v * (X + 2) + i - H + 1) * R, R)] = value
             if v < V and H <= i < H + X:
                 pre[v, i - H] = value[0:Y]
+    copies = [pltpu.make_async_copy(pre, pre_hbm, sems.at[0])]
+    copies[0].start()
 
     class View:
         def __getitem__(self, key):
@@ -662,9 +638,15 @@
         for v in range(V):
             around = fine_sum(view, v, H + x, V, lane)
             op[v, x] = c[x] * (6.0 * view[v, H + x][0:Y] - around[0:Y])
-
-
-def gram_kernel(old, prev, out):
+        if x % 2:
+            part = slice(x - 1, x + 1)
+            copies.append(pltpu.make_async_copy(op.at[:, part], op_hbm.at[:, part], sems.at[1 + x // 2]))
+            copies[-1].start()
+    for copy in copies:
+        copy.wait()
+
+
+def gram_kernel(old, prev, c, out, c2p):
     M, X, Y, Z = old.shape
     J = prev.shape[0]
     pairs = [(a, b) for a in range(M + J) for b in range(a, M + J)]
@@ -680,17 +662,29 @@
     rows = jnp.concatenate([jnp.sum(s, axis=0, keepdims=True) for s in sums], axis=0)
     pad = jnp.zeros((Z - len(pairs), Z), jnp.float32)
     out[...] = dot(ones, jnp.concatenate([rows, pad], axis=0), NT)
+    ny2, nz2 = Y // 4, Z // 4
+    sub, li, lo = iota((8, Z), 0), iota((Z, Z), 0), iota((Z, Z), 1)
+    total = None
+    for y in range(ny2):
+        sums = []
+        for x in range(X // 4):
+            quad = c[4 * x] + c[4 * x + 1] + c[4 * x + 2] + c[4 * x + 3]
+            sums.append(jnp.sum(quad[4 * y : 4 * y + 4], axis=0, keepdims=True))
+        rows = jnp.where(sub % 2 == 0, sums[0], sums[1])
+        part = dot(rows, onehot(lo == y * nz2 + li // 4, 1.0 / 64.0))
+        total = part if total is None else total + part
+    c2p[...] = total
 
 
 def ortho_kernel(count, cells, old, prev, slots, orth, proj, tri):
     M, X, Y, Z = old.shape
     J = prev.shape[0]
     if count <= 64:
-        total = slots[0, pl.ds(6, 1)]
+        total = slots[0, pl.ds(GRAM_ROW, 1)]
         for t in range(1, count):
-            total = total + slots[t, pl.ds(6, 1)]
+            total = total + slots[t, pl.ds(GRAM_ROW, 1)]
     else:
-        total = lax.fori_loop(0, count, lambda t, s: s + slots[t, pl.ds(6, 1)], jnp.zeros((1, Z), jnp.float32))
+        total = lax.fori_loop(0, count, lambda t, s: s + slots[t, pl.ds(GRAM_ROW, 1)], jnp.zeros((1, Z), jnp.float32))
     total = jnp.broadcast_to(total, (8, Z)) / cells
     value = {}
     p = 0
@@ -761,13 +755,21 @@
                 orth[j, x, y : y + 8] = s
 
 
-def run(kernel, shapes, args, scratch=(), name=None):
+def run(near, kernel, shapes, args, scratch=(), name=None, result=(), plain=(), sems=0, out_sems=0):
+    outs = []
+    for i, shape in enumerate(shapes):
+        kind = jax.ShapeDtypeStruct if i in result or not near else pltpu.VMEM
+        outs.append(kind(shape, jnp.float32))
+    if near:
+        spaces = [pltpu.HBM if sems else None if i in plain else pltpu.VMEM for i in range(len(args))]
+        args = [pltpu.with_memory_space_constraint(a, m) if m else a for a, m in zip(args, spaces)]
     fn = pl.pallas_call(
         kernel,
-        out_shape=[jax.ShapeDtypeStruct(s, jnp.float32) for s in shapes],
-        in_specs=[VM] * len(args),
-        out_specs=[VM] * len(shapes),
-        scratch_shapes=[pltpu.VMEM(s, jnp.float32) for s in scratch],
+        out_shape=outs,
+        in_specs=[HB if sems else VM] * len(args),
+        out_specs=[HB if out_sems and i in result else VM for i in range(len(shapes))],
+        scratch_shapes=[pltpu.VMEM(s, jnp.float32) for s in scratch] + [pltpu.SemaphoreType.DMA((sems + out_sems,))] * (sems + out_sems > 0),
+        compiler_params=pltpu.CompilerParams(vmem_limit_bytes=16 * 2**20) if near else None,
         name=name,
     )
     return fn(*args)
@@ -789,7 +791,7 @@
     return lax.all_to_all(slots, AXES, split_axis=0, concat_axis=0, tiled=True)
 
 
-def wide_coarse(counts, parts_y, slots0, slots2):
+def wide_coarse(counts, parts_y, slots1, slots2):
     nx, ny, nz = counts
     Z = slots2.shape[2]
     width = Z // parts_y
@@ -804,7 +806,7 @@
         return t.transpose(0, 2, 1, 3, 4).reshape(lead, nx * 2, ny * parts_y, nz * width)
 
     g2 = whole(slots2, 4)
-    c2 = whole(jnp.stack([slots0[:, 3], slots0[:, 7]], axis=1), 1)
+    c2 = whole(slots1[:, C_ROW : C_ROW + 2], 1)
 
     def around(v):
         p = jnp.pad(v, ((0, 0), (1, 1), (1, 1), (1, 1)))
@@ -856,69 +858,87 @@
     V, X, Y, Z = inc.shape
     count = counts[0] * counts[1] * counts[2]
     merge_y = counts[1] == 2
+    near = count <= 64
     R = Y + 8
     X1, Y1 = X // 2, Y // 2
     y_shape = (V, X // 2, 8, Z)
     shapes = [(V, X, Y, Z), (V, H, Y, Z), (V, H, Y, Z), y_shape]
     shapes += [] if merge_y else [y_shape]
-    shapes += [(count, 16, Z), (8, Z)]
-    outs = run(functools.partial(first_kernel, counts, merge_y), shapes, (inc, c), name="first")
+    shapes += [(count, H, V, Z)]
+    outs = run(near, functools.partial(first_kernel, counts, merge_y), shapes, (inc, c), [inc.shape, c.shape], name="first", plain=(0, 1), result=(len(shapes) - 1,), sems=V + 1)
     g, xlo, xhi = outs[:3]
-    slots0, c2p = outs[-2:]
-    slots0 = swap(slots0)
+    slots0 = swap(outs[-1])
     xl, xh = shift(xhi, "gx", 1), shift(xlo, "gx", -1)
     if merge_y:
         yl = yh = shift(outs[3], "gy", 1)
     else:
         yl, yh = shift(outs[4], "gy", 1), shift(outs[3], "gy", -1)
-    (gram,) = run(gram_kernel, [(8, Z)], (old, prev), name="gram")
+    gram, c2p = run(near, gram_kernel, [(8, Z), (8, Z)], (old, prev, c), name="gram", plain=(0, 1))
     ext0, ext1 = (V + 1, X + 2 * H, R, Z), (V, X1 + 2 * H, 2 * Y1, Z)
-    G, S, p1, slots1, c1 = run(
-        functools.partial(second_kernel, counts),
-        [ext0, ext0, (V // 2, X1, Y1, Z), (count, 8, Z), (X1, Y1, Z)],
-        (g, c, xl, xh, yl, yh, slots0, gram),
+    steps = edge_steps(merge_y)
+    G, S, p1, slots1, c1, *edges = run(
+        near,
+        functools.partial(second_kernel, counts, merge_y),
+        [ext0, ext0, (V // 2, X1, Y1, Z), (count, 8, Z), (X1, Y1, Z)] + [(16, Z)] * len(steps),
+        (g, c, xl, xh, yl, yh, slots0, gram, c2p),
         [(V * X1 * Y, Z), (X1 * Y, Z)],
         name="second",
+        result=(3,),
     )
     slots1 = swap(slots1)
+    edges = [diagonal(counts, e, dx, dy) for e, (dx, dy) in zip(edges, steps)]
     xl, xh = shift(p1, "gx", 1), shift(p1, "gx", -1)
     if merge_y:
         yl = yh = shift(p1, "gy", 1)
     else:
         yl, yh = shift(p1, "gy", 1), shift(p1, "gy", -1)
-    steps = edge_steps(merge_y)
-    G1, S1, slots2, *edges = run(
+    G1, S1, slots2 = run(
+        near,
         functools.partial(third_kernel, counts, merge_y),
-        [ext1, ext1, (count, 8, Z)] + [(16, Z)] * len(steps),
-        (p1, c1, xl, xh, yl, yh, slots1, c2p),
+        [ext1, ext1, (count, 8, Z)],
+        (p1, c1, xl, xh, yl, yh, slots1, c2p, *edges),
         [(V * X1 // 2 * Y1, Z)],
         name="third",
+        result=(2,),
     )
     slots2 = swap(slots2)
-    edges = [diagonal(counts, e, dx, dy) for e, (dx, dy) in zip(edges, steps)]
     orth, proj, tri = run(
+        near,
         functools.partial(ortho_kernel, count, float(count * X * Y * Z)),
         [(V, X, Y, Z), (4, 4), (4, 4)],
         (old, prev, slots1),
         name="ortho",
+        result=(0, 1, 2),
+        plain=(0, 1),
     )
     parts_y = Y // 4
-    if counts[2] * (Z // parts_y) == Z and count <= 64:
+    if near and counts[2] * (Z // parts_y) == Z:
+        sizes = [(counts[1] * parts_y, counts[0], 8, Z)]
+        for level in range(3, LEVELS):
+            y, x = sizes[-1][:2]
+            sizes += [(y // 2, x if level == 3 else x // 2, 8, Z)] * 2
+        weights = run(
+            near, functools.partial(weights_kernel, counts, parts_y), sizes, (slots1,), name="weights"
+        )
         (e2,) = run(
+            near,
             functools.partial(coarse_kernel, counts, parts_y),
             [(V, 4, 8, Z)],
-            (slots0, slots2),
-            [(counts[1] * parts_y, counts[0], 8, Z), (V, 4, 8, Z)],
+            (slots2, *weights),
+            [sizes[0], (V, 4, 8, Z)],
             name="coarse",
         )
     else:
-        e2 = wide_coarse(counts, parts_y, slots0, slots2)
+        e2 = wide_coarse(counts, parts_y, slots1, slots2)
     pre, op = run(
-        functools.partial(last_kernel, counts, merge_y),
+        near,
+        functools.partial(last_kernel, counts),
         [(V, X, Y, Z), (V, X, Y, Z)],
-        (e2, G1, S1, G, S, c, *edges),
-        [(V * X1 * 2 * Y1, Z), ext1, ((V + 1) * (X + 2) * R, Z), ext0],
+        (e2, G1, S1, G, S, c),
+        [(V * X1 * 2 * Y1, Z), ext1, ((V + 1) * (X + 2) * R, Z), ext0, (V, X, Y, Z), (V, X, Y, Z)],
         name="last",
+        result=(0, 1),
+        out_sems=1 + X // 2,
     )
     return orth, proj, tri, pre, op
 

time: 61.7 us -> 52.5 us (0.85)
  Pallas kernels: 21.7 us -> 12.9 us
  local copies, waits for them, and re-layouts: 2.63 us -> 0.02 us
  starting transfers between devices: 23.5 us -> 25.6 us
    pallas_call x7 -> x8, Pallas kernels: 21.7 us -> 12.9 us  [run(): return fn(*args)]
    unnamed x34 -> x6, local copies, waits for them, and re-layouts: 2.63 us -> 0.02 us
    all_to_all x3, starting transfers between devices: 13.8 us -> 15.8 us  [swap(): return lax.all_to_all(slots, AXES, split_axis=0, concat_axis=0, tiled=True)]
    ppermute x2, waiting for transfers between devices: 0.01 us -> 1.42 us  [diagonal(): return lax.ppermute(value, ('gx', 'gy'), pairs)]
    ppermute x6, waiting for transfers between devices: 3.3 us -> 2.32 us  [shift(): return lax.ppermute(value, axis, [(i, (i + step) % n) for i in range(n)])]
  transfers between devices with their start and end apart: 11 -> 11, of which waited for: 5 -> 5; matrix products, arithmetic and copies ran while one was open for 0% -> 0% of each run, Pallas kernels for 14% -> 4%
where the time goes in v2:
time: 52.5 us; the launch traced here: 52.1 us
  starting transfers between devices  25.6 us (49%)
  Pallas kernels  12.9 us (25%)
  waiting for transfers between devices  12.9 us (25%)
  between operations  0.72 us (1%)
    all_to_all x3, starting transfers between devices, swap(): return lax.all_to_all(slots, AXES, split_axis=0, concat_axis=0, tiled=True)  15.8 us
    pallas_call x8, Pallas kernels, run(): return fn(*args)  12.9 us
    all_to_all x3, waiting for transfers between devices, swap(): return lax.all_to_all(slots, AXES, split_axis=0, concat_axis=0, tiled=True)  9.21 us
    ppermute x6, starting transfers between devices, shift(): return lax.ppermute(value, axis, [(i, (i + step) % n) for i in range(n)])  7.13 us
    ppermute x2, starting transfers between devices, diagonal(): return lax.ppermute(value, ('gx', 'gy'), pairs)  2.64 us
    ppermute x6, waiting for transfers between devices, shift(): return lax.ppermute(value, axis, [(i, (i + step) % n) for i in range(n)])  2.32 us
    ppermute x2, waiting for transfers between devices, diagonal(): return lax.ppermute(value, ('gx', 'gy'), pairs)  1.42 us
  transfers between devices with their start and end apart: 11, of which 5 were waited for; matrix products, arithmetic and copies ran while one was open for 0% of the time, Pallas kernels for 4%

profile of v2, /device:TPU:0, one launch (start us, length us, event | category | flops | bytes accessed | tf_op | source)
XLA Modules:
  0.0 52.1 jit_solution(15946928684525760926)
XLA Ops:
  0.6 2.8 %first.1 = (f32[4,8,16,128]{3,2,1,0:T(8,128)S(1)}, f32[4,3,16,128]{3,2,1,0:T(8,128)S(1)}, f32[4,3,16,128]{3,2,1,0:T(8,128)S(1)}, f32[4,4,8,128]{3,2,1,0:T(8,128)S(1)}, f32[32,3,4,128]{3,2,1,0:T(4,128)}) custom-call(f32[4,8,16,128]{3,2,1,0:T(8,128)} %inc_hbm.1, f32[8,16,128]{2,1,0:T(8,128)} %c.5), custom_call_target="tpu_custom_call" | custom-call | tf_op jit(solution)/shard_map/first/pallas_call | solution.py:775
  3.4 0.0 copy-start.2
  3.4 7.3 %all-to-all-start = ((f32[32,3,4,128]{3,2,1,0:T(4,128)}), f32[32,3,4,128]{3,2,1,0:T(4,128)S(1)}, u32[]{:S(2)}, u32[]{:S(2)}) async-start(f32[32,3,4,128]{3,2,1,0:T(4,128)} %get-tuple-element.38), calls=%async_computation | async-start | bytes 393216 | tf_op jit(solution)/shard_map/all_to_all | solution.py:791
  10.8 0.3 collective-permute-start
  11.1 1.5 %collective-permute-start.1 = (f32[4,3,16,128]{3,2,1,0:T(8,128)S(1)}, f32[4,3,16,128]{3,2,1,0:T(8,128)S(1)}, u32[]{:S(2)}, u32[]{:S(2)}) collective-permute-start(f32[4,3,16,128]{3,2,1,0:T(8,128)S(1)} %get-tuple-element.36), channel_id=1, source_target_pairs={{0,24},{8,0},{16,8},{24,16},{1,25},{9,1},{17,9},{25,17},{2,26},{10... | collective-permute-start | bytes 294920 | tf_op jit(solution)/shard_map/ppermute | solution.py:780
  12.6 1.8 %collective-permute-start.2 = (f32[4,4,8,128]{3,2,1,0:T(8,128)S(1)}, f32[4,4,8,128]{3,2,1,0:T(8,128)S(1)}, u32[]{:S(2)}, u32[]{:S(2)}) collective-permute-start(f32[4,4,8,128]{3,2,1,0:T(8,128)S(1)} %get-tuple-element.37), channel_id=1, source_target_pairs={{0,4},{4,0},{1,5},{5,1},{2,6},{6,2},{3,7},{7,3},{8,12},{12,8},{9,1... | collective-permute-start | bytes 196616 | tf_op jit(solution)/shard_map/ppermute | solution.py:780
  14.4 0.5 gram.1
  14.9 2.3 %collective-permute-done.2.yl.yh = f32[4,4,8,128]{3,2,1,0:T(8,128)S(1)} collective-permute-done((f32[4,4,8,128]{3,2,1,0:T(8,128)S(1)}, f32[4,4,8,128]{3,2,1,0:T(8,128)S(1)}, u32[]{:S(2)}, u32[]{:S(2)}) %collective-permute-start.2) | collective-permute-done | bytes 65568 | tf_op jit(solution)/shard_map/ppermute | solution.py:780
  17.2 2.7 %all-to-all-done.slots = f32[32,3,4,128]{3,2,1,0:T(4,128)S(1)} async-done(((f32[32,3,4,128]{3,2,1,0:T(4,128)}), f32[32,3,4,128]{3,2,1,0:T(4,128)S(1)}, u32[]{:S(2)}, u32[]{:S(2)}) %all-to-all-start) | async-done | bytes 196640 | tf_op jit(solution)/shard_map/all_to_all | solution.py:791
  19.8 2.6 %second.1 = (f32[5,14,24,128]{3,2,1,0:T(8,128)S(1)}, f32[5,14,24,128]{3,2,1,0:T(8,128)S(1)}, f32[2,4,8,128]{3,2,1,0:T(8,128)S(1)}, f32[32,8,128]{2,1,0:T(8,128)}...) custom-call(f32[4,8,16,128]{3,2,1,0:T(8,128)S(1)} %get-tuple-element.34.g, ...), custom_call_target="tpu_custom_call" | custom-call | tf_op jit(solution)/shard_map/second/pallas_call | solution.py:775
  22.4 2.9 %all-to-all-start.1 = ((f32[32,8,128]{2,1,0:T(8,128)}), f32[32,8,128]{2,1,0:T(8,128)S(1)}, u32[]{:S(2)}, u32[]{:S(2)}) async-start(f32[32,8,128]{2,1,0:T(8,128)} %get-tuple-element.41), calls=%async_computation.1 | async-start | bytes 262144 | tf_op jit(solution)/shard_map/all_to_all | solution.py:791
  25.3 0.3 collective-permute-start.3
  25.6 1.5 %collective-permute-start.4 = (f32[2,4,8,128]{3,2,1,0:T(8,128)S(1)}, f32[2,4,8,128]{3,2,1,0:T(8,128)S(1)}, u32[]{:S(2)}, u32[]{:S(2)}) collective-permute-start(f32[2,4,8,128]{3,2,1,0:T(8,128)S(1)} %get-tuple-element.45.p1), channel_id=1, source_target_pairs={{0,24},{8,0},{16,8},{24,16},{1,25},{9,1},{17,9},{25,17},{2,26},{10... | collective-permute-start | bytes 98312 | tf_op jit(solution)/shard_map/ppermute | solution.py:780
  27.1 1.8 %collective-permute-start.5 = (f32[2,4,8,128]{3,2,1,0:T(8,128)S(1)}, f32[2,4,8,128]{3,2,1,0:T(8,128)S(1)}, u32[]{:S(2)}, u32[]{:S(2)}) collective-permute-start(f32[2,4,8,128]{3,2,1,0:T(8,128)S(1)} %get-tuple-element.45.p1), channel_id=1, source_target_pairs={{0,4},{4,0},{1,5},{5,1},{2,6},{6,2},{3,7},{7,3},{8,12},{12,8},{9,1... | collective-permute-start | bytes 98312 | tf_op jit(solution)/shard_map/ppermute | solution.py:780
  28.9 2.6 %collective-permute-start.7 = (f32[16,128]{1,0:T(8,128)S(1)}, f32[16,128]{1,0:T(8,128)S(1)}, u32[]{:S(2)}, u32[]{:S(2)}) collective-permute-start(f32[16,128]{1,0:T(8,128)S(1)} %get-tuple-element.48), channel_id=1, source_target_pairs={{0,28},{4,24},{8,4},{12,0},{16,12},{20,8},{24,20},{28,16},{1,29},{... | collective-permute-start | bytes 24584 | tf_op jit(solution)/shard_map/ppermute | solution.py:787
  31.5 1.4 %collective-permute-done.6.refs_0_ = f32[16,128]{1,0:T(8,128)S(1)} collective-permute-done((f32[16,128]{1,0:T(8,128)S(1)}, f32[16,128]{1,0:T(8,128)S(1)}, u32[]{:S(2)}, u32[]{:S(2)}) %collective-permute-start.6) | collective-permute-done | bytes 8224 | tf_op jit(solution)/shard_map/ppermute | solution.py:787
  33.0 0.1 all-to-all-done.1.slots.slots1
  33.1 1.9 %third.1 = (f32[4,10,16,128]{3,2,1,0:T(8,128)S(1)}, f32[4,10,16,128]{3,2,1,0:T(8,128)S(1)}, f32[32,8,128]{2,1,0:T(8,128)}) custom-call(f32[2,4,8,128]{3,2,1,0:T(8,128)S(1)} %get-tuple-element.45.p1, f32[4,8,128]{2,1,0:T(8,128)S(1)} %get-tuple-element.46.c1, f32[2,4,8,128]{3,2,1,0:T(8,128)S(1)} %collective-permute-done.3.xl, ...), custom_call_target="tpu_custom_call" | custom-call | tf_op jit(solution)/shard_map/third/pallas_call | solution.py:775
  35.0 5.6 %all-to-all-start.2 = ((f32[32,8,128]{2,1,0:T(8,128)}), f32[32,8,128]{2,1,0:T(8,128)S(1)}, u32[]{:S(2)}, u32[]{:S(2)}) async-start(f32[32,8,128]{2,1,0:T(8,128)} %get-tuple-element.49), calls=%async_computation.2 | async-start | bytes 262144 | tf_op jit(solution)/shard_map/all_to_all | solution.py:791
  40.6 0.4 weights.1
  41.0 1.0 %ortho.1 = (f32[4,8,16,128]{3,2,1,0:T(8,128)}, f32[4,4]{1,0:T(4,128)}, f32[4,4]{1,0:T(4,128)}) custom-call(f32[4,8,16,128]{3,2,1,0:T(8,128)S(1)} %copy-done, f32[4,8,16,128]{3,2,1,0:T(8,128)S(1)} %copy-done.1, f32[32,8,128]{2,1,0:T(8,128)S(1)} %all-to-all-done.1.slots.slots1), custom_call_target="tpu_custom_call" | custom-call | tf_op jit(solution)/shard_map/ortho/pallas_call | solution.py:775
  42.0 6.4 %all-to-all-done.2.slots2 = f32[32,8,128]{2,1,0:T(8,128)S(1)} async-done(((f32[32,8,128]{2,1,0:T(8,128)}), f32[32,8,128]{2,1,0:T(8,128)S(1)}, u32[]{:S(2)}, u32[]{:S(2)}) %all-to-all-start.2) | async-done | bytes 131104 | tf_op jit(solution)/shard_map/all_to_all | solution.py:791
  48.4 1.6 %coarse.1.e2 = f32[4,4,8,128]{3,2,1,0:T(8,128)S(1)} custom-call(f32[32,8,128]{2,1,0:T(8,128)S(1)} %all-to-all-done.2.slots2, f32[8,4,8,128]{3,2,1,0:T(8,128)S(1)} %get-tuple-element.50.refs_0_, f32[4,4,8,128]{3,2,1,0:T(8,128)S(1)} %get-tuple-element.51.refs_1_, f32[4,4,8,128]{3,2,1,0:T(8,128)S(1)} %get-tuple-element.52.refs_2_, ...), custom_call_target="tpu_custom_call" | custom-call | tf_op jit(solution)/shard_map/coarse/pallas_call | solution.py:775
  50.0 2.1 %last.1 = (f32[4,8,16,128]{3,2,1,0:T(8,128)}, f32[4,8,16,128]{3,2,1,0:T(8,128)}) custom-call(f32[4,4,8,128]{3,2,1,0:T(8,128)S(1)} %coarse.1.e2, f32[4,10,16,128]{3,2,1,0:T(8,128)S(1)} %get-tuple-element.57.G1, f32[4,10,16,128]{3,2,1,0:T(8,128)S(1)} %get-tuple-element.58.S1, f32[5,14,24,128]{3,2,1,0:T(8,128)S(1)} %get-tuple-element.59.G, ...), custom_call_target="tpu_custom_call" | custom-call | tf_op jit(solution)/shard_map/last/pallas_call | solution.py:775
  (12 shorter events, 0.0 us)
Async XLA Ops:
  0.6 13.7 %copy-start.1 = (f32[4,8,16,128]{3,2,1,0:T(8,128)S(1)}, f32[4,8,16,128]{3,2,1,0:T(8,128)}, u32[]{:S(2)}) copy-start(f32[4,8,16,128]{3,2,1,0:T(8,128)} %prev.3) | copy-start | bytes 786436
  3.4 10.9 %copy-start = (f32[4,8,16,128]{3,2,1,0:T(8,128)S(1)}, f32[4,8,16,128]{3,2,1,0:T(8,128)}, u32[]{:S(2)}) copy-start(f32[4,8,16,128]{3,2,1,0:T(8,128)} %old.3) | copy-start | bytes 786436
  3.4 10.9 %copy-start.2 = (f32[8,16,128]{2,1,0:T(8,128)S(1)}, f32[8,16,128]{2,1,0:T(8,128)}, u32[]{:S(2)}) copy-start(f32[8,16,128]{2,1,0:T(8,128)} %c.5) | copy-start | bytes 196612
  3.4 16.4 %all-to-all-start = ((f32[32,3,4,128]{3,2,1,0:T(4,128)}), f32[32,3,4,128]{3,2,1,0:T(4,128)S(1)}, u32[]{:S(2)}, u32[]{:S(2)}) async-start(f32[32,3,4,128]{3,2,1,0:T(4,128)} %get-tuple-element.38), calls=%async_computation | async-start | bytes 393216 | tf_op jit(solution)/shard_map/all_to_all | solution.py:791
  10.8 6.4 %collective-permute-start = (f32[4,3,16,128]{3,2,1,0:T(8,128)S(1)}, f32[4,3,16,128]{3,2,1,0:T(8,128)S(1)}, u32[]{:S(2)}, u32[]{:S(2)}) collective-permute-start(f32[4,3,16,128]{3,2,1,0:T(8,128)S(1)} %get-tuple-element.35), channel_id=1, source_target_pairs={{0,8},{8,16},{16,24},{24,0},{1,9},{9,17},{17,25},{25,1},{2,10},{10... | collective-permute-start | bytes 294920 | tf_op jit(solution)/shard_map/ppermute | solution.py:780
  11.1 6.1 %collective-permute-start.1 = (f32[4,3,16,128]{3,2,1,0:T(8,128)S(1)}, f32[4,3,16,128]{3,2,1,0:T(8,128)S(1)}, u32[]{:S(2)}, u32[]{:S(2)}) collective-permute-start(f32[4,3,16,128]{3,2,1,0:T(8,128)S(1)} %get-tuple-element.36), channel_id=1, source_target_pairs={{0,24},{8,0},{16,8},{24,16},{1,25},{9,1},{17,9},{25,17},{2,26},{10... | collective-permute-start | bytes 294920 | tf_op jit(solution)/shard_map/ppermute | solution.py:780
  12.6 4.6 %collective-permute-start.2 = (f32[4,4,8,128]{3,2,1,0:T(8,128)S(1)}, f32[4,4,8,128]{3,2,1,0:T(8,128)S(1)}, u32[]{:S(2)}, u32[]{:S(2)}) collective-permute-start(f32[4,4,8,128]{3,2,1,0:T(8,128)S(1)} %get-tuple-element.37), channel_id=1, source_target_pairs={{0,4},{4,0},{1,5},{5,1},{2,6},{6,2},{3,7},{7,3},{8,12},{12,8},{9,1... | collective-permute-start | bytes 196616 | tf_op jit(solution)/shard_map/ppermute | solution.py:780
  22.4 10.7 %all-to-all-start.1 = ((f32[32,8,128]{2,1,0:T(8,128)}), f32[32,8,128]{2,1,0:T(8,128)S(1)}, u32[]{:S(2)}, u32[]{:S(2)}) async-start(f32[32,8,128]{2,1,0:T(8,128)} %get-tuple-element.41), calls=%async_computation.1 | async-start | bytes 262144 | tf_op jit(solution)/shard_map/all_to_all | solution.py:791
  25.3 7.6 %collective-permute-start.3 = (f32[2,4,8,128]{3,2,1,0:T(8,128)S(1)}, f32[2,4,8,128]{3,2,1,0:T(8,128)S(1)}, u32[]{:S(2)}, u32[]{:S(2)}) collective-permute-start(f32[2,4,8,128]{3,2,1,0:T(8,128)S(1)} %get-tuple-element.45.p1), channel_id=1, source_target_pairs={{0,8},{8,16},{16,24},{24,0},{1,9},{9,17},{17,25},{25,1},{2,10},{10... | collective-permute-start | bytes 98312 | tf_op jit(solution)/shard_map/ppermute | solution.py:780
  25.6 7.3 %collective-permute-start.4 = (f32[2,4,8,128]{3,2,1,0:T(8,128)S(1)}, f32[2,4,8,128]{3,2,1,0:T(8,128)S(1)}, u32[]{:S(2)}, u32[]{:S(2)}) collective-permute-start(f32[2,4,8,128]{3,2,1,0:T(8,128)S(1)} %get-tuple-element.45.p1), channel_id=1, source_target_pairs={{0,24},{8,0},{16,8},{24,16},{1,25},{9,1},{17,9},{25,17},{2,26},{10... | collective-permute-start | bytes 98312 | tf_op jit(solution)/shard_map/ppermute | solution.py:780
  27.1 5.8 %collective-permute-start.5 = (f32[2,4,8,128]{3,2,1,0:T(8,128)S(1)}, f32[2,4,8,128]{3,2,1,0:T(8,128)S(1)}, u32[]{:S(2)}, u32[]{:S(2)}) collective-permute-start(f32[2,4,8,128]{3,2,1,0:T(8,128)S(1)} %get-tuple-element.45.p1), channel_id=1, source_target_pairs={{0,4},{4,0},{1,5},{5,1},{2,6},{6,2},{3,7},{7,3},{8,12},{12,8},{9,1... | collective-permute-start | bytes 98312 | tf_op jit(solution)/shard_map/ppermute | solution.py:780
  28.9 4.1 %collective-permute-start.6 = (f32[16,128]{1,0:T(8,128)S(1)}, f32[16,128]{1,0:T(8,128)S(1)}, u32[]{:S(2)}, u32[]{:S(2)}) collective-permute-start(f32[16,128]{1,0:T(8,128)S(1)} %get-tuple-element.47), channel_id=1, source_target_pairs={{0,12},{4,8},{8,20},{12,16},{16,28},{20,24},{24,4},{28,0},{1,13},{... | collective-permute-start | bytes 24584 | tf_op jit(solution)/shard_map/ppermute | solution.py:787
  28.9 4.1 %collective-permute-start.7 = (f32[16,128]{1,0:T(8,128)S(1)}, f32[16,128]{1,0:T(8,128)S(1)}, u32[]{:S(2)}, u32[]{:S(2)}) collective-permute-start(f32[16,128]{1,0:T(8,128)S(1)} %get-tuple-element.48), channel_id=1, source_target_pairs={{0,28},{4,24},{8,4},{12,0},{16,12},{20,8},{24,20},{28,16},{1,29},{... | collective-permute-start | bytes 24584 | tf_op jit(solution)/shard_map/ppermute | solution.py:787
  35.0 13.4 %all-to-all-start.2 = ((f32[32,8,128]{2,1,0:T(8,128)}), f32[32,8,128]{2,1,0:T(8,128)S(1)}, u32[]{:S(2)}, u32[]{:S(2)}) async-start(f32[32,8,128]{2,1,0:T(8,128)} %get-tuple-element.49), calls=%async_computation.2 | async-start | bytes 262144 | tf_op jit(solution)/shard_map/all_to_all | solution.py:791

commit v3 on v2

--- a/solution.py
+++ b/solution.py
@@ -24,7 +24,7 @@
 HB = pl.BlockSpec(memory_space=pltpu.HBM)
 EDGE = ((0, 0), (0, 1), (1, 0))
 EDGE1 = EDGE + ((1, 1), (0, 2), (2, 0))
-GRAM_ROW, C_ROW = 3, 4
+TAIL = 4
 
 
 def edge_steps(merge_y):
@@ -97,11 +97,22 @@
         lax.fori_loop(0, count, body, 0)
 
 
+def fill_tail(ref, count, k, value):
+    if count <= 64:
+        for t in range(count):
+            ref[t, k] = value
+    else:
+        def body(t, carry):
+            ref[t, k] = value
+            return carry
+        lax.fori_loop(0, count, body, 0)
+
+
 def first_kernel(counts, merge_y, inc_hbm, c_hbm, *refs):
     if merge_y:
-        g, xlo, xhi, ymsg, slots, inc, c, sems = refs
+        g, xlo, xhi, ymsg, slots, c1, inc, c, QC, sems = refs
     else:
-        g, xlo, xhi, ylo, yhi, slots, inc, c, sems = refs
+        g, xlo, xhi, ylo, yhi, slots, c1, inc, c, QC, sems = refs
     V, X, Y, Z = inc.shape
     place = Place(counts)
     copy_c = pltpu.make_async_copy(c_hbm, c, sems.at[V])
@@ -114,6 +125,45 @@
     layer = (row % 16) // 4
     wanted = jnp.where(row < 16, Z - H, 0) + layer
     copy_c.wait()
+    X1, Y1, half = X // 2, Y // 2, Z // 2
+    for x in range(X1):
+        QC[pl.ds(x * Y, Y)] = c[2 * x] + c[2 * x + 1]
+    li, lo = iota((Z, Z), 0), iota((Z, Z), 1)
+    n = X1 * Y1
+    cc = dot(QC[pl.ds(0, n, stride=2)] + QC[pl.ds(1, n, stride=2)], onehot(lo == li // 2, 0.125))
+    c1[...] = cc.reshape(X1, Y1, Z)
+    c2 = None
+    for y in range(Y // 4):
+        sums = []
+        for x in range(X // 4):
+            k = 2 * x * Y1 + 2 * y
+            pair = cc[k : k + 2] + cc[k + Y1 : k + Y1 + 2]
+            sums.append(pair[0:1] + pair[1:2])
+        rows = jnp.where(sub % 2 == 0, sums[0], sums[1])
+        part = dot(rows, onehot((lo == y * (half // 2) + li // 2) & (li < half), 0.125))
+        c2 = part if c2 is None else c2 + part
+    r8, l8, r4, l4 = iota((8, Z), 0), iota((8, Z), 1), iota((4, Z), 0), iota((4, Z), 1)
+    rim = dot(onehot((l8 == jnp.where(r8 < 2, half - 1 - r8, r8 - 2)) & (r8 < 4)), jnp.concatenate([cc] * (Z // n), 0), NT)
+    base = jnp.where(r4 < 2, c2[0:4], jnp.zeros((4, Z), jnp.float32))
+    fill_tail(slots, counts[0] * counts[1] * counts[2], H, base)
+
+    def tail(line):
+        return jnp.where(r4 == 2, line, base)
+
+    def rim_row(k):
+        first, second = rim[k : k + 1], rim[k + 1 : k + 2]
+        return jnp.where(l4 < n, first, jnp.where(l4 < 2 * n, second, jnp.zeros((4, Z), jnp.float32)))
+
+    up_tail, down_tail = tail(rim_row(0)), tail(rim_row(2))
+    wide8 = l8 < half
+    xlo[V * H, 0:Y1] = jnp.where(wide8, c1[0], roll(c1[1], half, 1))
+    xhi[V * H, 0:Y1] = jnp.where(wide8, c1[X1 - 1], roll(c1[X1 - 2], half, 1))
+    ends = [(ymsg, jnp.where(place.at[1] == 0, 1, 0))] if merge_y else [(ylo, 0), (yhi, 1)]
+    for ref, upper in ends:
+        for x in range(X1):
+            for b in range(2):
+                y = jnp.where(upper == 1, Y1 - 1 - b, b)
+                ref[V * (X // 2), pl.ds(2 * x + b, 1)] = c1[x, pl.ds(y, 1)]
     scale = [1.0 / (6.0 * c[x]) for x in range(X)]
     faces = None
     for v in range(V):
@@ -122,9 +172,9 @@
             value = inc[v, x] * scale[x]
             g[v, x] = value
             if x < H:
-                xlo[v, x] = value
+                xlo[v * H + x] = value
             if x >= X - H:
-                xhi[v, x - (X - H)] = value
+                xhi[v * H + x - (X - H)] = value
         pick = onehot((lane == wanted) & (layer < H) & (row % 4 == v))
         part = dot(pick, g[v].reshape(X * Y, Z), NT)
         faces = part if faces is None else faces + part
@@ -136,6 +186,8 @@
             for k in range(H):
                 slots[above, k] = up[k]
                 slots[below, k] = down[k]
+            slots[above, H] = up_tail
+            slots[below, H] = down_tail
             if dx and dy:
                 t = place.slot((dx, dy, 0))
                 for cell, (a, b) in enumerate(EDGE):
@@ -143,6 +195,7 @@
                     y = Y - 1 - b if dy > 0 else b
                     for v in range(V):
                         slots[t, cell, pl.ds(v, 1)] = g[v, x, pl.ds(y, 1)]
+                slots[t, H] = tail(c1[X1 - 1 if dx > 0 else 0, Y1 - 1 if dy > 0 else 0][None])
 
     def packed(v, j, start, own):
         return jnp.where(own, g[v, 2 * j, pl.ds(start, 8)], roll(g[v, 2 * j + 1, pl.ds(start, 8)], 4, 0))
@@ -153,10 +206,10 @@
                 first = place.at[1] == 0
                 start = pl.multiple_of(jnp.where(first, Y - 8, 0), 8)
                 own = (sub + jnp.where(first, 0, 4)) % 8 >= 4
-                ymsg[v, j] = packed(v, j, start, own)
+                ymsg[v * (X // 2) + j] = packed(v, j, start, own)
             else:
-                yhi[v, j] = packed(v, j, Y - 8, sub >= 4)
-                ylo[v, j] = packed(v, j, 0, sub < 4)
+                yhi[v * (X // 2) + j] = packed(v, j, Y - 8, sub >= 4)
+                ylo[v * (X // 2) + j] = packed(v, j, 0, sub < 4)
 
 
 def spread(cur, below, above, zl, zr):
@@ -199,8 +252,8 @@
     return mask if flag is None else mask * flag
 
 
-def second_kernel(counts, merge_y, g, c, xl, xh, yl, yh, slots, gram, c2p, G, S, p1, slots1, c1, *refs):
-    edges, (Q, QC) = refs[:-2], refs[-2:]
+def second_kernel(counts, merge_y, g, c, c1, xl, xh, yl, yh, slots, gram, G, S, p1, slots1, c2s, *refs):
+    edges, (Q, CE, GL, VL) = refs[:-4], refs[-4:]
     V, X, Y, Z = g.shape
     R = Y + 8
     place = Place(counts)
@@ -213,14 +266,14 @@
     for v in range(V):
         for x in range(X):
             G[v, H + x, 0:Y] = g[v, x]
-            hi, lo = yh[v, x // 2], yl[v, x // 2]
+            hi, lo = yh[v * (X // 2) + x // 2], yl[v * (X // 2) + x // 2]
             if x % 2:
                 hi, lo = roll(hi, 4, 0), roll(lo, 4, 0)
             G[v, H + x, Y:R] = jnp.where(m_hi, hi, jnp.where(m_lo, lo, zero8))
         for i in range(H):
-            G[v, i, 0:Y] = keep(has_xl, xl[v, i])
+            G[v, i, 0:Y] = keep(has_xl, xl[v * H + i])
             G[v, i, Y:R] = zero8
-            G[v, H + X + i, 0:Y] = keep(has_xh, xh[v, i])
+            G[v, H + X + i, 0:Y] = keep(has_xh, xh[v * H + i])
             G[v, H + X + i, Y:R] = zero8
     for dx in (-1, 1):
         for dy in (-1, 1):
@@ -285,13 +338,11 @@
                 part = c[i] * inner[0:Y]
                 total = part if total is None else total + part
             Q[pl.ds((v * (X // 2) + x) * Y, Y)] = total
-        QC[pl.ds(x * Y, Y)] = c[2 * x] + c[2 * x + 1]
     li, lo = iota((Z, Z), 0), iota((Z, Z), 1)
     halve = onehot(lo == li // 2, 0.125)
     n, nc = V * X * Y // 4, X * Y // 4
     b1 = dot(Q[pl.ds(0, n, stride=2)] + Q[pl.ds(1, n, stride=2)], halve)
-    cc = dot(QC[pl.ds(0, nc, stride=2)] + QC[pl.ds(1, nc, stride=2)], halve)
-    c1[...] = cc.reshape(X // 2, Y // 2, Z)
+    cc = c1[...].reshape(nc, Z)
     scale = 1.0 / (1.5 * jnp.where(iota((nc, Z), 1) < Z // 2, cc, jnp.float32(1.0)))
     U = jnp.concatenate([b1[v * nc : (v + 1) * nc] * scale for v in range(V)], axis=0)
     per = nc
@@ -302,16 +353,24 @@
     row, lane16 = iota((16, Z), 0), iota((16, Z), 1)
     wanted = jnp.where(row < 8, half - H, 0) + row % 8
     faces = dot(onehot((lane16 == wanted) & (row % 8 < H)), U, NT)
-    row = iota((8, Z), 0)
-    base = jnp.where(row == GRAM_ROW, gram[0:1], zero8)
-    base = jnp.where(row == C_ROW, c2p[0:1], jnp.where(row == C_ROW + 1, c2p[1:2], base))
-    fill_slots(slots1, counts[0] * counts[1] * counts[2], base, 8)
-    up, down = jnp.where(row < H, faces[0:8], base), jnp.where(row < H, faces[8:16], base)
+    X1, Y1 = X // 2, Y // 2
+    if counts[0] * counts[1] * counts[2] <= 64:
+        for t in range(counts[0] * counts[1] * counts[2]):
+            c2s[t] = slots[t, H]
+    else:
+        c2s[...] = slots[:, H]
+    around_c1(place, CE, c1, xl, xh, yl, yh, slots, V, X)
+    gram_row = gram[0:1]
+    tiles = contributions(place, U, gram_row, CE, GL, VL, Q, V)
+    up, down = faces[0:4], faces[8:12]
+    rest = counts[1] * counts[2]
+    for x in range(counts[0]):
+        for k, tile in enumerate(tiles[x % 2]):
+            fill_tail(slots1.at[pl.ds(x * rest, rest)], rest, k, tile)
     for dx in (-1, 0, 1):
         for dy in (-1, 0, 1):
-            slots1[place.slot((dx, dy, 1))] = up
-            slots1[place.slot((dx, dy, -1))] = down
-    X1, Y1 = X // 2, Y // 2
+            slots1[place.slot((dx, dy, 1)), TAIL] = up
+            slots1[place.slot((dx, dy, -1)), TAIL] = down
     for ref, (dx, dy) in zip(edges, edge_steps(merge_y)):
         for cell, (a, b) in enumerate(EDGE1):
             x = X1 - 1 - a if dx > 0 else a
@@ -323,6 +382,109 @@
                 ref[pl.ds(cell * (V // 2) + vp, 1)] = p1[vp, x, pl.ds(y, 1)]
 
 
+def around_c1(place, CE, c1, xl, xh, yl, yh, slots, V, X):
+    X1, Y1, Z = c1.shape
+    half, n = Z // 2, X1 * Y1
+    sub, lane = iota((8, Z), 0), iota((8, Z), 1)
+    zero = jnp.zeros((8, Z), jnp.float32)
+    body = lane < half
+    for i in range(1, 2 * H + X1 - 1):
+        CE[i, Y1 : 2 * Y1] = zero
+    for x in range(X1):
+        CE[H + x, 0:Y1] = c1[x]
+        for b in range(2):
+            k = 2 * x + b
+            hi, lo = yh[V * (X // 2), pl.ds(k, 1)], yl[V * (X // 2), pl.ds(k, 1)]
+            CE[H + x, pl.ds(Y1 + b, 1)] = keep(place.hi(1), hi)
+            CE[H + x, pl.ds(2 * Y1 - 1 - b, 1)] = keep(place.lo(1), lo)
+    for ref, ok, near, far in ((xl, place.lo(0), H - 1, H - 2), (xh, place.hi(0), H + X1, H + X1 + 1)):
+        tile = keep(ok, ref[V * H, 0:Y1])
+        CE[near, 0:Y1] = jnp.where(body, tile, zero)
+        CE[far, 0:Y1] = jnp.where(body, roll(tile, half, 1), zero)
+    for dx in (-1, 1):
+        for dy in (-1, 1):
+            d = (dx, dy, 0)
+            line = keep(place.has(d), slots[place.slot(d), H, pl.ds(2, 1)])
+            CE[H + X1 if dx > 0 else H - 1, pl.ds(Y1 if dy > 0 else 2 * Y1 - 1, 1)] = line
+    own = lane % Y1 == sub
+    rows = []
+    for dx, dy in ((0, 0), (-1, 0), (1, 0), (0, -1), (0, 1)):
+        pair = []
+        for dz in (-1, 1):
+            d = (dx, dy, dz)
+            line = keep(place.has(d), slots[place.slot(d), H, pl.ds(2, 1)])
+            pair.append(jnp.where(own, line, zero))
+        rows.append(jnp.concatenate(pair, axis=1))
+    rows = jnp.concatenate(rows, axis=0)
+    li, lo = iota((2 * Z, Z), 0), iota((2 * Z, Z), 1)
+    l = li % Z
+    k = l // n
+    target = jnp.where(li < Z, Z - 1 - k, half + k)
+    for x in range(X1):
+        d = dot(rows, onehot((lo == target) & (k < 2) & ((l % n) // Y1 == x)))
+        CE[H + x, 0:Y1] = CE[H + x, 0:Y1] + d[0:8]
+        if x == X1 - 1:
+            CE[H - 1, 0:Y1] = CE[H - 1, 0:Y1] + d[8:16]
+        if x == 0:
+            CE[H + X1, 0:Y1] = CE[H + X1, 0:Y1] + d[16:24]
+        edge = jnp.where(sub == 7, d[24:32], jnp.where(sub == 0, d[32:40], zero))
+        CE[H + x, Y1 : 2 * Y1] = CE[H + x, Y1 : 2 * Y1] + edge
+
+
+def contributions(place, U, gram_row, CE, GL, VL, Q, V):
+    X1, R1, Z = CE.shape[0] - 2 * H, CE.shape[1], CE.shape[2]
+    Y1, half = R1 // 2, Z // 2
+    zero = jnp.zeros((R1, Z), jnp.float32)
+    n = X1 * Y1
+    for v in range(V):
+        for i in range(2 * H + X1):
+            if H <= i < H + X1:
+                k = v * n + (i - H) * Y1
+                GL[v, i, 0:Y1] = U[k : k + Y1]
+                GL[v, i, Y1:R1] = zero[0:Y1]
+            else:
+                GL[v, i] = zero
+        for i in (0, 1, 2 * H + X1 - 2, 2 * H + X1 - 1):
+            VL[v, i] = zero
+    mask = coarse_masks(place, R1, Z)
+    for i in range(H - 1, H + X1 + 1):
+        m = scaled(x_flag(place, i, X1), mask)
+        for v in range(V):
+            get = lambda j: GL[v, j]
+            VL[v, i] = m * (PRE_G * GL[v, i] + PRE_N * level1_sum(get, i))
+    block = {1: 0, 2: 1, 3: 2 * V, 0: 2 * V + 1}
+    for w in range(X1 // 2 + 2):
+        for v in range(V):
+            total = None
+            for i in (H - 2 + 2 * w, H - 1 + 2 * w):
+                get = lambda j: VL[v, j]
+                part = CE[i] * (6.0 * (GL[v, i] - VL[v, i]) + level1_sum(get, i))
+                total = part if total is None else total + part
+            Q[pl.ds((block[w] + 2 * v) * R1, R1)] = total
+    li, lo = iota((Z, 2 * Z), 0), iota((Z, 2 * Z), 1)
+    width = half // 2
+    out = None
+    for j in range(-1, Y1 // 2 + 1):
+        r = (2 * j) % R1
+        rows = Q[pl.ds(r, 4 * V, stride=R1)] + Q[pl.ds(r + 1, 4 * V, stride=R1)]
+        start = Z if j < 0 else Z + width if j == Y1 // 2 else j * width
+        rim = Z + 2 * width + j + 1
+        to = jnp.where(li < half, start + li // 2, jnp.where(li < half + 2, rim + 8, rim))
+        used = (li < half + 2) | (li >= Z - 2)
+        part = dot(rows, onehot((lo == to) & used, 0.25 * 0.125))
+        out = part if out is None else out + part
+    lane4 = iota((4, Z), 1)
+    pairs = []
+    for p in range(V // 2):
+        r, q = 4 * p, 2 * V + 4 * p
+        own, rim = out[r : r + 4, 0:Z], out[r : r + 4, Z:]
+        beside, beside_rim = out[q : q + 4, 0:Z], out[q : q + 4, Z:]
+        edges = jnp.where(lane4 < half, rim, roll(beside_rim, half, 1))
+        ends = jnp.where(lane4 < half, gram_row, jnp.where(lane4 < half + 16, rim, roll(beside_rim, 16, 1)))
+        pairs.append((own, edges, beside, ends))
+    return pairs
+
+
 def coarse_masks(place, R, Z):
     half = Z // 2
     row, lane = iota((R, Z), 0), iota((R, Z), 1)
@@ -339,8 +501,8 @@
     return spread(cur, get(i - 1), get(i + 1), roll(cur, 1, 1), roll(cur, -1, 1))
 
 
-def third_kernel(counts, merge_y, p1, c1, xl, xh, yl, yh, slots, c2p, *refs):
-    edges, (G1, S1, slots2, Q) = refs[:-4], refs[-4:]
+def third_kernel(counts, merge_y, p1, xl, xh, yl, yh, slots, *refs):
+    edges, (G1, S1) = refs[:-2], refs[-2:]
     VP, X, Y, Z = p1.shape
     V, R, half = 2 * VP, 2 * Y, Z // 2
     place = Place(counts)
@@ -350,14 +512,14 @@
     def unpack(tile, v):
         return jnp.where(lane < half, roll(tile, half, 1) if v % 2 else tile, zero)
 
-    r16, l16 = iota((16, Z), 0), iota((16, Z), 1)
-    target = jnp.where(r16 < 8, Z - H, half) + r16 % 8
-    place_lanes = onehot((l16 == target) & (r16 % 8 < H))
+    r8, l8 = iota((8, Z), 0), iota((8, Z), 1)
+    target = jnp.where(r8 < 4, Z - H, half) + r8 % 4
+    place_lanes = onehot((l8 == target) & (r8 % 4 < H))
 
     def layers(dx, dy):
         below, above = (dx, dy, -1), (dx, dy, 1)
-        low = keep(place.has(below), slots[place.slot(below)])
-        high = keep(place.has(above), slots[place.slot(above)])
+        low = keep(place.has(below), slots[place.slot(below), TAIL])
+        high = keep(place.has(above), slots[place.slot(above), TAIL])
         return dot(jnp.concatenate([low, high], axis=0), place_lanes, TN)
 
     mid, up, down = layers(0, 0), layers(0, 1), layers(0, -1)
@@ -406,24 +568,6 @@
         for v in range(V):
             get = lambda j: G1[v, j]
             S1[v, i] = m * (PRE_G * G1[v, i] + PRE_N * level1_sum(get, i))
-    for x in range(X // 2):
-        for v in range(V):
-            total = None
-            for i in (2 * x, 2 * x + 1):
-                get = lambda j: S1[v, j]
-                inner = 6.0 * (G1[v, H + i] - S1[v, H + i]) + level1_sum(get, H + i)
-                part = c1[i] * inner[0:Y]
-                total = part if total is None else total + part
-            Q[pl.ds((v * (X // 2) + x) * Y, Y)] = total
-    li, lo = iota((Z, Z), 0), iota((Z, Z), 1)
-    rows = V * X // 2
-    msg = None
-    for y in range(Y // 2):
-        pair = Q[pl.ds(2 * y, rows, stride=Y)] + Q[pl.ds(2 * y + 1, rows, stride=Y)]
-        part = dot(pair, onehot((lo == y * (half // 2) + li // 2) & (li < half), 0.25 * 0.125))
-        msg = part if msg is None else msg + part
-    msg = msg / (6.0 * 0.0625 * c2p[...])
-    fill_slots(slots2, counts[0] * counts[1] * counts[2], msg, 8)
 
 
 def grid_of(count_y, count_x, fn):
@@ -440,6 +584,56 @@
         for z in range(1, nz):
             acc = jnp.where(lane // width == z, roll(tile[(x * ny + y) * nz + z], width * (z - j), 1), acc)
         return acc
+
+    return grid_of(ny * parts_y, nx, one)
+
+
+def gather_parts(counts, parts_y, slots, lane, odd):
+    nx, ny, nz = counts
+    width = lane.shape[1] // parts_y
+
+    def tile(x, y, z, k):
+        t = (x * ny + y) * nz + z
+        return jnp.concatenate([slots[t, k], slots[t, k]], axis=0)
+
+    def joined(own, beside, x, y, z):
+        zero = jnp.zeros(lane.shape, jnp.float32)
+        before = beside[x - 1, y, z] if x else zero
+        after = beside[x + 1, y, z] if x < nx - 1 else zero
+        return own[x, y, z] + jnp.where(odd, after, before)
+
+    half = lane.shape[1] // 2
+    every = [(x, y, z) for x in range(nx) for y in range(ny) for z in range(nz)]
+    edges, ends = {p: tile(*p, 1) for p in every}, {p: tile(*p, 3) for p in every}
+    own = {p: tile(*p, 0) for p in every}
+    beside = {p: tile(*p, 2) for p in every}
+    own_rim = {p: jnp.where(lane < half, edges[p], ends[p]) for p in every}
+    beside_rim = {p: jnp.where(lane < half, roll(edges[p], half, 1), roll(ends[p], -16, 1)) for p in every}
+    main = {p: joined(own, beside, *p) for p in every}
+    rim = {p: joined(own_rim, beside_rim, *p) for p in every}
+
+    def one(yy, x):
+        y, j = yy // parts_y, yy % parts_y
+        sources = [(main, y, j, j)]
+        if j == 0 and y:
+            sources.append((rim, y - 1, 1, parts_y))
+        if j == parts_y - 1 and y < ny - 1:
+            sources.append((rim, y + 1, 0, -1))
+        total = None
+        for grid, from_y, chunk, inner in sources:
+            acc = roll(grid[x, from_y, 0], -width * chunk, 1)
+            for z in range(1, nz):
+                acc = jnp.where(lane // width == z, roll(grid[x, from_y, z], width * (z - chunk), 1), acc)
+            for z in range(nz):
+                at = 2 * width + inner + 1
+                if z:
+                    to = width * z - 1
+                    acc = acc + jnp.where(lane == to, roll(rim[x, from_y, z], to - at, 1), jnp.zeros_like(acc))
+                if z < nz - 1:
+                    to = width * (z + 1)
+                    acc = acc + jnp.where(lane == to, roll(rim[x, from_y, z], to - at - 8, 1), jnp.zeros_like(acc))
+            total = acc if total is None else total + acc
+        return total
 
     return grid_of(ny * parts_y, nx, one)
 
@@ -467,39 +661,33 @@
     return combine(lambda t: 0.125 * (t + jnp.where(upper, roll(t, step, 1), roll(t, -step, 1))), v)
 
 
-def weights_kernel(counts, parts_y, slots1, *outs):
+def weights_kernel(counts, parts_y, c2s, *outs):
     lane = iota((8, outs[0].shape[-1]), 1)
     odd = iota(lane.shape, 0) % 2 == 1
     count = counts[0] * counts[1] * counts[2]
-    rows = [jnp.where(odd, slots1[t, pl.ds(C_ROW + 1, 1)], slots1[t, pl.ds(C_ROW, 1)]) for t in range(count)]
+    rows = [jnp.where(odd, c2s[t, pl.ds(1, 1)], c2s[t, pl.ds(0, 1)]) for t in range(count)]
     c = assemble(counts, parts_y, rows, lane)
-    level = 2
-    refs = list(outs)
-    while True:
-        ref = refs.pop(0)
+    for level in range(2, LEVELS):
         for y in range(len(c)):
             for x in range(len(c[0])):
-                ref[y, x] = (0.25**level) * c[y][x]
-                if level > 2:
-                    inverse[y, x] = 1.0 / ((6.0 * 0.25**level) * c[y][x])
-        if level == LEVELS - 1:
-            return
-        c = shrink_tiles(c, level, odd, lane)
-        level += 1
-        inverse = refs.pop(0)
-
-
-def coarse_kernel(counts, parts_y, slots2, *refs):
-    *weights, out, W, pre = refs
+                outs[level - 2][y, x] = (0.25**level) * c[y][x]
+        if level < LEVELS - 1:
+            c = shrink_tiles(c, level, odd, lane)
+
+
+def coarse_kernel(counts, parts_y, slots1, *refs):
+    *weights, mine, other, W, pre = refs
     nx, ny, nz = counts
-    Z = slots2.shape[2]
+    Z = slots1.shape[3]
     place = Place(counts)
     width = Z // parts_y
     lane = iota((8, Z), 1)
     odd = iota((8, Z), 0) % 2 == 1
     zero = jnp.zeros((8, Z), jnp.float32)
-    inverse = {3 + i: weights[1 + 2 * i] for i in range(LEVELS - 3)}
-    scale = {2: weights[0], **{3 + i: weights[2 + 2 * i] for i in range(LEVELS - 3)}}
+    scale = {2 + i: ref for i, ref in enumerate(weights)}
+    inverse = {}
+    for level, ref in scale.items():
+        inverse[level] = grid_of(ref.shape[0], ref.shape[1], lambda y, x: 1.0 / (6.0 * ref[y, x]))
 
     def at(v, y, x):
         inside = 0 <= y < len(v) and 0 <= x < len(v[0])
@@ -539,43 +727,47 @@
         c = grid_of(len(g), len(g[0]), lambda y, x: scale[level][y, x])
         r = combine(lambda c, b, a, s: c * (6.0 * (b - a) + s), c, g, v, neighbours(v, level))
         down = shrink_tiles(r, level, odd, lane)
-        down = grid_of(len(down), len(down[0]), lambda y, x: down[y][x] * inverse[level + 1][y, x])
+        down = grid_of(len(down), len(down[0]), lambda y, x: down[y][x] * inverse[level + 1][y][x])
         v = combine(lambda a, b: a + b, v, grow(cycle(down, level + 1), level))
         return sweep(v, g, level)
 
-    count = nx * ny * nz
-    v = cycle(assemble(counts, parts_y, [slots2[t] for t in range(count)], lane), 2)
+    b2 = gather_parts(counts, parts_y, slots1, lane, odd)
+    v = cycle(grid_of(len(b2), nx, lambda y, x: b2[y][x] * inverse[2][y][x]), 2)
     for y in range(len(v)):
         for x in range(nx):
             W[y, x] = v[y][x]
     pre[...] = jnp.zeros_like(pre)
     ix, iy, iz = place.at
-    for xw in range(4):
-        x = ix + (xw + 1) // 2 - 1
-        x_ok = jnp.logical_and(x >= 0, x < nx)
-        x = jnp.clip(x, 0, nx - 1)
-        for j in range(-1, parts_y + 1):
-            y = iy * parts_y + j
-            ok = jnp.logical_and(x_ok, jnp.logical_and(y >= 0, y < ny * parts_y))
-            y = jnp.clip(y, 0, ny * parts_y - 1)
-            for vec in range(4):
-                pre[vec, xw, pl.ds(j % 8, 1)] = keep(ok, W[y, x, pl.ds(vec * 2 + (xw + 1) % 2, 1)])
+    for side, dev in enumerate((ix, ix + 1 - 2 * (ix % 2))):
+        for xw in range(4):
+            x = dev + (xw + 1) // 2 - 1
+            x_ok = jnp.logical_and(x >= 0, x < nx)
+            x = jnp.clip(x, 0, nx - 1)
+            for j in range(-1, parts_y + 1):
+                y = iy * parts_y + j
+                ok = jnp.logical_and(x_ok, jnp.logical_and(y >= 0, y < ny * parts_y))
+                y = jnp.clip(y, 0, ny * parts_y - 1)
+                for vec in range(2):
+                    line = W[y, x, pl.ds(vec * 2 + (xw + 1) % 2, 1)]
+                    pre[2 * side + vec, xw, pl.ds(j % 8, 1)] = keep(ok, line)
     li, lo = iota((Z, Z), 0), iota((Z, Z), 1)
     z1 = jnp.where(lo < 96, lo, lo - Z)
     window = onehot(li == iz * width + jnp.floor_divide(z1 + 2, 2) - 1)
-    moved = dot(pre[...].reshape(4 * 4 * 8, Z), window)
-    out[...] = moved.reshape(4, 4, 8, Z)
-
-
-def last_kernel(counts, e2, G1, S1, G, S, c, pre_hbm, op_hbm, E1, C1, E0, C0, pre, op, sems):
-    V, X1, Y1, Z = e2.shape[0], S1.shape[1] - 2 * H, S1.shape[2] // 2, S1.shape[3]
+    moved = dot(pre[...].reshape(4 * 4 * 8, Z), window).reshape(4, 4, 8, Z)
+    mine[...] = moved[0:2]
+    other[...] = moved[2:4]
+
+
+def last_kernel(counts, mine, other, G1, S1, G, S, c, pre_hbm, op_hbm, E1, C1, E0, C0, pre, op, sems):
+    V, X1, Y1, Z = S1.shape[0], S1.shape[1] - 2 * H, S1.shape[2] // 2, S1.shape[3]
     X, Y = 2 * X1, 2 * Y1
     R1, R = 2 * Y1, Y + 8
     place = Place(counts)
     for v in range(V):
         for x in range(X1):
             k = (v * X1 + x) * R1
-            tile = e2[v, x]
+            held = place.at[0] % 2 == v // 2
+            tile = jnp.where(held, mine[v % 2, x], other[v % 2, x])
             E1[pl.ds(k, 8, stride=2)] = tile
             E1[pl.ds(k + 1, 8, stride=2)] = tile
     for v in range(V):
@@ -646,7 +838,7 @@
         copy.wait()
 
 
-def gram_kernel(old, prev, c, out, c2p):
+def gram_kernel(old, prev, out):
     M, X, Y, Z = old.shape
     J = prev.shape[0]
     pairs = [(a, b) for a in range(M + J) for b in range(a, M + J)]
@@ -662,29 +854,17 @@
     rows = jnp.concatenate([jnp.sum(s, axis=0, keepdims=True) for s in sums], axis=0)
     pad = jnp.zeros((Z - len(pairs), Z), jnp.float32)
     out[...] = dot(ones, jnp.concatenate([rows, pad], axis=0), NT)
-    ny2, nz2 = Y // 4, Z // 4
-    sub, li, lo = iota((8, Z), 0), iota((Z, Z), 0), iota((Z, Z), 1)
-    total = None
-    for y in range(ny2):
-        sums = []
-        for x in range(X // 4):
-            quad = c[4 * x] + c[4 * x + 1] + c[4 * x + 2] + c[4 * x + 3]
-            sums.append(jnp.sum(quad[4 * y : 4 * y + 4], axis=0, keepdims=True))
-        rows = jnp.where(sub % 2 == 0, sums[0], sums[1])
-        part = dot(rows, onehot(lo == y * nz2 + li // 4, 1.0 / 64.0))
-        total = part if total is None else total + part
-    c2p[...] = total
 
 
 def ortho_kernel(count, cells, old, prev, slots, orth, proj, tri):
     M, X, Y, Z = old.shape
     J = prev.shape[0]
     if count <= 64:
-        total = slots[0, pl.ds(GRAM_ROW, 1)]
+        total = slots[0, TAIL - 1, pl.ds(0, 1)]
         for t in range(1, count):
-            total = total + slots[t, pl.ds(GRAM_ROW, 1)]
+            total = total + slots[t, TAIL - 1, pl.ds(0, 1)]
     else:
-        total = lax.fori_loop(0, count, lambda t, s: s + slots[t, pl.ds(GRAM_ROW, 1)], jnp.zeros((1, Z), jnp.float32))
+        total = lax.fori_loop(0, count, lambda t, s: s + slots[t, TAIL - 1, pl.ds(0, 1)], jnp.zeros((1, Z), jnp.float32))
     total = jnp.broadcast_to(total, (8, Z)) / cells
     value = {}
     p = 0
@@ -791,10 +971,45 @@
     return lax.all_to_all(slots, AXES, split_axis=0, concat_axis=0, tiled=True)
 
 
-def wide_coarse(counts, parts_y, slots1, slots2):
+def wide_coarse(counts, parts_y, c2s, slots1):
     nx, ny, nz = counts
-    Z = slots2.shape[2]
+    Z = slots1.shape[3]
     width = Z // parts_y
+    lead, half = 2, Z // 2
+
+    def across_x(own, beside):
+        own, beside = (
+            t.reshape(nx, ny, nz, lead, 2, Z).transpose(3, 4, 0, 1, 2, 5) for t in (own, beside)
+        )
+        pad = ((0, 0), (1, 1), (0, 0), (0, 0), (0, 0))
+        first = own[:, 0] + jnp.pad(beside[:, 0], pad)[:, 0:nx]
+        last = own[:, 1] + jnp.pad(beside[:, 1], pad)[:, 2:]
+        return jnp.stack([first, last], axis=2).reshape(lead, 2 * nx, ny, nz, Z)
+
+    edges, ends = slots1[:, 1], slots1[:, 3]
+    low = iota((1, 1, Z), 2) < half
+    main = across_x(slots1[:, 0], slots1[:, 2])
+    rim = across_x(
+        jnp.where(low, edges, ends), jnp.where(low, jnp.roll(edges, half, 2), jnp.roll(ends, -16, 2))
+    )
+
+    def with_z(line, low, high):
+        pad = ((0, 0), (0, 0), (0, 0), (1, 1))
+        first = jnp.pad(high, pad)[..., 0:nz]
+        last = jnp.pad(low, pad)[..., 2:]
+        lanes = iota((1, width), 1)[0]
+        line = line + jnp.where(lanes == 0, first[..., None], 0.0) + jnp.where(lanes == width - 1, last[..., None], 0.0)
+        return line.reshape(lead, 2 * nx, ny, nz * width)
+
+    lines = []
+    for j in range(-1, parts_y + 1):
+        source, start = (rim, 0) if j < 0 else (rim, width) if j == parts_y else (main, j * width)
+        at = 2 * width + j + 1
+        lines.append(with_z(source[..., start : start + width], rim[..., at], rim[..., at + 8]))
+    pad = ((0, 0), (0, 0), (1, 1), (0, 0))
+    lines[1] = lines[1] + jnp.pad(lines[-1], pad)[:, :, 0:ny]
+    lines[parts_y] = lines[parts_y] + jnp.pad(lines[0], pad)[:, :, 2:]
+    b2 = jnp.stack(lines[1:-1], axis=3).reshape(lead, 2 * nx, ny * parts_y, nz * width)
 
     def whole(t, lead):
         t = t.reshape(nx, ny, nz, lead * 2, Z)
@@ -805,8 +1020,8 @@
         t = jnp.stack(parts, axis=3).reshape(lead, 2, nx, ny * parts_y, nz * width)
         return t.transpose(0, 2, 1, 3, 4).reshape(lead, nx * 2, ny * parts_y, nz * width)
 
-    g2 = whole(slots2, 4)
-    c2 = whole(slots1[:, C_ROW : C_ROW + 2], 1)
+    c2 = whole(c2s[:, 0:2], 1)
+    g2 = b2 / (6.0 * 0.0625 * c2)
 
     def around(v):
         p = jnp.pad(v, ((0, 0), (1, 1), (1, 1), (1, 1)))
@@ -843,15 +1058,18 @@
 
     e = jnp.pad(cycle(g2, c2, 2), ((0, 0), (1, 1), (1, 1), (1, 1)))
     ix, iy, iz = (lax.axis_index(a) for a in AXES)
-    e = lax.dynamic_slice(
-        e, (jnp.int32(0), ix * 2, iy * parts_y, iz * width), (4, 4, parts_y + 2, width + 2)
-    )
-    e = jnp.repeat(e, 2, axis=3)
-    e = jnp.concatenate(
-        [e[..., 2:], jnp.zeros(e.shape[:3] + (Z - 2 * width - 4,), e.dtype), e[..., :2]], axis=3
-    )
-    pad = jnp.zeros((4, 4, 8 - parts_y - 2, Z), e.dtype)
-    return jnp.concatenate([e[:, :, 1:], pad, e[:, :, :1]], axis=2)
+
+    def window(x):
+        w = lax.dynamic_slice(
+            e, (jnp.int32(0), x * 2, iy * parts_y, iz * width), (lead, 4, parts_y + 2, width + 2)
+        )
+        w = jnp.repeat(w, 2, axis=3)
+        gap = jnp.zeros(w.shape[:3] + (Z - 2 * width - 4,), w.dtype)
+        w = jnp.concatenate([w[..., 2:], gap, w[..., :2]], axis=3)
+        pad = jnp.zeros((lead, 4, 8 - parts_y - 2, Z), w.dtype)
+        return jnp.concatenate([w[:, :, 1:], pad, w[:, :, :1]], axis=2)
+
+    return window(ix), window(ix + 1 - 2 * (ix % 2))
 
 
 def per_device(counts, old, prev, inc, c):
@@ -861,27 +1079,37 @@
     near = count <= 64
     R = Y + 8
     X1, Y1 = X // 2, Y // 2
-    y_shape = (V, X // 2, 8, Z)
-    shapes = [(V, X, Y, Z), (V, H, Y, Z), (V, H, Y, Z), y_shape]
+    y_shape, x_shape = (V * (X // 2) + 1, 8, Z), (V * H + 1, Y, Z)
+    shapes = [(V, X, Y, Z), x_shape, x_shape, y_shape]
     shapes += [] if merge_y else [y_shape]
-    shapes += [(count, H, V, Z)]
-    outs = run(near, functools.partial(first_kernel, counts, merge_y), shapes, (inc, c), [inc.shape, c.shape], name="first", plain=(0, 1), result=(len(shapes) - 1,), sems=V + 1)
+    shapes += [(count, H + 1, V, Z), (X1, Y1, Z)]
+    outs = run(
+        near,
+        functools.partial(first_kernel, counts, merge_y),
+        shapes,
+        (inc, c),
+        [inc.shape, c.shape, (X1 * Y, Z)],
+        name="first",
+        result=(len(shapes) - 2,),
+        sems=V + 1,
+    )
     g, xlo, xhi = outs[:3]
-    slots0 = swap(outs[-1])
+    c1 = outs[-1]
+    slots0 = swap(outs[-2])
     xl, xh = shift(xhi, "gx", 1), shift(xlo, "gx", -1)
     if merge_y:
         yl = yh = shift(outs[3], "gy", 1)
     else:
         yl, yh = shift(outs[4], "gy", 1), shift(outs[3], "gy", -1)
-    gram, c2p = run(near, gram_kernel, [(8, Z), (8, Z)], (old, prev, c), name="gram", plain=(0, 1))
+    (gram,) = run(near, gram_kernel, [(8, Z)], (old, prev), name="gram", plain=(0, 1))
     ext0, ext1 = (V + 1, X + 2 * H, R, Z), (V, X1 + 2 * H, 2 * Y1, Z)
     steps = edge_steps(merge_y)
-    G, S, p1, slots1, c1, *edges = run(
+    G, S, p1, slots1, c2s, *edges = run(
         near,
         functools.partial(second_kernel, counts, merge_y),
-        [ext0, ext0, (V // 2, X1, Y1, Z), (count, 8, Z), (X1, Y1, Z)] + [(16, Z)] * len(steps),
-        (g, c, xl, xh, yl, yh, slots0, gram, c2p),
-        [(V * X1 * Y, Z), (X1 * Y, Z)],
+        [ext0, ext0, (V // 2, X1, Y1, Z), (count, TAIL + 1, V, Z), (count, V, Z)] + [(16, Z)] * len(steps),
+        (g, c, c1, xl, xh, yl, yh, slots0, gram),
+        [(V * X1 * Y, Z), ext1[1:], ext1, ext1],
         name="second",
         result=(3,),
     )
@@ -892,16 +1120,14 @@
         yl = yh = shift(p1, "gy", 1)
     else:
         yl, yh = shift(p1, "gy", 1), shift(p1, "gy", -1)
-    G1, S1, slots2 = run(
+    slots1, xl, xh, yl, yh, *edges = lax.optimization_barrier((slots1, xl, xh, yl, yh, *edges))
+    G1, S1 = run(
         near,
         functools.partial(third_kernel, counts, merge_y),
-        [ext1, ext1, (count, 8, Z)],
-        (p1, c1, xl, xh, yl, yh, slots1, c2p, *edges),
-        [(V * X1 // 2 * Y1, Z)],
+        [ext1, ext1],
+        (p1, xl, xh, yl, yh, slots1, *edges),
         name="third",
-        result=(2,),
     )
-    slots2 = swap(slots2)
     orth, proj, tri = run(
         near,
         functools.partial(ortho_kernel, count, float(count * X * Y * Z)),
@@ -916,25 +1142,26 @@
         sizes = [(counts[1] * parts_y, counts[0], 8, Z)]
         for level in range(3, LEVELS):
             y, x = sizes[-1][:2]
-            sizes += [(y // 2, x if level == 3 else x // 2, 8, Z)] * 2
+            sizes.append((y // 2, x if level == 3 else x // 2, 8, Z))
         weights = run(
-            near, functools.partial(weights_kernel, counts, parts_y), sizes, (slots1,), name="weights"
+            near, functools.partial(weights_kernel, counts, parts_y), sizes, (c2s,), name="weights"
         )
-        (e2,) = run(
+        e2, others = run(
             near,
             functools.partial(coarse_kernel, counts, parts_y),
-            [(V, 4, 8, Z)],
-            (slots2, *weights),
+            [(V // 2, 4, 8, Z)] * 2,
+            (slots1, *weights),
             [sizes[0], (V, 4, 8, Z)],
             name="coarse",
         )
     else:
-        e2 = wide_coarse(counts, parts_y, slots1, slots2)
+        e2, others = wide_coarse(counts, parts_y, c2s, slots1)
+    others = lax.ppermute(others, "gx", [(i, i ^ 1) for i in range(counts[0])])
     pre, op = run(
         near,
         functools.partial(last_kernel, counts),
         [(V, X, Y, Z), (V, X, Y, Z)],
-        (e2, G1, S1, G, S, c),
+        (e2, others, G1, S1, G, S, c),
         [(V * X1 * 2 * Y1, Z), ext1, ((V + 1) * (X + 2) * R, Z), ext0, (V, X, Y, Z), (V, X, Y, Z)],
         name="last",
         result=(0, 1),

time: 52.5 us -> 47 us (0.90)
  starting transfers between devices: 25.6 us -> 19 us
  Pallas kernels: 12.9 us -> 13.9 us
    all_to_all x3 -> x2, starting transfers between devices: 15.8 us -> 9.92 us  [swap(): return lax.all_to_all(slots, AXES, split_axis=0, concat_axis=0, tiled=True)]
    pallas_call x8, Pallas kernels: 12.9 us -> 13.9 us  [run(): return fn(*args)]
    ppermute x6, starting transfers between devices: 7.13 us -> 6.21 us  [shift(): return lax.ppermute(value, axis, [(i, (i + step) % n) for i in range(n)])]
    all_to_all x3 -> x2, waiting for transfers between devices: 9.21 us -> 9.37 us  [swap(): return lax.all_to_all(slots, AXES, split_axis=0, concat_axis=0, tiled=True)]
  transfers between devices with their start and end apart: 11 -> 11, of which waited for: 5 -> 5; matrix products, arithmetic and copies ran while one was open for 0% -> 0% of each run, Pallas kernels for 4% -> 5%
where the time goes in v3:
time: 47 us; the launch traced here: 46.7 us
  starting transfers between devices  19 us (40%)
  Pallas kernels  13.9 us (30%)
  waiting for transfers between devices  13.2 us (28%)
  between operations  0.71 us (2%)
    pallas_call x8, Pallas kernels, run(): return fn(*args)  13.9 us
    all_to_all x2, starting transfers between devices, swap(): return lax.all_to_all(slots, AXES, split_axis=0, concat_axis=0, tiled=True)  9.92 us
    all_to_all x2, waiting for transfers between devices, swap(): return lax.all_to_all(slots, AXES, split_axis=0, concat_axis=0, tiled=True)  9.37 us
    ppermute x6, starting transfers between devices, shift(): return lax.ppermute(value, axis, [(i, (i + step) % n) for i in range(n)])  6.21 us
    ppermute x6, waiting for transfers between devices, shift(): return lax.ppermute(value, axis, [(i, (i + step) % n) for i in range(n)])  2.74 us
    ppermute x2, starting transfers between devices, diagonal(): return lax.ppermute(value, ('gx', 'gy'), pairs)  2.64 us
    ppermute x2, waiting for transfers between devices, diagonal(): return lax.ppermute(value, ('gx', 'gy'), pairs)  1.09 us
  transfers between devices with their start and end apart: 11, of which 5 were waited for; matrix products, arithmetic and copies ran while one was open for 0% of the time, Pallas kernels for 5%

profile of v3, /device:TPU:0, one launch (start us, length us, event | category | flops | bytes accessed | tf_op | source)
XLA Modules:
  0.0 46.7 jit_solution(8140886796715079497)
XLA Ops:
  0.6 3.2 %first.1 = (f32[4,8,16,128]{3,2,1,0:T(8,128)S(1)}, f32[13,16,128]{2,1,0:T(8,128)S(1)}, f32[13,16,128]{2,1,0:T(8,128)S(1)}, f32[17,8,128]{2,1,0:T(8,128)S(1)}, f3...) custom-call(f32[4,8,16,128]{3,2,1,0:T(8,128)} %inc_hbm.1, f32[8,16,128]{2,1,0:T(8,128)} %c.3), custom_call_target="tpu_custom_call" | custom-call | tf_op jit(solution)/shard_map/first/pallas_call | solution.py:955
  3.9 0.0 copy-start
  3.9 7.3 %all-to-all-start = ((f32[32,4,4,128]{3,2,1,0:T(4,128)}), f32[32,4,4,128]{3,2,1,0:T(4,128)S(1)}, u32[]{:S(2)}, u32[]{:S(2)}) async-start(f32[32,4,4,128]{3,2,1,0:T(4,128)} %get-tuple-element.43), calls=%async_computation | async-start | bytes 524288 | tf_op jit(solution)/shard_map/all_to_all | solution.py:971
  11.2 0.3 collective-permute-start
  11.5 1.5 %collective-permute-start.1 = (f32[13,16,128]{2,1,0:T(8,128)S(1)}, f32[13,16,128]{2,1,0:T(8,128)S(1)}, u32[]{:S(2)}, u32[]{:S(2)}) collective-permute-start(f32[13,16,128]{2,1,0:T(8,128)S(1)} %get-tuple-element.41), channel_id=1, source_target_pairs={{0,24},{8,0},{16,8},{24,16},{1,25},{9,1},{17,9},{25,17},{2,26},{10... | collective-permute-start | bytes 319496 | tf_op jit(solution)/shard_map/ppermute | solution.py:960
  13.0 1.8 %collective-permute-start.2 = (f32[17,8,128]{2,1,0:T(8,128)S(1)}, f32[17,8,128]{2,1,0:T(8,128)S(1)}, u32[]{:S(2)}, u32[]{:S(2)}) collective-permute-start(f32[17,8,128]{2,1,0:T(8,128)S(1)} %get-tuple-element.42), channel_id=1, source_target_pairs={{0,4},{4,0},{1,5},{5,1},{2,6},{6,2},{3,7},{7,3},{8,12},{12,8},{9,1... | collective-permute-start | bytes 208904 | tf_op jit(solution)/shard_map/ppermute | solution.py:960
  14.8 0.3 gram.1
  15.1 2.7 %collective-permute-done.2.yl.yh = f32[17,8,128]{2,1,0:T(8,128)S(1)} collective-permute-done((f32[17,8,128]{2,1,0:T(8,128)S(1)}, f32[17,8,128]{2,1,0:T(8,128)S(1)}, u32[]{:S(2)}, u32[]{:S(2)}) %collective-permute-start.2) | collective-permute-done | bytes 69664 | tf_op jit(solution)/shard_map/ppermute | solution.py:960
  17.9 4.1 %all-to-all-done.slots = f32[32,4,4,128]{3,2,1,0:T(4,128)S(1)} async-done(((f32[32,4,4,128]{3,2,1,0:T(4,128)}), f32[32,4,4,128]{3,2,1,0:T(4,128)S(1)}, u32[]{:S(2)}, u32[]{:S(2)}) %all-to-all-start) | async-done | bytes 262176 | tf_op jit(solution)/shard_map/all_to_all | solution.py:971
  22.0 4.0 %second.1 = (f32[5,14,24,128]{3,2,1,0:T(8,128)S(1)}, f32[5,14,24,128]{3,2,1,0:T(8,128)S(1)}, f32[2,4,8,128]{3,2,1,0:T(8,128)S(1)}, f32[32,5,4,128]{3,2,1,0:T(4,1...) custom-call(f32[4,8,16,128]{3,2,1,0:T(8,128)S(1)} %get-tuple-element.38.g, ...), custom_call_target="tpu_custom_call" | custom-call | tf_op jit(solution)/shard_map/second/pallas_call | solution.py:955
  26.0 2.6 %all-to-all-start.1 = ((f32[32,5,4,128]{3,2,1,0:T(4,128)}), f32[32,5,4,128]{3,2,1,0:T(4,128)S(1)}, u32[]{:S(2)}, u32[]{:S(2)}) async-start(f32[32,5,4,128]{3,2,1,0:T(4,128)} %get-tuple-element.44), calls=%async_computation.1 | async-start | bytes 655360 | tf_op jit(solution)/shard_map/all_to_all | solution.py:971
  28.6 1.7 %collective-permute-start.5 = (f32[2,4,8,128]{3,2,1,0:T(8,128)S(1)}, f32[2,4,8,128]{3,2,1,0:T(8,128)S(1)}, u32[]{:S(2)}, u32[]{:S(2)}) collective-permute-start(f32[2,4,8,128]{3,2,1,0:T(8,128)S(1)} %get-tuple-element.45.p1), channel_id=1, source_target_pairs={{0,4},{4,0},{1,5},{5,1},{2,6},{6,2},{3,7},{7,3},{8,12},{12,8},{9,1... | collective-permute-start | bytes 98312 | tf_op jit(solution)/shard_map/ppermute | solution.py:960
  30.3 0.9 %collective-permute-start.4 = (f32[2,4,8,128]{3,2,1,0:T(8,128)S(1)}, f32[2,4,8,128]{3,2,1,0:T(8,128)S(1)}, u32[]{:S(2)}, u32[]{:S(2)}) collective-permute-start(f32[2,4,8,128]{3,2,1,0:T(8,128)S(1)} %get-tuple-element.45.p1), channel_id=1, source_target_pairs={{0,24},{8,0},{16,8},{24,16},{1,25},{9,1},{17,9},{25,17},{2,26},{10... | collective-permute-start | bytes 98312 | tf_op jit(solution)/shard_map/ppermute | solution.py:960
  31.2 0.8 %collective-permute-start.6 = (f32[16,128]{1,0:T(8,128)S(1)}, f32[16,128]{1,0:T(8,128)S(1)}, u32[]{:S(2)}, u32[]{:S(2)}) collective-permute-start(f32[16,128]{1,0:T(8,128)S(1)} %get-tuple-element.46), channel_id=1, source_target_pairs={{0,12},{4,8},{8,20},{12,16},{16,28},{20,24},{24,4},{28,0},{1,13},{... | collective-permute-start | bytes 24584 | tf_op jit(solution)/shard_map/ppermute | solution.py:967
  32.1 1.8 %collective-permute-start.7 = (f32[16,128]{1,0:T(8,128)S(1)}, f32[16,128]{1,0:T(8,128)S(1)}, u32[]{:S(2)}, u32[]{:S(2)}) collective-permute-start(f32[16,128]{1,0:T(8,128)S(1)} %get-tuple-element.47), channel_id=1, source_target_pairs={{0,28},{4,24},{8,4},{12,0},{16,12},{20,8},{24,20},{28,16},{1,29},{... | collective-permute-start | bytes 24584 | tf_op jit(solution)/shard_map/ppermute | solution.py:967
  33.9 0.4 weights.1
  34.3 1.0 %collective-permute-done.6.refs_0_ = f32[16,128]{1,0:T(8,128)S(1)} collective-permute-done((f32[16,128]{1,0:T(8,128)S(1)}, f32[16,128]{1,0:T(8,128)S(1)}, u32[]{:S(2)}, u32[]{:S(2)}) %collective-permute-start.6) | collective-permute-done | bytes 8224 | tf_op jit(solution)/shard_map/ppermute | solution.py:967
  35.2 0.1 collective-permute-done.7.refs_1_
  35.4 5.2 %all-to-all-done.1.slots.slots1 = f32[32,5,4,128]{3,2,1,0:T(4,128)S(1)} async-done(((f32[32,5,4,128]{3,2,1,0:T(4,128)}), f32[32,5,4,128]{3,2,1,0:T(4,128)S(1)}, u32[]{:S(2)}, u32[]{:S(2)}) %all-to-all-start.1) | async-done | bytes 327712 | tf_op jit(solution)/shard_map/all_to_all | solution.py:971
  40.6 2.0 %coarse.1 = (f32[2,4,8,128]{3,2,1,0:T(8,128)S(1)}, f32[2,4,8,128]{3,2,1,0:T(8,128)S(1)}) custom-call(f32[32,5,4,128]{3,2,1,0:T(4,128)S(1)} %all-to-all-done.1.slots.slots1, f32[8,4,8,128]{3,2,1,0:T(8,128)S(1)} %get-tuple-element.53.refs_0_, f32[4,4,8,128]{3,2,1,0:T(8,128)S(1)} %get-tuple-element.54.refs_1_, f32[2,2,8,128]{3,2,1,0:T(8,128)S(1)} %get-tuple-element.55.refs_2_, ...), custom_call_target="tpu_custom_call" | custom-call | tf_op jit(solution)/shard_map/coarse/pallas_call | solution.py:955
  42.6 0.2 collective-permute-start.8
  42.8 1.0 %ortho.1 = (f32[4,8,16,128]{3,2,1,0:T(8,128)}, f32[4,4]{1,0:T(4,128)}, f32[4,4]{1,0:T(4,128)}) custom-call(f32[4,8,16,128]{3,2,1,0:T(8,128)S(1)} %copy-done, f32[4,8,16,128]{3,2,1,0:T(8,128)S(1)} %copy-done.1, f32[32,5,4,128]{3,2,1,0:T(4,128)S(1)} %all-to-all-done.1.slots.slots1), custom_call_target="tpu_custom_call" | custom-call | tf_op jit(solution)/shard_map/ortho/pallas_call | solution.py:955
  43.8 0.8 %third.1 = (f32[4,10,16,128]{3,2,1,0:T(8,128)S(1)}, f32[4,10,16,128]{3,2,1,0:T(8,128)S(1)}) custom-call(f32[2,4,8,128]{3,2,1,0:T(8,128)S(1)} %get-tuple-element.45.p1, f32[2,4,8,128]{3,2,1,0:T(8,128)S(1)} %collective-permute-done.3.xl, f32[2,4,8,128]{3,2,1,0:T(8,128)S(1)} %collective-permute-done.4.xh, f32[2,4,8,128]{3,2,1,0:T(8,128)S(1)} %collective-permute-done.5.yl.yh, ...), custom_call_target="tpu_custom_call" | custom-call | tf_op jit(solution)/shard_map/third/pallas_call | solution.py:955
  44.6 2.1 %last.1 = (f32[4,8,16,128]{3,2,1,0:T(8,128)}, f32[4,8,16,128]{3,2,1,0:T(8,128)}) custom-call(f32[2,4,8,128]{3,2,1,0:T(8,128)S(1)} %get-tuple-element.57.mine, f32[2,4,8,128]{3,2,1,0:T(8,128)S(1)} %collective-permute-done.8.other, f32[4,10,16,128]{3,2,1,0:T(8,128)S(1)} %get-tuple-element.65.G1, f32[4,10,16,128]{3,2,1,0:T(8,128)S(1)} %get-tuple-element.66.S1, ...), custom_call_target="tpu_custom_call" | custom-call | tf_op jit(solution)/shard_map/last/pallas_call | solution.py:955
  (12 shorter events, 0.0 us)
Async XLA Ops:
  3.9 10.9 %copy-start = (f32[4,8,16,128]{3,2,1,0:T(8,128)S(1)}, f32[4,8,16,128]{3,2,1,0:T(8,128)}, u32[]{:S(2)}) copy-start(f32[4,8,16,128]{3,2,1,0:T(8,128)} %old.3) | copy-start | bytes 786436
  3.9 10.9 %copy-start.1 = (f32[4,8,16,128]{3,2,1,0:T(8,128)S(1)}, f32[4,8,16,128]{3,2,1,0:T(8,128)}, u32[]{:S(2)}) copy-start(f32[4,8,16,128]{3,2,1,0:T(8,128)} %prev.3) | copy-start | bytes 786436
  3.9 18.1 %all-to-all-start = ((f32[32,4,4,128]{3,2,1,0:T(4,128)}), f32[32,4,4,128]{3,2,1,0:T(4,128)S(1)}, u32[]{:S(2)}, u32[]{:S(2)}) async-start(f32[32,4,4,128]{3,2,1,0:T(4,128)} %get-tuple-element.43), calls=%async_computation | async-start | bytes 524288 | tf_op jit(solution)/shard_map/all_to_all | solution.py:971
  11.2 6.6 %collective-permute-start = (f32[13,16,128]{2,1,0:T(8,128)S(1)}, f32[13,16,128]{2,1,0:T(8,128)S(1)}, u32[]{:S(2)}, u32[]{:S(2)}) collective-permute-start(f32[13,16,128]{2,1,0:T(8,128)S(1)} %get-tuple-element.40), channel_id=1, source_target_pairs={{0,8},{8,16},{16,24},{24,0},{1,9},{9,17},{17,25},{25,1},{2,10},{10... | collective-permute-start | bytes 319496 | tf_op jit(solution)/shard_map/ppermute | solution.py:960
  11.5 6.3 %collective-permute-start.1 = (f32[13,16,128]{2,1,0:T(8,128)S(1)}, f32[13,16,128]{2,1,0:T(8,128)S(1)}, u32[]{:S(2)}, u32[]{:S(2)}) collective-permute-start(f32[13,16,128]{2,1,0:T(8,128)S(1)} %get-tuple-element.41), channel_id=1, source_target_pairs={{0,24},{8,0},{16,8},{24,16},{1,25},{9,1},{17,9},{25,17},{2,26},{10... | collective-permute-start | bytes 319496 | tf_op jit(solution)/shard_map/ppermute | solution.py:960
  13.0 9.0 %copy-start.2 = (f32[8,16,128]{2,1,0:T(8,128)S(1)}, f32[8,16,128]{2,1,0:T(8,128)}, u32[]{:S(2)}) copy-start(f32[8,16,128]{2,1,0:T(8,128)} %c.3) | copy-start | bytes 196612
  13.0 4.8 %collective-permute-start.2 = (f32[17,8,128]{2,1,0:T(8,128)S(1)}, f32[17,8,128]{2,1,0:T(8,128)S(1)}, u32[]{:S(2)}, u32[]{:S(2)}) collective-permute-start(f32[17,8,128]{2,1,0:T(8,128)S(1)} %get-tuple-element.42), channel_id=1, source_target_pairs={{0,4},{4,0},{1,5},{5,1},{2,6},{6,2},{3,7},{7,3},{8,12},{12,8},{9,1... | collective-permute-start | bytes 208904 | tf_op jit(solution)/shard_map/ppermute | solution.py:960
  26.0 14.6 %all-to-all-start.1 = ((f32[32,5,4,128]{3,2,1,0:T(4,128)}), f32[32,5,4,128]{3,2,1,0:T(4,128)S(1)}, u32[]{:S(2)}, u32[]{:S(2)}) async-start(f32[32,5,4,128]{3,2,1,0:T(4,128)} %get-tuple-element.44), calls=%async_computation.1 | async-start | bytes 655360 | tf_op jit(solution)/shard_map/all_to_all | solution.py:971
  28.6 6.8 %collective-permute-start.5 = (f32[2,4,8,128]{3,2,1,0:T(8,128)S(1)}, f32[2,4,8,128]{3,2,1,0:T(8,128)S(1)}, u32[]{:S(2)}, u32[]{:S(2)}) collective-permute-start(f32[2,4,8,128]{3,2,1,0:T(8,128)S(1)} %get-tuple-element.45.p1), channel_id=1, source_target_pairs={{0,4},{4,0},{1,5},{5,1},{2,6},{6,2},{3,7},{7,3},{8,12},{12,8},{9,1... | collective-permute-start | bytes 98312 | tf_op jit(solution)/shard_map/ppermute | solution.py:960
  30.3 5.1 %collective-permute-start.4 = (f32[2,4,8,128]{3,2,1,0:T(8,128)S(1)}, f32[2,4,8,128]{3,2,1,0:T(8,128)S(1)}, u32[]{:S(2)}, u32[]{:S(2)}) collective-permute-start(f32[2,4,8,128]{3,2,1,0:T(8,128)S(1)} %get-tuple-element.45.p1), channel_id=1, source_target_pairs={{0,24},{8,0},{16,8},{24,16},{1,25},{9,1},{17,9},{25,17},{2,26},{10... | collective-permute-start | bytes 98312 | tf_op jit(solution)/shard_map/ppermute | solution.py:960
  31.2 4.1 %collective-permute-start.3 = (f32[2,4,8,128]{3,2,1,0:T(8,128)S(1)}, f32[2,4,8,128]{3,2,1,0:T(8,128)S(1)}, u32[]{:S(2)}, u32[]{:S(2)}) collective-permute-start(f32[2,4,8,128]{3,2,1,0:T(8,128)S(1)} %get-tuple-element.45.p1), channel_id=1, source_target_pairs={{0,8},{8,16},{16,24},{24,0},{1,9},{9,17},{17,25},{25,1},{2,10},{10... | collective-permute-start | bytes 98312 | tf_op jit(solution)/shard_map/ppermute | solution.py:960
  31.2 4.0 %collective-permute-start.6 = (f32[16,128]{1,0:T(8,128)S(1)}, f32[16,128]{1,0:T(8,128)S(1)}, u32[]{:S(2)}, u32[]{:S(2)}) collective-permute-start(f32[16,128]{1,0:T(8,128)S(1)} %get-tuple-element.46), channel_id=1, source_target_pairs={{0,12},{4,8},{8,20},{12,16},{16,28},{20,24},{24,4},{28,0},{1,13},{... | collective-permute-start | bytes 24584 | tf_op jit(solution)/shard_map/ppermute | solution.py:967
  32.1 3.3 %collective-permute-start.7 = (f32[16,128]{1,0:T(8,128)S(1)}, f32[16,128]{1,0:T(8,128)S(1)}, u32[]{:S(2)}, u32[]{:S(2)}) collective-permute-start(f32[16,128]{1,0:T(8,128)S(1)} %get-tuple-element.47), channel_id=1, source_target_pairs={{0,28},{4,24},{8,4},{12,0},{16,12},{20,8},{24,20},{28,16},{1,29},{... | collective-permute-start | bytes 24584 | tf_op jit(solution)/shard_map/ppermute | solution.py:967
  42.6 2.0 %collective-permute-start.8 = (f32[2,4,8,128]{3,2,1,0:T(8,128)S(1)}, f32[2,4,8,128]{3,2,1,0:T(8,128)S(1)}, u32[]{:S(2)}, u32[]{:S(2)}) collective-permute-start(f32[2,4,8,128]{3,2,1,0:T(8,128)S(1)} %get-tuple-element.58), channel_id=1, source_target_pairs={{0,8},{8,0},{16,24},{24,16},{1,9},{9,1},{17,25},{25,17},{2,10},{10... | collective-permute-start | bytes 98312 | tf_op jit(solution)/shard_map/ppermute | solution.py:1159

commit v4 on v3

--- a/solution.py
+++ b/solution.py
@@ -121,9 +121,7 @@
     for copy in copies:
         copy.start()
     sub = iota((8, Z), 0)
-    row, lane = iota((32, Z), 0), iota((32, Z), 1)
-    layer = (row % 16) // 4
-    wanted = jnp.where(row < 16, Z - H, 0) + layer
+    lane = iota((8, Z), 1)
     copy_c.wait()
     X1, Y1, half = X // 2, Y // 2, Z // 2
     for x in range(X1):
@@ -132,30 +130,25 @@
     n = X1 * Y1
     cc = dot(QC[pl.ds(0, n, stride=2)] + QC[pl.ds(1, n, stride=2)], onehot(lo == li // 2, 0.125))
     c1[...] = cc.reshape(X1, Y1, Z)
-    c2 = None
+    stack = []
     for y in range(Y // 4):
         sums = []
         for x in range(X // 4):
             k = 2 * x * Y1 + 2 * y
             pair = cc[k : k + 2] + cc[k + Y1 : k + Y1 + 2]
             sums.append(pair[0:1] + pair[1:2])
-        rows = jnp.where(sub % 2 == 0, sums[0], sums[1])
-        part = dot(rows, onehot((lo == y * (half // 2) + li // 2) & (li < half), 0.125))
-        c2 = part if c2 is None else c2 + part
-    r8, l8, r4, l4 = iota((8, Z), 0), iota((8, Z), 1), iota((4, Z), 0), iota((4, Z), 1)
-    rim = dot(onehot((l8 == jnp.where(r8 < 2, half - 1 - r8, r8 - 2)) & (r8 < 4)), jnp.concatenate([cc] * (Z // n), 0), NT)
-    base = jnp.where(r4 < 2, c2[0:4], jnp.zeros((4, Z), jnp.float32))
-    fill_tail(slots, counts[0] * counts[1] * counts[2], H, base)
-
-    def tail(line):
-        return jnp.where(r4 == 2, line, base)
-
-    def rim_row(k):
-        first, second = rim[k : k + 1], rim[k + 1 : k + 2]
-        return jnp.where(l4 < n, first, jnp.where(l4 < 2 * n, second, jnp.zeros((4, Z), jnp.float32)))
-
-    up_tail, down_tail = tail(rim_row(0)), tail(rim_row(2))
-    wide8 = l8 < half
+        stack.append(jnp.where(sub % 2 == 0, sums[0], sums[1]))
+    stack = dot(jnp.concatenate(stack, axis=0), onehot((lo == li // 2) & (li < half), 0.125))
+    c2 = stack[0:8]
+    for y in range(1, Y // 4):
+        c2 = c2 + roll(stack[8 * y : 8 * y + 8], y * (half // 2), 1)
+    r4, l4 = iota((4, Z), 0), iota((4, Z), 1)
+    zero4 = jnp.zeros((4, Z), jnp.float32)
+    base = [jnp.where(r4 == H, c2[x : x + 1], zero4) for x in range(2)] + [zero4] * (V - 2)
+    for v in range(2):
+        fill_tail(slots, counts[0] * counts[1] * counts[2], v, base[v])
+
+    wide8 = lane < half
     xlo[V * H, 0:Y1] = jnp.where(wide8, c1[0], roll(c1[1], half, 1))
     xhi[V * H, 0:Y1] = jnp.where(wide8, c1[X1 - 1], roll(c1[X1 - 2], half, 1))
     ends = [(ymsg, jnp.where(place.at[1] == 0, 1, 0))] if merge_y else [(ylo, 0), (yhi, 1)]
@@ -165,7 +158,6 @@
                 y = jnp.where(upper == 1, Y1 - 1 - b, b)
                 ref[V * (X // 2), pl.ds(2 * x + b, 1)] = c1[x, pl.ds(y, 1)]
     scale = [1.0 / (6.0 * c[x]) for x in range(X)]
-    faces = None
     for v in range(V):
         copies[v].wait()
         for x in range(X):
@@ -175,27 +167,40 @@
                 xlo[v * H + x] = value
             if x >= X - H:
                 xhi[v * H + x - (X - H)] = value
-        pick = onehot((lane == wanted) & (layer < H) & (row % 4 == v))
-        part = dot(pick, g[v].reshape(X * Y, Z), NT)
-        faces = part if faces is None else faces + part
-    up = [faces[4 * k : 4 * k + 4] for k in range(H)]
-    down = [faces[16 + 4 * k : 20 + 4 * k] for k in range(H)]
+    faces = []
+    for x in range(X):
+        for y in range(0, Y, 8):
+            acc = jnp.zeros((8, Z), jnp.float32)
+            for v in range(V):
+                acc = jnp.where(lane // 8 == v, roll(g[v, x, y : y + 8], 8 * v + H, 1), acc)
+            m = len(faces)
+            if m < X1:
+                acc = jnp.where(lane // 2 == 4 * V, roll(c1[m], 8 * V - half + 2, 1), acc)
+                acc = jnp.where(lane // 2 == 4 * V + 1, roll(c1[m], 8 * V + 2, 1), acc)
+            faces.append(acc)
+    faces = jnp.concatenate(faces, axis=0).T
+    k = 8 * V
+    c_up = jnp.where(l4 < n, faces[k + 1 : k + 2], roll(faces[k : k + 8], n, 1)[0:1])
+    c_down = jnp.where(l4 < n, faces[k + 2 : k + 3], roll(faces[k : k + 8], n, 1)[3:4])
+    rows_up = [jnp.where(r4 < H, faces[8 * v : 8 * v + 4], base[v]) for v in range(V)]
+    rows_down = [jnp.where(r4 < H, faces[8 * v + H : 8 * v + H + 4], base[v]) for v in range(V)]
+    rows_up[2] = jnp.where(r4 < H, rows_up[2], jnp.where(l4 < 2 * n, c_up, zero4))
+    rows_down[2] = jnp.where(r4 < H, rows_down[2], jnp.where(l4 < 2 * n, c_down, zero4))
     for dx in (-1, 0, 1):
         for dy in (-1, 0, 1):
             above, below = place.slot((dx, dy, 1)), place.slot((dx, dy, -1))
-            for k in range(H):
-                slots[above, k] = up[k]
-                slots[below, k] = down[k]
-            slots[above, H] = up_tail
-            slots[below, H] = down_tail
+            for v in range(V):
+                slots[above, v] = rows_up[v]
+                slots[below, v] = rows_down[v]
             if dx and dy:
                 t = place.slot((dx, dy, 0))
                 for cell, (a, b) in enumerate(EDGE):
                     x = X - 1 - a if dx > 0 else a
                     y = Y - 1 - b if dy > 0 else b
                     for v in range(V):
-                        slots[t, cell, pl.ds(v, 1)] = g[v, x, pl.ds(y, 1)]
-                slots[t, H] = tail(c1[X1 - 1 if dx > 0 else 0, Y1 - 1 if dy > 0 else 0][None])
+                        slots[t, v, pl.ds(cell, 1)] = g[v, x, pl.ds(y, 1)]
+                corner = c1[X1 - 1 if dx > 0 else 0, pl.ds(Y1 - 1 if dy > 0 else 0, 1)]
+                slots[t, 2, pl.ds(H, 1)] = corner
 
     def packed(v, j, start, own):
         return jnp.where(own, g[v, 2 * j, pl.ds(start, 8)], roll(g[v, 2 * j + 1, pl.ds(start, 8)], 4, 0))
@@ -223,7 +228,7 @@
         rim = ref[V, i]
         last = lane.shape[1] - 1
         zl = jnp.where(lane == 0, roll(rim, -(16 * v + 2), 1), zl)
-        zr = jnp.where(lane == last, roll(rim, last - (16 * v + 10), 1), zr)
+        zr = jnp.where(lane == last, roll(rim, last - (16 * v + 8), 1), zr)
     return spread(cur, ref[v, i - 1], ref[v, i + 1], zl, zr)
 
 
@@ -233,9 +238,7 @@
     ym = onehot(row < Y) + onehot((row >= Y) & (row < Y + H)) * f32(place.hi(1))
     ym = ym + onehot(row >= R - H) * f32(place.lo(1))
     lane = iota((R, Z), 1)
-    k = lane % 8
-    outside_lo = ((lane // 8) % 2 == 0) & (k < H)
-    outside_hi = ((lane // 8) % 2 == 1) & (k >= 2)
+    outside_lo, outside_hi = lane % 16 < H, lane % 16 >= 8
     zm = jnp.where(outside_lo, f32(place.lo(2)), jnp.where(outside_hi, f32(place.hi(2)), jnp.float32(1.0)))
     return ym, ym * zm
 
@@ -282,47 +285,50 @@
                 i = H + X + a if dx > 0 else H - 1 - a
                 r = Y + b if dy > 0 else R - 1 - b
                 for v in range(V):
-                    G[v, i, pl.ds(r, 1)] = keep(ok, slots[t, cell, pl.ds(v, 1)])
-    row, lane24 = iota((8 * H, Z), 0), iota((8 * H, Z), 1)
-    target = jnp.where(row < 4 * H, 0, 10 - H) + 16 * (row % 4) + row // 4
-    place_lanes = onehot(lane24 == target)
-
-    def layers(dx, dy, lanes):
-        below, above = (dx, dy, -1), (dx, dy, 1)
-        low, high = place.slot(below), place.slot(above)
-        rows = [keep(place.has(below), slots[low, k]) for k in range(H)]
-        rows += [keep(place.has(above), slots[high, k]) for k in range(H)]
-        return dot(jnp.concatenate(rows, axis=0)[:, lanes], place_lanes, TN)
-
-    everything = slice(0, X * Y)
+                    G[v, i, pl.ds(r, 1)] = keep(ok, slots[t, v, pl.ds(cell, 1)])
+    r4 = iota((4, Z), 0)
+    zero4 = jnp.zeros((4, Z), jnp.float32)
+
+    def layers(dx, dy):
+        tiles = []
+        for v in range(V):
+            for dz in (-1, 1):
+                d = (dx, dy, dz)
+                use = jnp.logical_and(r4 < H, place.has(d))
+                tiles += [jnp.where(use, slots[place.slot(d), v], zero4), zero4]
+        return jnp.concatenate(tiles, axis=0)
+
+    wide = iota((16 * V, Z), 1)
+    mid = layers(0, 0)
+    sides = jnp.where(wide % Y < 8, layers(0, 1), layers(0, -1))
+    first = jnp.concatenate([mid, sides], axis=0).T
+    edges_x = jnp.where(wide < 2 * Y, layers(1, 0), layers(-1, 0))
+    for d, start, to in (((1, 1), 0, 2), ((1, -1), 0, 3), ((-1, 1), X - 1, 4), ((-1, -1), X - 1, 5)):
+        edges_x = jnp.where(wide // Y == to, roll(layers(*d), (to - start) * Y, 1), edges_x)
+    second = jnp.concatenate([edges_x, jnp.zeros((Z - 16 * V, Z), jnp.float32)], axis=0).T
+    lane_y, lane_8 = iota((Y, Z), 1) < 16 * V, iota((8, Z), 1) < 16 * V
     for i in (0, H + X + H - 1):
         G[V, i] = jnp.zeros((R, Z), jnp.float32)
-    mid = layers(0, 0, everything)
-    up = layers(0, 1, everything)
-    down = layers(0, -1, everything)
     for x in range(X):
-        G[V, H + x, 0:Y] = mid[x * Y : (x + 1) * Y]
-        tile = jnp.where(sub < 2, up[x * Y : x * Y + 8], zero8)
-        G[V, H + x, Y:R] = jnp.where(sub >= 6, down[(x + 1) * Y - 8 : (x + 1) * Y], tile)
-    for dx in (-1, 1):
-        first = slice(0, 2 * Y) if dx > 0 else slice((X - 2) * Y, X * Y)
-        side = layers(dx, 0, first)
-        base = H + X if dx > 0 else H - 2
+        tile = first[x * Y : (x + 1) * Y]
+        G[V, H + x, 0:Y] = jnp.where(lane_y, tile, zero_y)
+        other = roll(tile, Z - 16 * V, 1)
+        edge = jnp.where(sub < 2, other[0:8], jnp.where(sub >= 6, other[Y - 8 : Y], zero8))
+        G[V, H + x, Y:R] = jnp.where(lane_8, edge, zero8)
+    for base, at in ((H + X, 0), (H - 2, X - 2)):
         for a in range(2):
-            G[V, base + a, 0:Y] = side[a * Y : (a + 1) * Y]
+            G[V, base + a, 0:Y] = second[(at + a) * Y : (at + a + 1) * Y]
             G[V, base + a, Y:R] = zero8
-        near = slice(0, Y) if dx > 0 else slice((X - 1) * Y, X * Y)
-        up = layers(dx, 1, near)
-        down = layers(dx, -1, near)
-        tile = jnp.where(sub < 2, up[0:8], zero8)
-        G[V, H + X if dx > 0 else H - 1, Y:R] = jnp.where(sub >= 6, down[Y - 8 : Y], tile)
+    for i, a in ((H + X, 2), (H - 1, 4)):
+        up, down = second[a * Y : a * Y + 8], second[(a + 2) * Y - 8 : (a + 2) * Y]
+        G[V, i, Y:R] = jnp.where(sub < 2, up, jnp.where(sub >= 6, down, zero8))
     lane = iota((R, Z), 1)
     for i in range(1, 2 * H + X - 1):
         rim = G[V, i]
         for v in range(V):
             body = G[v, i]
             rim = jnp.where((lane == 16 * v + 3) | (lane == 16 * v + 4), roll(body, 16 * v + 3, 1), rim)
-            rim = jnp.where((lane == 16 * v + 8) | (lane == 16 * v + 9), roll(body, 16 * v + 10, 1), rim)
+            rim = jnp.where((lane == 16 * v + 6) | (lane == 16 * v + 7), roll(body, 16 * v + 8, 1), rim)
         G[V, i] = rim
     ym, zm = fine_masks(place, Y, Z)
     for i in range(1, 2 * H + X - 1):
@@ -350,15 +356,19 @@
         both = U[2 * vp * per : (2 * vp + 1) * per] + roll(U[(2 * vp + 1) * per : (2 * vp + 2) * per], Z // 2, 1)
         p1[vp] = both.reshape(X // 2, Y // 2, Z)
     half = Z // 2
-    row, lane16 = iota((16, Z), 0), iota((16, Z), 1)
-    wanted = jnp.where(row < 8, half - H, 0) + row % 8
-    faces = dot(onehot((lane16 == wanted) & (row % 8 < H)), U, NT)
+    ends = jnp.where(iota(U.shape, 1) < 8, roll(U, H - half, 1), roll(U, 8, 1)).T
+    faces = ends[0:16]
     X1, Y1 = X // 2, Y // 2
     if counts[0] * counts[1] * counts[2] <= 64:
         for t in range(counts[0] * counts[1] * counts[2]):
-            c2s[t] = slots[t, H]
+            for x in range(2):
+                c2s[t, pl.ds(x, 1)] = slots[t, x, pl.ds(H, 1)]
     else:
-        c2s[...] = slots[:, H]
+        def move(t, carry):
+            for x in range(2):
+                c2s[t, pl.ds(x, 1)] = slots[t, x, pl.ds(H, 1)]
+            return carry
+        lax.fori_loop(0, c2s.shape[0], move, 0)
     around_c1(place, CE, c1, xl, xh, yl, yh, slots, V, X)
     gram_row = gram[0:1]
     tiles = contributions(place, U, gram_row, CE, GL, VL, Q, V)
@@ -404,30 +414,29 @@
     for dx in (-1, 1):
         for dy in (-1, 1):
             d = (dx, dy, 0)
-            line = keep(place.has(d), slots[place.slot(d), H, pl.ds(2, 1)])
+            line = keep(place.has(d), slots[place.slot(d), 2, pl.ds(H, 1)])
             CE[H + X1 if dx > 0 else H - 1, pl.ds(Y1 if dy > 0 else 2 * Y1 - 1, 1)] = line
-    own = lane % Y1 == sub
     rows = []
-    for dx, dy in ((0, 0), (-1, 0), (1, 0), (0, -1), (0, 1)):
+    steps = ((0, 0), (-1, 0), (1, 0), (0, -1), (0, 1))
+    wanted = [range(X1), (X1 - 1,), (0,), range(X1), range(X1)]
+    for (dx, dy), xs in zip(steps, wanted):
         pair = []
         for dz in (-1, 1):
             d = (dx, dy, dz)
-            line = keep(place.has(d), slots[place.slot(d), H, pl.ds(2, 1)])
-            pair.append(jnp.where(own, line, zero))
-        rows.append(jnp.concatenate(pair, axis=1))
-    rows = jnp.concatenate(rows, axis=0)
+            pair.append(keep(place.has(d), slots[place.slot(d), 2, pl.ds(H, 1)]))
+        for x in xs:
+            own = lane % n == x * Y1 + sub
+            rows.append(jnp.concatenate([jnp.where(own, line, zero) for line in pair], axis=1))
     li, lo = iota((2 * Z, Z), 0), iota((2 * Z, Z), 1)
     l = li % Z
-    k = l // n
-    target = jnp.where(li < Z, Z - 1 - k, half + k)
+    target = jnp.where(li < Z, Z - 1 - l // n, half + l // n)
+    d = dot(jnp.concatenate(rows, axis=0), onehot((lo == target) & (l < 2 * n)))
+    d = [d[8 * m : 8 * m + 8] for m in range(len(rows))]
+    CE[H - 1, 0:Y1] = CE[H - 1, 0:Y1] + d[X1]
+    CE[H + X1, 0:Y1] = CE[H + X1, 0:Y1] + d[X1 + 1]
     for x in range(X1):
-        d = dot(rows, onehot((lo == target) & (k < 2) & ((l % n) // Y1 == x)))
-        CE[H + x, 0:Y1] = CE[H + x, 0:Y1] + d[0:8]
-        if x == X1 - 1:
-            CE[H - 1, 0:Y1] = CE[H - 1, 0:Y1] + d[8:16]
-        if x == 0:
-            CE[H + X1, 0:Y1] = CE[H + X1, 0:Y1] + d[16:24]
-        edge = jnp.where(sub == 7, d[24:32], jnp.where(sub == 0, d[32:40], zero))
+        CE[H + x, 0:Y1] = CE[H + x, 0:Y1] + d[x]
+        edge = jnp.where(sub == 7, d[X1 + 2 + x], jnp.where(sub == 0, d[2 * X1 + 2 + x], zero))
         CE[H + x, Y1 : 2 * Y1] = CE[H + x, Y1 : 2 * Y1] + edge
 
 
@@ -461,24 +470,33 @@
                 part = CE[i] * (6.0 * (GL[v, i] - VL[v, i]) + level1_sum(get, i))
                 total = part if total is None else total + part
             Q[pl.ds((block[w] + 2 * v) * R1, R1)] = total
-    li, lo = iota((Z, 2 * Z), 0), iota((Z, 2 * Z), 1)
-    width = half // 2
-    out = None
+    li, lo = iota((Z, Z), 0), iota((Z, Z), 1)
+    width, m = half // 2, 4 * V
+    stack = []
     for j in range(-1, Y1 // 2 + 1):
         r = (2 * j) % R1
-        rows = Q[pl.ds(r, 4 * V, stride=R1)] + Q[pl.ds(r + 1, 4 * V, stride=R1)]
-        start = Z if j < 0 else Z + width if j == Y1 // 2 else j * width
-        rim = Z + 2 * width + j + 1
-        to = jnp.where(li < half, start + li // 2, jnp.where(li < half + 2, rim + 8, rim))
-        used = (li < half + 2) | (li >= Z - 2)
-        part = dot(rows, onehot((lo == to) & used, 0.25 * 0.125))
-        out = part if out is None else out + part
+        stack.append(Q[pl.ds(r, m, stride=R1)] + Q[pl.ds(r + 1, m, stride=R1)])
+    to = jnp.where(li < half, li // 2, jnp.where(li < half + 2, width + 1, width))
+    used = (li < half + 2) | (li >= Z - 2)
+    small = dot(jnp.concatenate(stack, axis=0), onehot((lo == to) & used, 0.25 * 0.125))
+    lane_m = iota((m, Z), 1)
+    body, rims = jnp.zeros((m, Z), jnp.float32), jnp.zeros((m, Z), jnp.float32)
+    for j in range(-1, Y1 // 2 + 1):
+        piece = small[(j + 1) * m : (j + 2) * m]
+        if 0 <= j < Y1 // 2:
+            body = jnp.where(lane_m // width == j, roll(piece, j * width, 1), body)
+        else:
+            chunk = 0 if j < 0 else 1
+            rims = jnp.where(lane_m // width == chunk, roll(piece, chunk * width, 1), rims)
+        at = 2 * width + j + 1
+        rims = jnp.where(lane_m == at, roll(piece, at - width, 1), rims)
+        rims = jnp.where(lane_m == at + 8, roll(piece, at + 7 - width, 1), rims)
     lane4 = iota((4, Z), 1)
     pairs = []
     for p in range(V // 2):
         r, q = 4 * p, 2 * V + 4 * p
-        own, rim = out[r : r + 4, 0:Z], out[r : r + 4, Z:]
-        beside, beside_rim = out[q : q + 4, 0:Z], out[q : q + 4, Z:]
+        own, rim = body[r : r + 4], rims[r : r + 4]
+        beside, beside_rim = body[q : q + 4], rims[q : q + 4]
         edges = jnp.where(lane4 < half, rim, roll(beside_rim, half, 1))
         ends = jnp.where(lane4 < half, gram_row, jnp.where(lane4 < half + 16, rim, roll(beside_rim, 16, 1)))
         pairs.append((own, edges, beside, ends))
@@ -786,9 +804,8 @@
     li, lo = iota((Z, Z), 0), iota((Z, Z), 1)
     double = onehot(li == lo // 2)
     half = Z // 2
-    k = lo % 8
-    low_side = (lo // 8) % 2 == 0
-    source = jnp.where(low_side, jnp.where(k < H, Z - 1, 0), jnp.where(k < 2, half - 1, half))
+    k = lo % 16
+    source = jnp.where(k < H, Z - 1, jnp.where(k < 6, 0, jnp.where(k < 8, half - 1, half)))
     rim = None
     for v in range(V):
         part = dot(fine[v], onehot((li == source) & (lo // 16 == v)))
@@ -1082,7 +1099,7 @@
     y_shape, x_shape = (V * (X // 2) + 1, 8, Z), (V * H + 1, Y, Z)
     shapes = [(V, X, Y, Z), x_shape, x_shape, y_shape]
     shapes += [] if merge_y else [y_shape]
-    shapes += [(count, H + 1, V, Z), (X1, Y1, Z)]
+    shapes += [(count, V, H + 1, Z), (X1, Y1, Z)]
     outs = run(
         near,
         functools.partial(first_kernel, counts, merge_y),

time: 47 us -> 45.4 us (0.966)
  Pallas kernels: 13.9 us -> 12.2 us
    pallas_call x8, Pallas kernels: 13.9 us -> 12.2 us  [run(): return fn(*args)]
  transfers between devices with their start and end apart: 11 -> 11, of which waited for: 5 -> 5; matrix products, arithmetic and copies ran while one was open for 0% -> 0% of each run, Pallas kernels for 5% -> 6%
where the time goes in v4:
time: 45.4 us; the launch traced here: 45.1 us
  starting transfers between devices  19 us (42%)
  waiting for transfers between devices  13.2 us (29%)
  Pallas kernels  12.2 us (27%)
  between operations  0.71 us (2%)
    pallas_call x8, Pallas kernels, run(): return fn(*args)  12.2 us
    all_to_all x2, starting transfers between devices, swap(): return lax.all_to_all(slots, AXES, split_axis=0, concat_axis=0, tiled=True)  9.92 us
    all_to_all x2, waiting for transfers between devices, swap(): return lax.all_to_all(slots, AXES, split_axis=0, concat_axis=0, tiled=True)  9.37 us
    ppermute x6, starting transfers between devices, shift(): return lax.ppermute(value, axis, [(i, (i + step) % n) for i in range(n)])  6.21 us
    ppermute x6, waiting for transfers between devices, shift(): return lax.ppermute(value, axis, [(i, (i + step) % n) for i in range(n)])  2.74 us
    ppermute x2, starting transfers between devices, diagonal(): return lax.ppermute(value, ('gx', 'gy'), pairs)  2.64 us
    ppermute x2, waiting for transfers between devices, diagonal(): return lax.ppermute(value, ('gx', 'gy'), pairs)  1.09 us
  transfers between devices with their start and end apart: 11, of which 5 were waited for; matrix products, arithmetic and copies ran while one was open for 0% of the time, Pallas kernels for 6%

profile of v4, /device:TPU:0, one launch (start us, length us, event | category | flops | bytes accessed | tf_op | source)
XLA Modules:
  0.0 45.1 jit_solution(17258505132412487633)
XLA Ops:
  0.6 2.4 %first.1 = (f32[4,8,16,128]{3,2,1,0:T(8,128)S(1)}, f32[13,16,128]{2,1,0:T(8,128)S(1)}, f32[13,16,128]{2,1,0:T(8,128)S(1)}, f32[17,8,128]{2,1,0:T(8,128)S(1)}, f3...) custom-call(f32[4,8,16,128]{3,2,1,0:T(8,128)} %inc_hbm.1, f32[8,16,128]{2,1,0:T(8,128)} %c.3), custom_call_target="tpu_custom_call" | custom-call | tf_op jit(solution)/shard_map/first/pallas_call | solution.py:972
  3.1 0.0 copy-start.1
  3.1 7.3 %all-to-all-start = ((f32[32,4,4,128]{3,2,1,0:T(4,128)}), f32[32,4,4,128]{3,2,1,0:T(4,128)S(1)}, u32[]{:S(2)}, u32[]{:S(2)}) async-start(f32[32,4,4,128]{3,2,1,0:T(4,128)} %get-tuple-element.43), calls=%async_computation | async-start | bytes 524288 | tf_op jit(solution)/shard_map/all_to_all | solution.py:988
  10.4 0.3 collective-permute-start
  10.7 1.5 %collective-permute-start.1 = (f32[13,16,128]{2,1,0:T(8,128)S(1)}, f32[13,16,128]{2,1,0:T(8,128)S(1)}, u32[]{:S(2)}, u32[]{:S(2)}) collective-permute-start(f32[13,16,128]{2,1,0:T(8,128)S(1)} %get-tuple-element.41), channel_id=1, source_target_pairs={{0,24},{8,0},{16,8},{24,16},{1,25},{9,1},{17,9},{25,17},{2,26},{10... | collective-permute-start | bytes 319496 | tf_op jit(solution)/shard_map/ppermute | solution.py:977
  12.2 1.8 %collective-permute-start.2 = (f32[17,8,128]{2,1,0:T(8,128)S(1)}, f32[17,8,128]{2,1,0:T(8,128)S(1)}, u32[]{:S(2)}, u32[]{:S(2)}) collective-permute-start(f32[17,8,128]{2,1,0:T(8,128)S(1)} %get-tuple-element.42), channel_id=1, source_target_pairs={{0,4},{4,0},{1,5},{5,1},{2,6},{6,2},{3,7},{7,3},{8,12},{12,8},{9,1... | collective-permute-start | bytes 208904 | tf_op jit(solution)/shard_map/ppermute | solution.py:977
  14.0 0.3 gram.1
  14.3 2.7 %collective-permute-done.2.yl.yh = f32[17,8,128]{2,1,0:T(8,128)S(1)} collective-permute-done((f32[17,8,128]{2,1,0:T(8,128)S(1)}, f32[17,8,128]{2,1,0:T(8,128)S(1)}, u32[]{:S(2)}, u32[]{:S(2)}) %collective-permute-start.2) | collective-permute-done | bytes 69664 | tf_op jit(solution)/shard_map/ppermute | solution.py:977
  17.0 4.1 %all-to-all-done.slots = f32[32,4,4,128]{3,2,1,0:T(4,128)S(1)} async-done(((f32[32,4,4,128]{3,2,1,0:T(4,128)}), f32[32,4,4,128]{3,2,1,0:T(4,128)S(1)}, u32[]{:S(2)}, u32[]{:S(2)}) %all-to-all-start) | async-done | bytes 262176 | tf_op jit(solution)/shard_map/all_to_all | solution.py:988
  21.2 3.2 %second.1 = (f32[5,14,24,128]{3,2,1,0:T(8,128)S(1)}, f32[5,14,24,128]{3,2,1,0:T(8,128)S(1)}, f32[2,4,8,128]{3,2,1,0:T(8,128)S(1)}, f32[32,5,4,128]{3,2,1,0:T(4,1...) custom-call(f32[4,8,16,128]{3,2,1,0:T(8,128)S(1)} %get-tuple-element.38.g, ...), custom_call_target="tpu_custom_call" | custom-call | tf_op jit(solution)/shard_map/second/pallas_call | solution.py:972
  24.3 2.6 %all-to-all-start.1 = ((f32[32,5,4,128]{3,2,1,0:T(4,128)}), f32[32,5,4,128]{3,2,1,0:T(4,128)S(1)}, u32[]{:S(2)}, u32[]{:S(2)}) async-start(f32[32,5,4,128]{3,2,1,0:T(4,128)} %get-tuple-element.44), calls=%async_computation.1 | async-start | bytes 655360 | tf_op jit(solution)/shard_map/all_to_all | solution.py:988
  26.9 1.7 %collective-permute-start.5 = (f32[2,4,8,128]{3,2,1,0:T(8,128)S(1)}, f32[2,4,8,128]{3,2,1,0:T(8,128)S(1)}, u32[]{:S(2)}, u32[]{:S(2)}) collective-permute-start(f32[2,4,8,128]{3,2,1,0:T(8,128)S(1)} %get-tuple-element.45.p1), channel_id=1, source_target_pairs={{0,4},{4,0},{1,5},{5,1},{2,6},{6,2},{3,7},{7,3},{8,12},{12,8},{9,1... | collective-permute-start | bytes 98312 | tf_op jit(solution)/shard_map/ppermute | solution.py:977
  28.6 0.9 %collective-permute-start.4 = (f32[2,4,8,128]{3,2,1,0:T(8,128)S(1)}, f32[2,4,8,128]{3,2,1,0:T(8,128)S(1)}, u32[]{:S(2)}, u32[]{:S(2)}) collective-permute-start(f32[2,4,8,128]{3,2,1,0:T(8,128)S(1)} %get-tuple-element.45.p1), channel_id=1, source_target_pairs={{0,24},{8,0},{16,8},{24,16},{1,25},{9,1},{17,9},{25,17},{2,26},{10... | collective-permute-start | bytes 98312 | tf_op jit(solution)/shard_map/ppermute | solution.py:977
  29.6 0.8 %collective-permute-start.6 = (f32[16,128]{1,0:T(8,128)S(1)}, f32[16,128]{1,0:T(8,128)S(1)}, u32[]{:S(2)}, u32[]{:S(2)}) collective-permute-start(f32[16,128]{1,0:T(8,128)S(1)} %get-tuple-element.46), channel_id=1, source_target_pairs={{0,12},{4,8},{8,20},{12,16},{16,28},{20,24},{24,4},{28,0},{1,13},{... | collective-permute-start | bytes 24584 | tf_op jit(solution)/shard_map/ppermute | solution.py:984
  30.4 1.8 %collective-permute-start.7 = (f32[16,128]{1,0:T(8,128)S(1)}, f32[16,128]{1,0:T(8,128)S(1)}, u32[]{:S(2)}, u32[]{:S(2)}) collective-permute-start(f32[16,128]{1,0:T(8,128)S(1)} %get-tuple-element.47), channel_id=1, source_target_pairs={{0,28},{4,24},{8,4},{12,0},{16,12},{20,8},{24,20},{28,16},{1,29},{... | collective-permute-start | bytes 24584 | tf_op jit(solution)/shard_map/ppermute | solution.py:984
  32.2 0.4 weights.1
  32.6 1.0 %collective-permute-done.6.refs_0_ = f32[16,128]{1,0:T(8,128)S(1)} collective-permute-done((f32[16,128]{1,0:T(8,128)S(1)}, f32[16,128]{1,0:T(8,128)S(1)}, u32[]{:S(2)}, u32[]{:S(2)}) %collective-permute-start.6) | collective-permute-done | bytes 8224 | tf_op jit(solution)/shard_map/ppermute | solution.py:984
  33.6 0.1 collective-permute-done.7.refs_1_
  33.7 5.2 %all-to-all-done.1.slots.slots1 = f32[32,5,4,128]{3,2,1,0:T(4,128)S(1)} async-done(((f32[32,5,4,128]{3,2,1,0:T(4,128)}), f32[32,5,4,128]{3,2,1,0:T(4,128)S(1)}, u32[]{:S(2)}, u32[]{:S(2)}) %all-to-all-start.1) | async-done | bytes 327712 | tf_op jit(solution)/shard_map/all_to_all | solution.py:988
  39.0 2.0 %coarse.1 = (f32[2,4,8,128]{3,2,1,0:T(8,128)S(1)}, f32[2,4,8,128]{3,2,1,0:T(8,128)S(1)}) custom-call(f32[32,5,4,128]{3,2,1,0:T(4,128)S(1)} %all-to-all-done.1.slots.slots1, f32[8,4,8,128]{3,2,1,0:T(8,128)S(1)} %get-tuple-element.53.refs_0_, f32[4,4,8,128]{3,2,1,0:T(8,128)S(1)} %get-tuple-element.54.refs_1_, f32[2,2,8,128]{3,2,1,0:T(8,128)S(1)} %get-tuple-element.55.refs_2_, ...), custom_call_target="tpu_custom_call" | custom-call | tf_op jit(solution)/shard_map/coarse/pallas_call | solution.py:972
  41.0 0.2 collective-permute-start.8
  41.1 1.0 %ortho.1 = (f32[4,8,16,128]{3,2,1,0:T(8,128)}, f32[4,4]{1,0:T(4,128)}, f32[4,4]{1,0:T(4,128)}) custom-call(f32[4,8,16,128]{3,2,1,0:T(8,128)S(1)} %copy-done, f32[4,8,16,128]{3,2,1,0:T(8,128)S(1)} %copy-done.1, f32[32,5,4,128]{3,2,1,0:T(4,128)S(1)} %all-to-all-done.1.slots.slots1), custom_call_target="tpu_custom_call" | custom-call | tf_op jit(solution)/shard_map/ortho/pallas_call | solution.py:972
  42.1 0.8 %third.1 = (f32[4,10,16,128]{3,2,1,0:T(8,128)S(1)}, f32[4,10,16,128]{3,2,1,0:T(8,128)S(1)}) custom-call(f32[2,4,8,128]{3,2,1,0:T(8,128)S(1)} %get-tuple-element.45.p1, f32[2,4,8,128]{3,2,1,0:T(8,128)S(1)} %collective-permute-done.3.xl, f32[2,4,8,128]{3,2,1,0:T(8,128)S(1)} %collective-permute-done.4.xh, f32[2,4,8,128]{3,2,1,0:T(8,128)S(1)} %collective-permute-done.5.yl.yh, ...), custom_call_target="tpu_custom_call" | custom-call | tf_op jit(solution)/shard_map/third/pallas_call | solution.py:972
  43.0 2.1 %last.1 = (f32[4,8,16,128]{3,2,1,0:T(8,128)}, f32[4,8,16,128]{3,2,1,0:T(8,128)}) custom-call(f32[2,4,8,128]{3,2,1,0:T(8,128)S(1)} %get-tuple-element.57.mine, f32[2,4,8,128]{3,2,1,0:T(8,128)S(1)} %collective-permute-done.8.other, f32[4,10,16,128]{3,2,1,0:T(8,128)S(1)} %get-tuple-element.65.G1, f32[4,10,16,128]{3,2,1,0:T(8,128)S(1)} %get-tuple-element.66.S1, ...), custom_call_target="tpu_custom_call" | custom-call | tf_op jit(solution)/shard_map/last/pallas_call | solution.py:972
  (12 shorter events, 0.0 us)
Async XLA Ops:
  3.0 10.9 %copy-start = (f32[4,8,16,128]{3,2,1,0:T(8,128)S(1)}, f32[4,8,16,128]{3,2,1,0:T(8,128)}, u32[]{:S(2)}) copy-start(f32[4,8,16,128]{3,2,1,0:T(8,128)} %old.3) | copy-start | bytes 786436
  3.1 10.9 %copy-start.1 = (f32[4,8,16,128]{3,2,1,0:T(8,128)S(1)}, f32[4,8,16,128]{3,2,1,0:T(8,128)}, u32[]{:S(2)}) copy-start(f32[4,8,16,128]{3,2,1,0:T(8,128)} %prev.3) | copy-start | bytes 786436
  3.1 18.1 %all-to-all-start = ((f32[32,4,4,128]{3,2,1,0:T(4,128)}), f32[32,4,4,128]{3,2,1,0:T(4,128)S(1)}, u32[]{:S(2)}, u32[]{:S(2)}) async-start(f32[32,4,4,128]{3,2,1,0:T(4,128)} %get-tuple-element.43), calls=%async_computation | async-start | bytes 524288 | tf_op jit(solution)/shard_map/all_to_all | solution.py:988
  10.4 6.6 %collective-permute-start = (f32[13,16,128]{2,1,0:T(8,128)S(1)}, f32[13,16,128]{2,1,0:T(8,128)S(1)}, u32[]{:S(2)}, u32[]{:S(2)}) collective-permute-start(f32[13,16,128]{2,1,0:T(8,128)S(1)} %get-tuple-element.40), channel_id=1, source_target_pairs={{0,8},{8,16},{16,24},{24,0},{1,9},{9,17},{17,25},{25,1},{2,10},{10... | collective-permute-start | bytes 319496 | tf_op jit(solution)/shard_map/ppermute | solution.py:977
  10.7 6.3 %collective-permute-start.1 = (f32[13,16,128]{2,1,0:T(8,128)S(1)}, f32[13,16,128]{2,1,0:T(8,128)S(1)}, u32[]{:S(2)}, u32[]{:S(2)}) collective-permute-start(f32[13,16,128]{2,1,0:T(8,128)S(1)} %get-tuple-element.41), channel_id=1, source_target_pairs={{0,24},{8,0},{16,8},{24,16},{1,25},{9,1},{17,9},{25,17},{2,26},{10... | collective-permute-start | bytes 319496 | tf_op jit(solution)/shard_map/ppermute | solution.py:977
  12.2 9.0 %copy-start.2 = (f32[8,16,128]{2,1,0:T(8,128)S(1)}, f32[8,16,128]{2,1,0:T(8,128)}, u32[]{:S(2)}) copy-start(f32[8,16,128]{2,1,0:T(8,128)} %c.3) | copy-start | bytes 196612
  12.2 4.8 %collective-permute-start.2 = (f32[17,8,128]{2,1,0:T(8,128)S(1)}, f32[17,8,128]{2,1,0:T(8,128)S(1)}, u32[]{:S(2)}, u32[]{:S(2)}) collective-permute-start(f32[17,8,128]{2,1,0:T(8,128)S(1)} %get-tuple-element.42), channel_id=1, source_target_pairs={{0,4},{4,0},{1,5},{5,1},{2,6},{6,2},{3,7},{7,3},{8,12},{12,8},{9,1... | collective-permute-start | bytes 208904 | tf_op jit(solution)/shard_map/ppermute | solution.py:977
  24.3 14.6 %all-to-all-start.1 = ((f32[32,5,4,128]{3,2,1,0:T(4,128)}), f32[32,5,4,128]{3,2,1,0:T(4,128)S(1)}, u32[]{:S(2)}, u32[]{:S(2)}) async-start(f32[32,5,4,128]{3,2,1,0:T(4,128)} %get-tuple-element.44), calls=%async_computation.1 | async-start | bytes 655360 | tf_op jit(solution)/shard_map/all_to_all | solution.py:988
  26.9 6.8 %collective-permute-start.5 = (f32[2,4,8,128]{3,2,1,0:T(8,128)S(1)}, f32[2,4,8,128]{3,2,1,0:T(8,128)S(1)}, u32[]{:S(2)}, u32[]{:S(2)}) collective-permute-start(f32[2,4,8,128]{3,2,1,0:T(8,128)S(1)} %get-tuple-element.45.p1), channel_id=1, source_target_pairs={{0,4},{4,0},{1,5},{5,1},{2,6},{6,2},{3,7},{7,3},{8,12},{12,8},{9,1... | collective-permute-start | bytes 98312 | tf_op jit(solution)/shard_map/ppermute | solution.py:977
  28.6 5.1 %collective-permute-start.4 = (f32[2,4,8,128]{3,2,1,0:T(8,128)S(1)}, f32[2,4,8,128]{3,2,1,0:T(8,128)S(1)}, u32[]{:S(2)}, u32[]{:S(2)}) collective-permute-start(f32[2,4,8,128]{3,2,1,0:T(8,128)S(1)} %get-tuple-element.45.p1), channel_id=1, source_target_pairs={{0,24},{8,0},{16,8},{24,16},{1,25},{9,1},{17,9},{25,17},{2,26},{10... | collective-permute-start | bytes 98312 | tf_op jit(solution)/shard_map/ppermute | solution.py:977
  29.6 4.1 %collective-permute-start.3 = (f32[2,4,8,128]{3,2,1,0:T(8,128)S(1)}, f32[2,4,8,128]{3,2,1,0:T(8,128)S(1)}, u32[]{:S(2)}, u32[]{:S(2)}) collective-permute-start(f32[2,4,8,128]{3,2,1,0:T(8,128)S(1)} %get-tuple-element.45.p1), channel_id=1, source_target_pairs={{0,8},{8,16},{16,24},{24,0},{1,9},{9,17},{17,25},{25,1},{2,10},{10... | collective-permute-start | bytes 98312 | tf_op jit(solution)/shard_map/ppermute | solution.py:977
  29.6 4.0 %collective-permute-start.6 = (f32[16,128]{1,0:T(8,128)S(1)}, f32[16,128]{1,0:T(8,128)S(1)}, u32[]{:S(2)}, u32[]{:S(2)}) collective-permute-start(f32[16,128]{1,0:T(8,128)S(1)} %get-tuple-element.46), channel_id=1, source_target_pairs={{0,12},{4,8},{8,20},{12,16},{16,28},{20,24},{24,4},{28,0},{1,13},{... | collective-permute-start | bytes 24584 | tf_op jit(solution)/shard_map/ppermute | solution.py:984
  30.4 3.3 %collective-permute-start.7 = (f32[16,128]{1,0:T(8,128)S(1)}, f32[16,128]{1,0:T(8,128)S(1)}, u32[]{:S(2)}, u32[]{:S(2)}) collective-permute-start(f32[16,128]{1,0:T(8,128)S(1)} %get-tuple-element.47), channel_id=1, source_target_pairs={{0,28},{4,24},{8,4},{12,0},{16,12},{20,8},{24,20},{28,16},{1,29},{... | collective-permute-start | bytes 24584 | tf_op jit(solution)/shard_map/ppermute | solution.py:984
  41.0 2.0 %collective-permute-start.8 = (f32[2,4,8,128]{3,2,1,0:T(8,128)S(1)}, f32[2,4,8,128]{3,2,1,0:T(8,128)S(1)}, u32[]{:S(2)}, u32[]{:S(2)}) collective-permute-start(f32[2,4,8,128]{3,2,1,0:T(8,128)S(1)} %get-tuple-element.58), channel_id=1, source_target_pairs={{0,8},{8,0},{16,24},{24,16},{1,9},{9,1},{17,25},{25,17},{2,10},{10... | collective-permute-start | bytes 98312 | tf_op jit(solution)/shard_map/ppermute | solution.py:1176

commit v5 on v4

--- a/solution.py
+++ b/solution.py
@@ -460,16 +460,24 @@
         m = scaled(x_flag(place, i, X1), mask)
         for v in range(V):
             get = lambda j: GL[v, j]
-            VL[v, i] = m * (PRE_G * GL[v, i] + PRE_N * level1_sum(get, i))
-    block = {1: 0, 2: 1, 3: 2 * V, 0: 2 * V + 1}
+            if H <= i < H + X1:
+                VL[v, i] = m * (PRE_G * GL[v, i] + PRE_N * level1_sum(get, i))
+            else:
+                VL[v, i] = m * (PRE_N * GL[v, i + 1 if i < H else i - 1])
+    block = {1: 0, 2: 2, 3: 2 * V, 0: 2 * V + 2}
     for w in range(X1 // 2 + 2):
         for v in range(V):
             total = None
             for i in (H - 2 + 2 * w, H - 1 + 2 * w):
                 get = lambda j: VL[v, j]
-                part = CE[i] * (6.0 * (GL[v, i] - VL[v, i]) + level1_sum(get, i))
+                if i == H - 2 or i == H + X1 + 1:
+                    part = CE[i] * VL[v, i + 1 if i < H else i - 1]
+                elif H <= i < H + X1:
+                    part = CE[i] * (6.0 * (GL[v, i] - VL[v, i]) + level1_sum(get, i))
+                else:
+                    part = CE[i] * (level1_sum(get, i) - 6.0 * VL[v, i])
                 total = part if total is None else total + part
-            Q[pl.ds((block[w] + 2 * v) * R1, R1)] = total
+            Q[pl.ds((block[w] + 4 * (v // 2) + v % 2) * R1, R1)] = total
     li, lo = iota((Z, Z), 0), iota((Z, Z), 1)
     width, m = half // 2, 4 * V
     stack = []
@@ -598,35 +606,39 @@
 
     def one(y, x):
         y, j = y // parts_y, y % parts_y
-        acc = roll(tile[(x * ny + y) * nz], -width * j, 1)
+        acc = roll(tile[x, y, 0], -width * j, 1)
         for z in range(1, nz):
-            acc = jnp.where(lane // width == z, roll(tile[(x * ny + y) * nz + z], width * (z - j), 1), acc)
+            acc = jnp.where(lane // width == z, roll(tile[x, y, z], width * (z - j), 1), acc)
         return acc
 
-    return grid_of(ny * parts_y, nx, one)
-
-
-def gather_parts(counts, parts_y, slots, lane, odd):
+    return grid_of(ny * parts_y, nx // 2, one)
+
+
+def gather_parts(counts, parts_y, slots, lane, row):
     nx, ny, nz = counts
     width = lane.shape[1] // parts_y
 
+    half = lane.shape[1] // 2
+
     def tile(x, y, z, k):
-        t = (x * ny + y) * nz + z
-        return jnp.concatenate([slots[t, k], slots[t, k]], axis=0)
-
-    def joined(own, beside, x, y, z):
-        zero = jnp.zeros(lane.shape, jnp.float32)
-        before = beside[x - 1, y, z] if x else zero
-        after = beside[x + 1, y, z] if x < nx - 1 else zero
-        return own[x, y, z] + jnp.where(odd, after, before)
-
-    half = lane.shape[1] // 2
-    every = [(x, y, z) for x in range(nx) for y in range(ny) for z in range(nz)]
+        t = (2 * x * ny + y) * nz + z
+        return jnp.concatenate([slots[t, k], slots[t + ny * nz, k]], axis=0)
+
+    every = [(x, y, z) for x in range(nx // 2) for y in range(ny) for z in range(nz)]
     edges, ends = {p: tile(*p, 1) for p in every}, {p: tile(*p, 3) for p in every}
     own = {p: tile(*p, 0) for p in every}
-    beside = {p: tile(*p, 2) for p in every}
+    beside = {p: roll(tile(*p, 2), 4, 0) for p in every}
     own_rim = {p: jnp.where(lane < half, edges[p], ends[p]) for p in every}
-    beside_rim = {p: jnp.where(lane < half, roll(edges[p], half, 1), roll(ends[p], -16, 1)) for p in every}
+    beside_rim = {
+        p: roll(jnp.where(lane < half, roll(edges[p], half, 1), roll(ends[p], -16, 1)), 4, 0) for p in every
+    }
+    zero = jnp.zeros(lane.shape, jnp.float32)
+
+    def joined(own, beside, x, y, z):
+        before = beside[x - 1, y, z] if x else zero
+        after = beside[x + 1, y, z] if x < nx // 2 - 1 else zero
+        return own[x, y, z] + jnp.where(row < 2, before, jnp.where(row >= 6, after, beside[x, y, z]))
+
     main = {p: joined(own, beside, *p) for p in every}
     rim = {p: joined(own_rim, beside_rim, *p) for p in every}
 
@@ -653,7 +665,7 @@
             total = acc if total is None else total + acc
         return total
 
-    return grid_of(ny * parts_y, nx, one)
+    return grid_of(ny * parts_y, nx // 2, one)
 
 
 def combine(fn, *grids):
@@ -668,11 +680,13 @@
     return total
 
 
-def shrink_tiles(v, level, odd, lane):
+def shrink_tiles(v, level, row, lane):
     step = 2 ** (level - 2)
     v = [[a + b for a, b in zip(v[2 * y], v[2 * y + 1])] for y in range(len(v) // 2)]
     if level == 2:
-        v = combine(lambda t: t + jnp.where(odd, roll(t, 1, 0), roll(t, -1, 0)), v)
+        v = combine(lambda t: t + jnp.where((row // 2) % 2 == 1, roll(t, 2, 0), roll(t, -2, 0)), v)
+    elif level == 3:
+        v = combine(lambda t: t + roll(t, 4, 0), v)
     else:
         v = [[line[2 * x] + line[2 * x + 1] for x in range(len(line) // 2)] for line in v]
     upper = (lane // step) % 2 == 1
@@ -681,16 +695,23 @@
 
 def weights_kernel(counts, parts_y, c2s, *outs):
     lane = iota((8, outs[0].shape[-1]), 1)
-    odd = iota(lane.shape, 0) % 2 == 1
-    count = counts[0] * counts[1] * counts[2]
-    rows = [jnp.where(odd, c2s[t, pl.ds(1, 1)], c2s[t, pl.ds(0, 1)]) for t in range(count)]
-    c = assemble(counts, parts_y, rows, lane)
+    row = iota(lane.shape, 0)
+    nx, ny, nz = counts
+
+    def tile(x, y, z):
+        t = (2 * x * ny + y) * nz + z
+        u = t + ny * nz
+        low = jnp.where(row < 2, c2s[t, pl.ds(0, 1)], c2s[t, pl.ds(1, 1)])
+        return jnp.where(row < 4, low, jnp.where(row < 6, c2s[u, pl.ds(0, 1)], c2s[u, pl.ds(1, 1)]))
+
+    every = [(x, y, z) for x in range(nx // 2) for y in range(ny) for z in range(nz)]
+    c = assemble(counts, parts_y, {p: tile(*p) for p in every}, lane)
     for level in range(2, LEVELS):
         for y in range(len(c)):
             for x in range(len(c[0])):
                 outs[level - 2][y, x] = (0.25**level) * c[y][x]
         if level < LEVELS - 1:
-            c = shrink_tiles(c, level, odd, lane)
+            c = shrink_tiles(c, level, row, lane)
 
 
 def coarse_kernel(counts, parts_y, slots1, *refs):
@@ -700,7 +721,7 @@
     place = Place(counts)
     width = Z // parts_y
     lane = iota((8, Z), 1)
-    odd = iota((8, Z), 0) % 2 == 1
+    row = iota((8, Z), 0)
     zero = jnp.zeros((8, Z), jnp.float32)
     scale = {2 + i: ref for i, ref in enumerate(weights)}
     inverse = {}
@@ -713,24 +734,26 @@
 
     def neighbours(v, level):
         step = 2 ** (level - 2)
-        ahead = [[roll(t, -1, 0) for t in line] for line in v] if level == 2 else None
-        back = [[roll(t, 1, 0) for t in line] for line in v] if level == 2 else None
+        shift = {2: 2, 3: 4}.get(level)
+        ahead = combine(lambda t: roll(t, -shift, 0), v) if shift else v
+        back = combine(lambda t: roll(t, shift, 0), v) if level == 2 else ahead
 
         def one(y, x):
             t = v[y][x]
             zs = jnp.where(lane < step, zero, roll(t, step, 1)) + jnp.where(lane >= Z - step, zero, roll(t, -step, 1))
             ys = add(zs, at(v, y - 1, x), at(v, y + 1, x))
-            if level > 2:
+            if not shift:
                 return add(ys, at(v, y, x - 1), at(v, y, x + 1))
-            return ys + jnp.where(
-                odd, add(back[y][x], at(back, y, x + 1)), add(ahead[y][x], at(ahead, y, x - 1))
-            )
+            after, before = at(ahead, y, x + 1), at(back, y, x - 1)
+            after, before = zero if after is None else after, zero if before is None else before
+            up = jnp.where(row >= 8 - shift, after, ahead[y][x])
+            return ys + up + jnp.where(row < shift, before, back[y][x])
 
         return grid_of(len(v), len(v[0]), one)
 
     def grow(v, level):
         v = [line for line in v for _ in range(2)]
-        return v if level == 2 else [[t for t in line for _ in range(2)] for line in v]
+        return v if level < 4 else [[t for t in line for _ in range(2)] for line in v]
 
     def sweep(v, g, level):
         return combine(lambda a, b, s: KEEP * a + OMEGA * b + SIXTH * s, v, g, neighbours(v, level))
@@ -744,29 +767,29 @@
         v = combine(lambda b, s: PRE_G * b + PRE_N * s, g, neighbours(g, level))
         c = grid_of(len(g), len(g[0]), lambda y, x: scale[level][y, x])
         r = combine(lambda c, b, a, s: c * (6.0 * (b - a) + s), c, g, v, neighbours(v, level))
-        down = shrink_tiles(r, level, odd, lane)
+        down = shrink_tiles(r, level, row, lane)
         down = grid_of(len(down), len(down[0]), lambda y, x: down[y][x] * inverse[level + 1][y][x])
         v = combine(lambda a, b: a + b, v, grow(cycle(down, level + 1), level))
         return sweep(v, g, level)
 
-    b2 = gather_parts(counts, parts_y, slots1, lane, odd)
-    v = cycle(grid_of(len(b2), nx, lambda y, x: b2[y][x] * inverse[2][y][x]), 2)
+    b2 = gather_parts(counts, parts_y, slots1, lane, row)
+    v = cycle(grid_of(len(b2), nx // 2, lambda y, x: b2[y][x] * inverse[2][y][x]), 2)
     for y in range(len(v)):
-        for x in range(nx):
+        for x in range(nx // 2):
             W[y, x] = v[y][x]
     pre[...] = jnp.zeros_like(pre)
     ix, iy, iz = place.at
     for side, dev in enumerate((ix, ix + 1 - 2 * (ix % 2))):
         for xw in range(4):
-            x = dev + (xw + 1) // 2 - 1
-            x_ok = jnp.logical_and(x >= 0, x < nx)
-            x = jnp.clip(x, 0, nx - 1)
+            x = 2 * dev + xw - 1
+            x_ok = jnp.logical_and(x >= 0, x < 2 * nx)
+            x = jnp.clip(x, 0, 2 * nx - 1)
             for j in range(-1, parts_y + 1):
                 y = iy * parts_y + j
                 ok = jnp.logical_and(x_ok, jnp.logical_and(y >= 0, y < ny * parts_y))
                 y = jnp.clip(y, 0, ny * parts_y - 1)
                 for vec in range(2):
-                    line = W[y, x, pl.ds(vec * 2 + (xw + 1) % 2, 1)]
+                    line = W[y, x // 4, pl.ds(2 * (x % 4) + vec, 1)]
                     pre[2 * side + vec, xw, pl.ds(j % 8, 1)] = keep(ok, line)
     li, lo = iota((Z, Z), 0), iota((Z, Z), 1)
     z1 = jnp.where(lo < 96, lo, lo - Z)
@@ -801,19 +824,20 @@
             get = lambda j: C1[v, j]
             tiles.append(m * (KEEP * C1[v, i] + OMEGA * G1[v, i] + SIXTH * level1_sum(get, i)))
         fine.append(jnp.concatenate(tiles, axis=0))
-    li, lo = iota((Z, Z), 0), iota((Z, Z), 1)
-    double = onehot(li == lo // 2)
+    li, lo = iota((Z, 2 * Z), 0), iota((Z, 2 * Z), 1)
     half = Z // 2
     k = lo % 16
     source = jnp.where(k < H, Z - 1, jnp.where(k < 6, 0, jnp.where(k < 8, half - 1, half)))
-    rim = None
+    group = (lo - Z) // 16
+    rim, doubled = None, []
     for v in range(V):
-        part = dot(fine[v], onehot((li == source) & (lo // 16 == v)))
-        rim = part if rim is None else rim + part
+        both = dot(fine[v], onehot(((lo < Z) & (li == lo // 2)) | ((lo >= Z) & (li == source) & (group == v))))
+        doubled.append(both[:, 0:Z])
+        rim = both[:, Z:] if rim is None else rim + both[:, Z:]
     sub = iota((8, Z), 0)
     zero8 = jnp.zeros((8, Z), jnp.float32)
     for v in range(V + 1):
-        wide = dot(fine[v], double) if v < V else rim
+        wide = doubled[v] if v < V else rim
         for i in range(n):
             base = (v * n + i) * R
             tile = wide[i * R1 : i * R1 + Y1]
@@ -996,7 +1020,7 @@
 
     def across_x(own, beside):
         own, beside = (
-            t.reshape(nx, ny, nz, lead, 2, Z).transpose(3, 4, 0, 1, 2, 5) for t in (own, beside)
+            t.reshape(nx, ny, nz, 2, lead, Z).transpose(4, 3, 0, 1, 2, 5) for t in (own, beside)
         )
         pad = ((0, 0), (1, 1), (0, 0), (0, 0), (0, 0))
         first = own[:, 0] + jnp.pad(beside[:, 0], pad)[:, 0:nx]
@@ -1155,11 +1179,11 @@
         plain=(0, 1),
     )
     parts_y = Y // 4
-    if near and counts[2] * (Z // parts_y) == Z:
-        sizes = [(counts[1] * parts_y, counts[0], 8, Z)]
+    if near and counts[2] * (Z // parts_y) == Z and counts[0] % 4 == 0:
+        sizes = [(counts[1] * parts_y, counts[0] // 2, 8, Z)]
         for level in range(3, LEVELS):
             y, x = sizes[-1][:2]
-            sizes.append((y // 2, x if level == 3 else x // 2, 8, Z))
+            sizes.append((y // 2, x if level < 5 else x // 2, 8, Z))
         weights = run(
             near, functools.partial(weights_kernel, counts, parts_y), sizes, (c2s,), name="weights"
         )

time: 45.4 us -> 45 us (level)
  transfers between devices with their start and end apart: 11 -> 11, of which waited for: 5 -> 5; matrix products, arithmetic and copies ran while one was open for 0% -> 0% of each run, Pallas kernels for 6% -> 5%
where the time goes in v5:
time: 45 us; the launch traced here: 44.7 us
  starting transfers between devices  19 us (42%)
  waiting for transfers between devices  13.3 us (30%)
  Pallas kernels  11.8 us (26%)
  between operations  0.7 us (2%)
    pallas_call x8, Pallas kernels, run(): return fn(*args)  11.8 us
    all_to_all x2, starting transfers between devices, swap(): return lax.all_to_all(slots, AXES, split_axis=0, concat_axis=0, tiled=True)  9.92 us
    all_to_all x2, waiting for transfers between devices, swap(): return lax.all_to_all(slots, AXES, split_axis=0, concat_axis=0, tiled=True)  9.37 us
    ppermute x6, starting transfers between devices, shift(): return lax.ppermute(value, axis, [(i, (i + step) % n) for i in range(n)])  6.21 us
    ppermute x6, waiting for transfers between devices, shift(): return lax.ppermute(value, axis, [(i, (i + step) % n) for i in range(n)])  2.74 us
    ppermute x2, starting transfers between devices, diagonal(): return lax.ppermute(value, ('gx', 'gy'), pairs)  2.64 us
    ppermute x2, waiting for transfers between devices, diagonal(): return lax.ppermute(value, ('gx', 'gy'), pairs)  1.15 us
  transfers between devices with their start and end apart: 11, of which 5 were waited for; matrix products, arithmetic and copies ran while one was open for 0% of the time, Pallas kernels for 5%

profile of v5, /device:TPU:0, one launch (start us, length us, event | category | flops | bytes accessed | tf_op | source)
XLA Modules:
  0.0 44.7 jit_solution(15284989447513144095)
XLA Ops:
  0.6 2.4 %first.1 = (f32[4,8,16,128]{3,2,1,0:T(8,128)S(1)}, f32[13,16,128]{2,1,0:T(8,128)S(1)}, f32[13,16,128]{2,1,0:T(8,128)S(1)}, f32[17,8,128]{2,1,0:T(8,128)S(1)}, f3...) custom-call(f32[4,8,16,128]{3,2,1,0:T(8,128)} %inc_hbm.1, f32[8,16,128]{2,1,0:T(8,128)} %c.3), custom_call_target="tpu_custom_call" | custom-call | tf_op jit(solution)/shard_map/first/pallas_call | solution.py:996
  3.1 0.0 copy-start.1
  3.1 7.3 %all-to-all-start = ((f32[32,4,4,128]{3,2,1,0:T(4,128)}), f32[32,4,4,128]{3,2,1,0:T(4,128)S(1)}, u32[]{:S(2)}, u32[]{:S(2)}) async-start(f32[32,4,4,128]{3,2,1,0:T(4,128)} %get-tuple-element.43), calls=%async_computation | async-start | bytes 524288 | tf_op jit(solution)/shard_map/all_to_all | solution.py:1012
  10.4 0.3 collective-permute-start
  10.7 1.5 %collective-permute-start.1 = (f32[13,16,128]{2,1,0:T(8,128)S(1)}, f32[13,16,128]{2,1,0:T(8,128)S(1)}, u32[]{:S(2)}, u32[]{:S(2)}) collective-permute-start(f32[13,16,128]{2,1,0:T(8,128)S(1)} %get-tuple-element.41), channel_id=1, source_target_pairs={{0,24},{8,0},{16,8},{24,16},{1,25},{9,1},{17,9},{25,17},{2,26},{10... | collective-permute-start | bytes 319496 | tf_op jit(solution)/shard_map/ppermute | solution.py:1001
  12.2 1.8 %collective-permute-start.2 = (f32[17,8,128]{2,1,0:T(8,128)S(1)}, f32[17,8,128]{2,1,0:T(8,128)S(1)}, u32[]{:S(2)}, u32[]{:S(2)}) collective-permute-start(f32[17,8,128]{2,1,0:T(8,128)S(1)} %get-tuple-element.42), channel_id=1, source_target_pairs={{0,4},{4,0},{1,5},{5,1},{2,6},{6,2},{3,7},{7,3},{8,12},{12,8},{9,1... | collective-permute-start | bytes 208904 | tf_op jit(solution)/shard_map/ppermute | solution.py:1001
  14.0 0.3 gram.1
  14.3 2.7 %collective-permute-done.2.yl.yh = f32[17,8,128]{2,1,0:T(8,128)S(1)} collective-permute-done((f32[17,8,128]{2,1,0:T(8,128)S(1)}, f32[17,8,128]{2,1,0:T(8,128)S(1)}, u32[]{:S(2)}, u32[]{:S(2)}) %collective-permute-start.2) | collective-permute-done | bytes 69664 | tf_op jit(solution)/shard_map/ppermute | solution.py:1001
  17.0 4.1 %all-to-all-done.slots = f32[32,4,4,128]{3,2,1,0:T(4,128)S(1)} async-done(((f32[32,4,4,128]{3,2,1,0:T(4,128)}), f32[32,4,4,128]{3,2,1,0:T(4,128)S(1)}, u32[]{:S(2)}, u32[]{:S(2)}) %all-to-all-start) | async-done | bytes 262176 | tf_op jit(solution)/shard_map/all_to_all | solution.py:1012
  21.2 3.1 %second.1 = (f32[5,14,24,128]{3,2,1,0:T(8,128)S(1)}, f32[5,14,24,128]{3,2,1,0:T(8,128)S(1)}, f32[2,4,8,128]{3,2,1,0:T(8,128)S(1)}, f32[32,5,4,128]{3,2,1,0:T(4,1...) custom-call(f32[4,8,16,128]{3,2,1,0:T(8,128)S(1)} %get-tuple-element.38.g, ...), custom_call_target="tpu_custom_call" | custom-call | tf_op jit(solution)/shard_map/second/pallas_call | solution.py:996
  24.2 2.6 %all-to-all-start.1 = ((f32[32,5,4,128]{3,2,1,0:T(4,128)}), f32[32,5,4,128]{3,2,1,0:T(4,128)S(1)}, u32[]{:S(2)}, u32[]{:S(2)}) async-start(f32[32,5,4,128]{3,2,1,0:T(4,128)} %get-tuple-element.44), calls=%async_computation.1 | async-start | bytes 655360 | tf_op jit(solution)/shard_map/all_to_all | solution.py:1012
  26.8 1.7 %collective-permute-start.5 = (f32[2,4,8,128]{3,2,1,0:T(8,128)S(1)}, f32[2,4,8,128]{3,2,1,0:T(8,128)S(1)}, u32[]{:S(2)}, u32[]{:S(2)}) collective-permute-start(f32[2,4,8,128]{3,2,1,0:T(8,128)S(1)} %get-tuple-element.45.p1), channel_id=1, source_target_pairs={{0,4},{4,0},{1,5},{5,1},{2,6},{6,2},{3,7},{7,3},{8,12},{12,8},{9,1... | collective-permute-start | bytes 98312 | tf_op jit(solution)/shard_map/ppermute | solution.py:1001
  28.5 0.9 %collective-permute-start.4 = (f32[2,4,8,128]{3,2,1,0:T(8,128)S(1)}, f32[2,4,8,128]{3,2,1,0:T(8,128)S(1)}, u32[]{:S(2)}, u32[]{:S(2)}) collective-permute-start(f32[2,4,8,128]{3,2,1,0:T(8,128)S(1)} %get-tuple-element.45.p1), channel_id=1, source_target_pairs={{0,24},{8,0},{16,8},{24,16},{1,25},{9,1},{17,9},{25,17},{2,26},{10... | collective-permute-start | bytes 98312 | tf_op jit(solution)/shard_map/ppermute | solution.py:1001
  29.5 0.8 %collective-permute-start.6 = (f32[16,128]{1,0:T(8,128)S(1)}, f32[16,128]{1,0:T(8,128)S(1)}, u32[]{:S(2)}, u32[]{:S(2)}) collective-permute-start(f32[16,128]{1,0:T(8,128)S(1)} %get-tuple-element.46), channel_id=1, source_target_pairs={{0,12},{4,8},{8,20},{12,16},{16,28},{20,24},{24,4},{28,0},{1,13},{... | collective-permute-start | bytes 24584 | tf_op jit(solution)/shard_map/ppermute | solution.py:1008
  30.3 1.8 %collective-permute-start.7 = (f32[16,128]{1,0:T(8,128)S(1)}, f32[16,128]{1,0:T(8,128)S(1)}, u32[]{:S(2)}, u32[]{:S(2)}) collective-permute-start(f32[16,128]{1,0:T(8,128)S(1)} %get-tuple-element.47), channel_id=1, source_target_pairs={{0,28},{4,24},{8,4},{12,0},{16,12},{20,8},{24,20},{28,16},{1,29},{... | collective-permute-start | bytes 24584 | tf_op jit(solution)/shard_map/ppermute | solution.py:1008
  32.1 0.3 weights.1
  32.5 1.0 %collective-permute-done.6.refs_0_ = f32[16,128]{1,0:T(8,128)S(1)} collective-permute-done((f32[16,128]{1,0:T(8,128)S(1)}, f32[16,128]{1,0:T(8,128)S(1)}, u32[]{:S(2)}, u32[]{:S(2)}) %collective-permute-start.6) | collective-permute-done | bytes 8224 | tf_op jit(solution)/shard_map/ppermute | solution.py:1008
  33.5 0.1 collective-permute-done.7.refs_1_
  33.6 5.2 %all-to-all-done.1.slots.slots1 = f32[32,5,4,128]{3,2,1,0:T(4,128)S(1)} async-done(((f32[32,5,4,128]{3,2,1,0:T(4,128)}), f32[32,5,4,128]{3,2,1,0:T(4,128)S(1)}, u32[]{:S(2)}, u32[]{:S(2)}) %all-to-all-start.1) | async-done | bytes 327712 | tf_op jit(solution)/shard_map/all_to_all | solution.py:1012
  38.9 1.8 %coarse.1 = (f32[2,4,8,128]{3,2,1,0:T(8,128)S(1)}, f32[2,4,8,128]{3,2,1,0:T(8,128)S(1)}) custom-call(f32[32,5,4,128]{3,2,1,0:T(4,128)S(1)} %all-to-all-done.1.slots.slots1, f32[8,2,8,128]{3,2,1,0:T(8,128)S(1)} %get-tuple-element.53.refs_0_, f32[4,2,8,128]{3,2,1,0:T(8,128)S(1)} %get-tuple-element.54.refs_1_, f32[2,2,8,128]{3,2,1,0:T(8,128)S(1)} %get-tuple-element.55.refs_2_, ...), custom_call_target="tpu_custom_call" | custom-call | tf_op jit(solution)/shard_map/coarse/pallas_call | solution.py:996
  40.7 0.2 collective-permute-start.8
  40.8 1.0 %ortho.1 = (f32[4,8,16,128]{3,2,1,0:T(8,128)}, f32[4,4]{1,0:T(4,128)}, f32[4,4]{1,0:T(4,128)}) custom-call(f32[4,8,16,128]{3,2,1,0:T(8,128)S(1)} %copy-done, f32[4,8,16,128]{3,2,1,0:T(8,128)S(1)} %copy-done.1, f32[32,5,4,128]{3,2,1,0:T(4,128)S(1)} %all-to-all-done.1.slots.slots1), custom_call_target="tpu_custom_call" | custom-call | tf_op jit(solution)/shard_map/ortho/pallas_call | solution.py:996
  41.8 0.8 %third.1 = (f32[4,10,16,128]{3,2,1,0:T(8,128)S(1)}, f32[4,10,16,128]{3,2,1,0:T(8,128)S(1)}) custom-call(f32[2,4,8,128]{3,2,1,0:T(8,128)S(1)} %get-tuple-element.45.p1, f32[2,4,8,128]{3,2,1,0:T(8,128)S(1)} %collective-permute-done.3.xl, f32[2,4,8,128]{3,2,1,0:T(8,128)S(1)} %collective-permute-done.4.xh, f32[2,4,8,128]{3,2,1,0:T(8,128)S(1)} %collective-permute-done.5.yl.yh, ...), custom_call_target="tpu_custom_call" | custom-call | tf_op jit(solution)/shard_map/third/pallas_call | solution.py:996
  42.6 2.1 %last.1 = (f32[4,8,16,128]{3,2,1,0:T(8,128)}, f32[4,8,16,128]{3,2,1,0:T(8,128)}) custom-call(f32[2,4,8,128]{3,2,1,0:T(8,128)S(1)} %get-tuple-element.57.mine, f32[2,4,8,128]{3,2,1,0:T(8,128)S(1)} %collective-permute-done.8.other, f32[4,10,16,128]{3,2,1,0:T(8,128)S(1)} %get-tuple-element.65.G1, f32[4,10,16,128]{3,2,1,0:T(8,128)S(1)} %get-tuple-element.66.S1, ...), custom_call_target="tpu_custom_call" | custom-call | tf_op jit(solution)/shard_map/last/pallas_call | solution.py:996
  (12 shorter events, 0.0 us)
Async XLA Ops:
  3.0 10.9 %copy-start = (f32[4,8,16,128]{3,2,1,0:T(8,128)S(1)}, f32[4,8,16,128]{3,2,1,0:T(8,128)}, u32[]{:S(2)}) copy-start(f32[4,8,16,128]{3,2,1,0:T(8,128)} %old.3) | copy-start | bytes 786436
  3.1 10.9 %copy-start.1 = (f32[4,8,16,128]{3,2,1,0:T(8,128)S(1)}, f32[4,8,16,128]{3,2,1,0:T(8,128)}, u32[]{:S(2)}) copy-start(f32[4,8,16,128]{3,2,1,0:T(8,128)} %prev.3) | copy-start | bytes 786436
  3.1 18.1 %all-to-all-start = ((f32[32,4,4,128]{3,2,1,0:T(4,128)}), f32[32,4,4,128]{3,2,1,0:T(4,128)S(1)}, u32[]{:S(2)}, u32[]{:S(2)}) async-start(f32[32,4,4,128]{3,2,1,0:T(4,128)} %get-tuple-element.43), calls=%async_computation | async-start | bytes 524288 | tf_op jit(solution)/shard_map/all_to_all | solution.py:1012
  10.4 6.6 %collective-permute-start = (f32[13,16,128]{2,1,0:T(8,128)S(1)}, f32[13,16,128]{2,1,0:T(8,128)S(1)}, u32[]{:S(2)}, u32[]{:S(2)}) collective-permute-start(f32[13,16,128]{2,1,0:T(8,128)S(1)} %get-tuple-element.40), channel_id=1, source_target_pairs={{0,8},{8,16},{16,24},{24,0},{1,9},{9,17},{17,25},{25,1},{2,10},{10... | collective-permute-start | bytes 319496 | tf_op jit(solution)/shard_map/ppermute | solution.py:1001
  10.7 6.3 %collective-permute-start.1 = (f32[13,16,128]{2,1,0:T(8,128)S(1)}, f32[13,16,128]{2,1,0:T(8,128)S(1)}, u32[]{:S(2)}, u32[]{:S(2)}) collective-permute-start(f32[13,16,128]{2,1,0:T(8,128)S(1)} %get-tuple-element.41), channel_id=1, source_target_pairs={{0,24},{8,0},{16,8},{24,16},{1,25},{9,1},{17,9},{25,17},{2,26},{10... | collective-permute-start | bytes 319496 | tf_op jit(solution)/shard_map/ppermute | solution.py:1001
  12.2 9.0 %copy-start.2 = (f32[8,16,128]{2,1,0:T(8,128)S(1)}, f32[8,16,128]{2,1,0:T(8,128)}, u32[]{:S(2)}) copy-start(f32[8,16,128]{2,1,0:T(8,128)} %c.3) | copy-start | bytes 196612
  12.2 4.8 %collective-permute-start.2 = (f32[17,8,128]{2,1,0:T(8,128)S(1)}, f32[17,8,128]{2,1,0:T(8,128)S(1)}, u32[]{:S(2)}, u32[]{:S(2)}) collective-permute-start(f32[17,8,128]{2,1,0:T(8,128)S(1)} %get-tuple-element.42), channel_id=1, source_target_pairs={{0,4},{4,0},{1,5},{5,1},{2,6},{6,2},{3,7},{7,3},{8,12},{12,8},{9,1... | collective-permute-start | bytes 208904 | tf_op jit(solution)/shard_map/ppermute | solution.py:1001
  24.2 14.6 %all-to-all-start.1 = ((f32[32,5,4,128]{3,2,1,0:T(4,128)}), f32[32,5,4,128]{3,2,1,0:T(4,128)S(1)}, u32[]{:S(2)}, u32[]{:S(2)}) async-start(f32[32,5,4,128]{3,2,1,0:T(4,128)} %get-tuple-element.44), calls=%async_computation.1 | async-start | bytes 655360 | tf_op jit(solution)/shard_map/all_to_all | solution.py:1012
  26.8 6.8 %collective-permute-start.5 = (f32[2,4,8,128]{3,2,1,0:T(8,128)S(1)}, f32[2,4,8,128]{3,2,1,0:T(8,128)S(1)}, u32[]{:S(2)}, u32[]{:S(2)}) collective-permute-start(f32[2,4,8,128]{3,2,1,0:T(8,128)S(1)} %get-tuple-element.45.p1), channel_id=1, source_target_pairs={{0,4},{4,0},{1,5},{5,1},{2,6},{6,2},{3,7},{7,3},{8,12},{12,8},{9,1... | collective-permute-start | bytes 98312 | tf_op jit(solution)/shard_map/ppermute | solution.py:1001
  28.5 5.1 %collective-permute-start.4 = (f32[2,4,8,128]{3,2,1,0:T(8,128)S(1)}, f32[2,4,8,128]{3,2,1,0:T(8,128)S(1)}, u32[]{:S(2)}, u32[]{:S(2)}) collective-permute-start(f32[2,4,8,128]{3,2,1,0:T(8,128)S(1)} %get-tuple-element.45.p1), channel_id=1, source_target_pairs={{0,24},{8,0},{16,8},{24,16},{1,25},{9,1},{17,9},{25,17},{2,26},{10... | collective-permute-start | bytes 98312 | tf_op jit(solution)/shard_map/ppermute | solution.py:1001
  29.5 4.1 %collective-permute-start.3 = (f32[2,4,8,128]{3,2,1,0:T(8,128)S(1)}, f32[2,4,8,128]{3,2,1,0:T(8,128)S(1)}, u32[]{:S(2)}, u32[]{:S(2)}) collective-permute-start(f32[2,4,8,128]{3,2,1,0:T(8,128)S(1)} %get-tuple-element.45.p1), channel_id=1, source_target_pairs={{0,8},{8,16},{16,24},{24,0},{1,9},{9,17},{17,25},{25,1},{2,10},{10... | collective-permute-start | bytes 98312 | tf_op jit(solution)/shard_map/ppermute | solution.py:1001
  29.5 4.0 %collective-permute-start.6 = (f32[16,128]{1,0:T(8,128)S(1)}, f32[16,128]{1,0:T(8,128)S(1)}, u32[]{:S(2)}, u32[]{:S(2)}) collective-permute-start(f32[16,128]{1,0:T(8,128)S(1)} %get-tuple-element.46), channel_id=1, source_target_pairs={{0,12},{4,8},{8,20},{12,16},{16,28},{20,24},{24,4},{28,0},{1,13},{... | collective-permute-start | bytes 24584 | tf_op jit(solution)/shard_map/ppermute | solution.py:1008
  30.3 3.3 %collective-permute-start.7 = (f32[16,128]{1,0:T(8,128)S(1)}, f32[16,128]{1,0:T(8,128)S(1)}, u32[]{:S(2)}, u32[]{:S(2)}) collective-permute-start(f32[16,128]{1,0:T(8,128)S(1)} %get-tuple-element.47), channel_id=1, source_target_pairs={{0,28},{4,24},{8,4},{12,0},{16,12},{20,8},{24,20},{28,16},{1,29},{... | collective-permute-start | bytes 24584 | tf_op jit(solution)/shard_map/ppermute | solution.py:1008
  40.7 2.0 %collective-permute-start.8 = (f32[2,4,8,128]{3,2,1,0:T(8,128)S(1)}, f32[2,4,8,128]{3,2,1,0:T(8,128)S(1)}, u32[]{:S(2)}, u32[]{:S(2)}) collective-permute-start(f32[2,4,8,128]{3,2,1,0:T(8,128)S(1)} %get-tuple-element.58), channel_id=1, source_target_pairs={{0,8},{8,0},{16,24},{24,16},{1,9},{9,1},{17,25},{25,17},{2,10},{10... | collective-permute-start | bytes 98312 | tf_op jit(solution)/shard_map/ppermute | solution.py:1200

commit v6 on v5

--- a/solution.py
+++ b/solution.py
@@ -24,7 +24,8 @@
 HB = pl.BlockSpec(memory_space=pltpu.HBM)
 EDGE = ((0, 0), (0, 1), (1, 0))
 EDGE1 = EDGE + ((1, 1), (0, 2), (2, 0))
-TAIL = 4
+TAIL = 3
+CHUNKS = (0, 1, 3)
 
 
 def edge_steps(merge_y):
@@ -108,17 +109,17 @@
         lax.fori_loop(0, count, body, 0)
 
 
-def first_kernel(counts, merge_y, inc_hbm, c_hbm, *refs):
+def first_kernel(counts, merge_y, inc_hbm, c_hbm, old_hbm, prev_hbm, *refs):
     if merge_y:
-        g, xlo, xhi, ymsg, slots, c1, inc, c, QC, sems = refs
+        g, xlo, xhi, ymsg, slots, c1, inc, c, QC, old, prev, sems = refs
     else:
-        g, xlo, xhi, ylo, yhi, slots, c1, inc, c, QC, sems = refs
+        g, xlo, xhi, ylo, yhi, slots, c1, inc, c, QC, old, prev, sems = refs
     V, X, Y, Z = inc.shape
     place = Place(counts)
     copy_c = pltpu.make_async_copy(c_hbm, c, sems.at[V])
     copies = [pltpu.make_async_copy(inc_hbm.at[v], inc.at[v], sems.at[v]) for v in range(V)]
-    copy_c.start()
-    for copy in copies:
+    basis = [pltpu.make_async_copy(a, b, sems.at[V + 1 + i]) for i, (a, b) in enumerate(((old_hbm, old), (prev_hbm, prev)))]
+    for copy in [copy_c] + copies + basis:
         copy.start()
     sub = iota((8, Z), 0)
     lane = iota((8, Z), 1)
@@ -182,6 +183,10 @@
     k = 8 * V
     c_up = jnp.where(l4 < n, faces[k + 1 : k + 2], roll(faces[k : k + 8], n, 1)[0:1])
     c_down = jnp.where(l4 < n, faces[k + 2 : k + 3], roll(faces[k : k + 8], n, 1)[3:4])
+    for copy in basis:
+        copy.wait()
+    base[V - 1] = jnp.where(r4 == H, gram_row(old, prev), zero4)
+    fill_tail(slots, counts[0] * counts[1] * counts[2], V - 1, base[V - 1])
     rows_up = [jnp.where(r4 < H, faces[8 * v : 8 * v + 4], base[v]) for v in range(V)]
     rows_down = [jnp.where(r4 < H, faces[8 * v + H : 8 * v + H + 4], base[v]) for v in range(V)]
     rows_up[2] = jnp.where(r4 < H, rows_up[2], jnp.where(l4 < 2 * n, c_up, zero4))
@@ -255,7 +260,7 @@
     return mask if flag is None else mask * flag
 
 
-def second_kernel(counts, merge_y, g, c, c1, xl, xh, yl, yh, slots, gram, G, S, p1, slots1, c2s, *refs):
+def second_kernel(counts, merge_y, g, c, c1, xl, xh, yl, yh, slots, G, S, p1, slots1, c2s, *refs):
     edges, (Q, CE, GL, VL) = refs[:-4], refs[-4:]
     V, X, Y, Z = g.shape
     R = Y + 8
@@ -370,17 +375,33 @@
             return carry
         lax.fori_loop(0, c2s.shape[0], move, 0)
     around_c1(place, CE, c1, xl, xh, yl, yh, slots, V, X)
-    gram_row = gram[0:1]
-    tiles = contributions(place, U, gram_row, CE, GL, VL, Q, V)
-    up, down = faces[0:4], faces[8:12]
+    tiles = contributions(place, U, CE, GL, VL, Q, V)
+    r4, l4 = iota((4, Z), 0), iota((4, Z), 1)
+
+    def spread_layers(rows):
+        turned = [roll(rows, 32 * k, 1) for k in range(4)]
+        out = jnp.zeros((4, Z), jnp.float32)
+        for v in range(V):
+            for k, chunk in enumerate(CHUNKS):
+                out = jnp.where((r4 == v) & (l4 // 32 == chunk), turned[(chunk - v) % 4][k : k + 1], out)
+        return out
+
+    up, down = spread_layers(faces[0:8]), spread_layers(faces[8:16])
     rest = counts[1] * counts[2]
     for x in range(counts[0]):
         for k, tile in enumerate(tiles[x % 2]):
             fill_tail(slots1.at[pl.ds(x * rest, rest)], rest, k, tile)
+    middle = l4 // 32 == 2
     for dx in (-1, 0, 1):
+        even = (place.at[0] + 2 + dx) % 2 == 0
+        ends = jnp.where(even, tiles[0][TAIL], tiles[1][TAIL])
         for dy in (-1, 0, 1):
-            slots1[place.slot((dx, dy, 1)), TAIL] = up
-            slots1[place.slot((dx, dy, -1)), TAIL] = down
+            for dz, layer in ((1, up), (-1, down)):
+                d = (dx, dy, dz)
+
+                @pl.when(place.has(d))
+                def _():
+                    slots1[place.slot(d), TAIL] = jnp.where(middle, ends, layer)
     for ref, (dx, dy) in zip(edges, edge_steps(merge_y)):
         for cell, (a, b) in enumerate(EDGE1):
             x = X1 - 1 - a if dx > 0 else a
@@ -440,7 +461,7 @@
         CE[H + x, Y1 : 2 * Y1] = CE[H + x, Y1 : 2 * Y1] + edge
 
 
-def contributions(place, U, gram_row, CE, GL, VL, Q, V):
+def contributions(place, U, CE, GL, VL, Q, V):
     X1, R1, Z = CE.shape[0] - 2 * H, CE.shape[1], CE.shape[2]
     Y1, half = R1 // 2, Z // 2
     zero = jnp.zeros((R1, Z), jnp.float32)
@@ -506,7 +527,7 @@
         own, rim = body[r : r + 4], rims[r : r + 4]
         beside, beside_rim = body[q : q + 4], rims[q : q + 4]
         edges = jnp.where(lane4 < half, rim, roll(beside_rim, half, 1))
-        ends = jnp.where(lane4 < half, gram_row, jnp.where(lane4 < half + 16, rim, roll(beside_rim, 16, 1)))
+        ends = jnp.where(lane4 < half + 16, rim, roll(beside_rim, 16, 1))
         pairs.append((own, edges, beside, ends))
     return pairs
 
@@ -546,7 +567,16 @@
         below, above = (dx, dy, -1), (dx, dy, 1)
         low = keep(place.has(below), slots[place.slot(below), TAIL])
         high = keep(place.has(above), slots[place.slot(above), TAIL])
-        return dot(jnp.concatenate([low, high], axis=0), place_lanes, TN)
+        both = jnp.concatenate([low, high], axis=0)
+        turned = [roll(both, 32 * k, 1) for k in range(4)]
+        lines = jnp.zeros((8, Z), jnp.float32)
+        for v in range(V):
+            for k, chunk in enumerate(CHUNKS):
+                source = turned[(v - chunk) % 4]
+                here = l8 // 32 == v
+                lines = jnp.where(here & (r8 == k), source[v : v + 1], lines)
+                lines = jnp.where(here & (r8 == 4 + k), source[4 + v : 5 + v], lines)
+        return dot(lines, place_lanes, TN)
 
     mid, up, down = layers(0, 0), layers(0, 1), layers(0, -1)
     m_hi = jnp.logical_and(row < H, place.hi(1))
@@ -879,7 +909,7 @@
         copy.wait()
 
 
-def gram_kernel(old, prev, out):
+def gram_row(old, prev):
     M, X, Y, Z = old.shape
     J = prev.shape[0]
     pairs = [(a, b) for a in range(M + J) for b in range(a, M + J)]
@@ -894,18 +924,18 @@
     lane = iota((8, Z), 1)
     rows = jnp.concatenate([jnp.sum(s, axis=0, keepdims=True) for s in sums], axis=0)
     pad = jnp.zeros((Z - len(pairs), Z), jnp.float32)
-    out[...] = dot(ones, jnp.concatenate([rows, pad], axis=0), NT)
+    return dot(ones, jnp.concatenate([rows, pad], axis=0), NT)[0:1]
 
 
 def ortho_kernel(count, cells, old, prev, slots, orth, proj, tri):
     M, X, Y, Z = old.shape
     J = prev.shape[0]
     if count <= 64:
-        total = slots[0, TAIL - 1, pl.ds(0, 1)]
+        total = slots[0, M - 1, pl.ds(H, 1)]
         for t in range(1, count):
-            total = total + slots[t, TAIL - 1, pl.ds(0, 1)]
+            total = total + slots[t, M - 1, pl.ds(H, 1)]
     else:
-        total = lax.fori_loop(0, count, lambda t, s: s + slots[t, TAIL - 1, pl.ds(0, 1)], jnp.zeros((1, Z), jnp.float32))
+        total = lax.fori_loop(0, count, lambda t, s: s + slots[t, M - 1, pl.ds(H, 1)], jnp.zeros((1, Z), jnp.float32))
     total = jnp.broadcast_to(total, (8, Z)) / cells
     value = {}
     p = 0
@@ -1128,11 +1158,11 @@
         near,
         functools.partial(first_kernel, counts, merge_y),
         shapes,
-        (inc, c),
-        [inc.shape, c.shape, (X1 * Y, Z)],
+        (inc, c, old, prev),
+        [inc.shape, c.shape, (X1 * Y, Z), old.shape, prev.shape],
         name="first",
         result=(len(shapes) - 2,),
-        sems=V + 1,
+        sems=V + 3,
     )
     g, xlo, xhi = outs[:3]
     c1 = outs[-1]
@@ -1142,14 +1172,13 @@
         yl = yh = shift(outs[3], "gy", 1)
     else:
         yl, yh = shift(outs[4], "gy", 1), shift(outs[3], "gy", -1)
-    (gram,) = run(near, gram_kernel, [(8, Z)], (old, prev), name="gram", plain=(0, 1))
     ext0, ext1 = (V + 1, X + 2 * H, R, Z), (V, X1 + 2 * H, 2 * Y1, Z)
     steps = edge_steps(merge_y)
     G, S, p1, slots1, c2s, *edges = run(
         near,
         functools.partial(second_kernel, counts, merge_y),
         [ext0, ext0, (V // 2, X1, Y1, Z), (count, TAIL + 1, V, Z), (count, V, Z)] + [(16, Z)] * len(steps),
-        (g, c, c1, xl, xh, yl, yh, slots0, gram),
+        (g, c, c1, xl, xh, yl, yh, slots0),
         [(V * X1 * Y, Z), ext1[1:], ext1, ext1],
         name="second",
         result=(3,),
@@ -1173,7 +1202,7 @@
         near,
         functools.partial(ortho_kernel, count, float(count * X * Y * Z)),
         [(V, X, Y, Z), (4, 4), (4, 4)],
-        (old, prev, slots1),
+        (old, prev, slots0),
         name="ortho",
         result=(0, 1, 2),
         plain=(0, 1),

time: 45 us -> 44.5 us (0.989)
  waiting for transfers between devices: 13.3 us -> 11.5 us
  starting transfers between devices: 19 us -> 19.9 us
    all_to_all x2, waiting for transfers between devices: 9.37 us -> 7.18 us  [swap(): return lax.all_to_all(slots, AXES, split_axis=0, concat_axis=0, tiled=True)]
    ppermute x6, starting transfers between devices: 6.21 us -> 7 us  [shift(): return lax.ppermute(value, axis, [(i, (i + step) % n) for i in range(n)])]
    pallas_call x8 -> x7, Pallas kernels: 11.8 us -> 12.2 us  [run(): return fn(*args)]
where the time goes in v6:
time: 44.5 us; the launch traced here: 44.2 us
  starting transfers between devices  19.9 us (45%)
  Pallas kernels  12.2 us (27%)
  waiting for transfers between devices  11.5 us (26%)
  between operations  0.7 us (2%)
    pallas_call x7, Pallas kernels, run(): return fn(*args)  12.2 us
    all_to_all x2, starting transfers between devices, swap(): return lax.all_to_all(slots, AXES, split_axis=0, concat_axis=0, tiled=True)  10 us
    all_to_all x2, waiting for transfers between devices, swap(): return lax.all_to_all(slots, AXES, split_axis=0, concat_axis=0, tiled=True)  7.18 us
    ppermute x6, starting transfers between devices, shift(): return lax.ppermute(value, axis, [(i, (i + step) % n) for i in range(n)])  7 us
    ppermute x6, waiting for transfers between devices, shift(): return lax.ppermute(value, axis, [(i, (i + step) % n) for i in range(n)])  3.06 us
    ppermute x2, starting transfers between devices, diagonal(): return lax.ppermute(value, ('gx', 'gy'), pairs)  2.64 us
    ppermute x2, waiting for transfers between devices, diagonal(): return lax.ppermute(value, ('gx', 'gy'), pairs)  1.25 us
  transfers between devices with their start and end apart: 11, of which 5 were waited for; matrix products, arithmetic and copies ran while one was open for 0% of the time, Pallas kernels for 5%

profile of v6, /device:TPU:0, one launch (start us, length us, event | category | flops | bytes accessed | tf_op | source)
XLA Modules:
  0.0 44.2 jit_solution(4306560915772907264)
XLA Ops:
  0.6 2.8 %first.1 = (f32[4,8,16,128]{3,2,1,0:T(8,128)S(1)}, f32[13,16,128]{2,1,0:T(8,128)S(1)}, f32[13,16,128]{2,1,0:T(8,128)S(1)}, f32[17,8,128]{2,1,0:T(8,128)S(1)}, f3...) custom-call(f32[4,8,16,128]{3,2,1,0:T(8,128)} %inc_hbm.1, f32[8,16,128]{2,1,0:T(8,128)} %c.3, f32[4,8,16,128]{3,2,1,0:T(8,128)} %old.1, ...), custom_call_target="tpu_custom_call" | custom-call | tf_op jit(solution)/shard_map/first/pallas_call | solution.py:1026
  3.4 0.0 copy-start.2
  3.5 7.3 %all-to-all-start = ((f32[32,4,4,128]{3,2,1,0:T(4,128)}), f32[32,4,4,128]{3,2,1,0:T(4,128)S(1)}, u32[]{:S(2)}, u32[]{:S(2)}) async-start(f32[32,4,4,128]{3,2,1,0:T(4,128)} %get-tuple-element.38), calls=%async_computation | async-start | bytes 524288 | tf_op jit(solution)/shard_map/all_to_all | solution.py:1042
  10.8 0.3 collective-permute-start
  11.1 1.5 %collective-permute-start.1 = (f32[13,16,128]{2,1,0:T(8,128)S(1)}, f32[13,16,128]{2,1,0:T(8,128)S(1)}, u32[]{:S(2)}, u32[]{:S(2)}) collective-permute-start(f32[13,16,128]{2,1,0:T(8,128)S(1)} %get-tuple-element.45), channel_id=1, source_target_pairs={{0,24},{8,0},{16,8},{24,16},{1,25},{9,1},{17,9},{25,17},{2,26},{10... | collective-permute-start | bytes 319496 | tf_op jit(solution)/shard_map/ppermute | solution.py:1031
  12.6 1.8 %collective-permute-start.2 = (f32[17,8,128]{2,1,0:T(8,128)S(1)}, f32[17,8,128]{2,1,0:T(8,128)S(1)}, u32[]{:S(2)}, u32[]{:S(2)}) collective-permute-start(f32[17,8,128]{2,1,0:T(8,128)S(1)} %get-tuple-element.46), channel_id=1, source_target_pairs={{0,4},{4,0},{1,5},{5,1},{2,6},{6,2},{3,7},{7,3},{8,12},{12,8},{9,1... | collective-permute-start | bytes 208904 | tf_op jit(solution)/shard_map/ppermute | solution.py:1031
  14.4 3.0 %collective-permute-done.2.yl.yh = f32[17,8,128]{2,1,0:T(8,128)S(1)} collective-permute-done((f32[17,8,128]{2,1,0:T(8,128)S(1)}, f32[17,8,128]{2,1,0:T(8,128)S(1)}, u32[]{:S(2)}, u32[]{:S(2)}) %collective-permute-start.2) | collective-permute-done | bytes 69664 | tf_op jit(solution)/shard_map/ppermute | solution.py:1031
  17.4 4.1 %all-to-all-done.slots = f32[32,4,4,128]{3,2,1,0:T(4,128)S(1)} async-done(((f32[32,4,4,128]{3,2,1,0:T(4,128)}), f32[32,4,4,128]{3,2,1,0:T(4,128)S(1)}, u32[]{:S(2)}, u32[]{:S(2)}) %all-to-all-start) | async-done | bytes 262176 | tf_op jit(solution)/shard_map/all_to_all | solution.py:1042
  21.5 3.2 %second.1 = (f32[5,14,24,128]{3,2,1,0:T(8,128)S(1)}, f32[5,14,24,128]{3,2,1,0:T(8,128)S(1)}, f32[2,4,8,128]{3,2,1,0:T(8,128)S(1)}, f32[32,4,4,128]{3,2,1,0:T(4,1...) custom-call(f32[4,8,16,128]{3,2,1,0:T(8,128)S(1)} %get-tuple-element.42.g, ...), custom_call_target="tpu_custom_call" | custom-call | tf_op jit(solution)/shard_map/second/pallas_call | solution.py:1026
  24.8 2.7 %all-to-all-start.1 = ((f32[32,4,4,128]{3,2,1,0:T(4,128)}), f32[32,4,4,128]{3,2,1,0:T(4,128)S(1)}, u32[]{:S(2)}, u32[]{:S(2)}) async-start(f32[32,4,4,128]{3,2,1,0:T(4,128)} %get-tuple-element.47), calls=%async_computation.1 | async-start | bytes 524288 | tf_op jit(solution)/shard_map/all_to_all | solution.py:1042
  27.5 0.0 copy-start
  27.5 0.2 collective-permute-start.3
  27.7 1.6 %collective-permute-start.4 = (f32[2,4,8,128]{3,2,1,0:T(8,128)S(1)}, f32[2,4,8,128]{3,2,1,0:T(8,128)S(1)}, u32[]{:S(2)}, u32[]{:S(2)}) collective-permute-start(f32[2,4,8,128]{3,2,1,0:T(8,128)S(1)} %get-tuple-element.48.p1), channel_id=1, source_target_pairs={{0,24},{8,0},{16,8},{24,16},{1,25},{9,1},{17,9},{25,17},{2,26},{10... | collective-permute-start | bytes 98312 | tf_op jit(solution)/shard_map/ppermute | solution.py:1031
  29.3 1.6 %collective-permute-start.5 = (f32[2,4,8,128]{3,2,1,0:T(8,128)S(1)}, f32[2,4,8,128]{3,2,1,0:T(8,128)S(1)}, u32[]{:S(2)}, u32[]{:S(2)}) collective-permute-start(f32[2,4,8,128]{3,2,1,0:T(8,128)S(1)} %get-tuple-element.48.p1), channel_id=1, source_target_pairs={{0,4},{4,0},{1,5},{5,1},{2,6},{6,2},{3,7},{7,3},{8,12},{12,8},{9,1... | collective-permute-start | bytes 98312 | tf_op jit(solution)/shard_map/ppermute | solution.py:1031
  30.9 2.6 %collective-permute-start.7 = (f32[16,128]{1,0:T(8,128)S(1)}, f32[16,128]{1,0:T(8,128)S(1)}, u32[]{:S(2)}, u32[]{:S(2)}) collective-permute-start(f32[16,128]{1,0:T(8,128)S(1)} %get-tuple-element.50), channel_id=1, source_target_pairs={{0,28},{4,24},{8,4},{12,0},{16,12},{20,8},{24,20},{28,16},{1,29},{... | collective-permute-start | bytes 24584 | tf_op jit(solution)/shard_map/ppermute | solution.py:1038
  33.6 0.3 weights.1
  33.9 1.1 %collective-permute-done.6.refs_0_ = f32[16,128]{1,0:T(8,128)S(1)} collective-permute-done((f32[16,128]{1,0:T(8,128)S(1)}, f32[16,128]{1,0:T(8,128)S(1)}, u32[]{:S(2)}, u32[]{:S(2)}) %collective-permute-start.6) | collective-permute-done | bytes 8224 | tf_op jit(solution)/shard_map/ppermute | solution.py:1038
  35.0 0.2 collective-permute-done.7.refs_1_
  35.2 3.1 %all-to-all-done.1.slots1.slots = f32[32,4,4,128]{3,2,1,0:T(4,128)S(1)} async-done(((f32[32,4,4,128]{3,2,1,0:T(4,128)}), f32[32,4,4,128]{3,2,1,0:T(4,128)S(1)}, u32[]{:S(2)}, u32[]{:S(2)}) %all-to-all-start.1) | async-done | bytes 262176 | tf_op jit(solution)/shard_map/all_to_all | solution.py:1042
  38.2 1.8 %coarse.1 = (f32[2,4,8,128]{3,2,1,0:T(8,128)S(1)}, f32[2,4,8,128]{3,2,1,0:T(8,128)S(1)}) custom-call(f32[32,4,4,128]{3,2,1,0:T(4,128)S(1)} %all-to-all-done.1.slots1.slots, f32[8,2,8,128]{3,2,1,0:T(8,128)S(1)} %get-tuple-element.53.refs_0_, f32[4,2,8,128]{3,2,1,0:T(8,128)S(1)} %get-tuple-element.54.refs_1_, f32[2,2,8,128]{3,2,1,0:T(8,128)S(1)} %get-tuple-element.55.refs_2_, ...), custom_call_target="tpu_custom_call" | custom-call | tf_op jit(solution)/shard_map/coarse/pallas_call | solution.py:1026
  40.0 0.2 collective-permute-start.8
  40.2 1.0 %ortho.1 = (f32[4,8,16,128]{3,2,1,0:T(8,128)}, f32[4,4]{1,0:T(4,128)}, f32[4,4]{1,0:T(4,128)}) custom-call(f32[4,8,16,128]{3,2,1,0:T(8,128)S(1)} %copy-done, f32[4,8,16,128]{3,2,1,0:T(8,128)S(1)} %copy-done.1, f32[32,4,4,128]{3,2,1,0:T(4,128)S(1)} %all-to-all-done.slots), custom_call_target="tpu_custom_call" | custom-call | tf_op jit(solution)/shard_map/ortho/pallas_call | solution.py:1026
  41.2 1.0 %third.1 = (f32[4,10,16,128]{3,2,1,0:T(8,128)S(1)}, f32[4,10,16,128]{3,2,1,0:T(8,128)S(1)}) custom-call(f32[2,4,8,128]{3,2,1,0:T(8,128)S(1)} %get-tuple-element.48.p1, f32[2,4,8,128]{3,2,1,0:T(8,128)S(1)} %collective-permute-done.3.xl, f32[2,4,8,128]{3,2,1,0:T(8,128)S(1)} %collective-permute-done.4.xh, f32[2,4,8,128]{3,2,1,0:T(8,128)S(1)} %collective-permute-done.5.yl.yh, ...), custom_call_target="tpu_custom_call" | custom-call | tf_op jit(solution)/shard_map/third/pallas_call | solution.py:1026
  42.2 2.1 %last.1 = (f32[4,8,16,128]{3,2,1,0:T(8,128)}, f32[4,8,16,128]{3,2,1,0:T(8,128)}) custom-call(f32[2,4,8,128]{3,2,1,0:T(8,128)S(1)} %get-tuple-element.57.mine, f32[2,4,8,128]{3,2,1,0:T(8,128)S(1)} %collective-permute-done.8.other, f32[4,10,16,128]{3,2,1,0:T(8,128)S(1)} %get-tuple-element.65.G1, f32[4,10,16,128]{3,2,1,0:T(8,128)S(1)} %get-tuple-element.66.S1, ...), custom_call_target="tpu_custom_call" | custom-call | tf_op jit(solution)/shard_map/last/pallas_call | solution.py:1026
  (11 shorter events, 0.0 us)
Async XLA Ops:
  3.4 18.1 %copy-start.2 = (f32[8,16,128]{2,1,0:T(8,128)S(1)}, f32[8,16,128]{2,1,0:T(8,128)}, u32[]{:S(2)}) copy-start(f32[8,16,128]{2,1,0:T(8,128)} %c.3) | copy-start | bytes 196612
  3.5 18.1 %all-to-all-start = ((f32[32,4,4,128]{3,2,1,0:T(4,128)}), f32[32,4,4,128]{3,2,1,0:T(4,128)S(1)}, u32[]{:S(2)}, u32[]{:S(2)}) async-start(f32[32,4,4,128]{3,2,1,0:T(4,128)} %get-tuple-element.38), calls=%async_computation | async-start | bytes 524288 | tf_op jit(solution)/shard_map/all_to_all | solution.py:1042
  10.8 6.6 %collective-permute-start = (f32[13,16,128]{2,1,0:T(8,128)S(1)}, f32[13,16,128]{2,1,0:T(8,128)S(1)}, u32[]{:S(2)}, u32[]{:S(2)}) collective-permute-start(f32[13,16,128]{2,1,0:T(8,128)S(1)} %get-tuple-element.44), channel_id=1, source_target_pairs={{0,8},{8,16},{16,24},{24,0},{1,9},{9,17},{17,25},{25,1},{2,10},{10... | collective-permute-start | bytes 319496 | tf_op jit(solution)/shard_map/ppermute | solution.py:1031
  11.1 6.3 %collective-permute-start.1 = (f32[13,16,128]{2,1,0:T(8,128)S(1)}, f32[13,16,128]{2,1,0:T(8,128)S(1)}, u32[]{:S(2)}, u32[]{:S(2)}) collective-permute-start(f32[13,16,128]{2,1,0:T(8,128)S(1)} %get-tuple-element.45), channel_id=1, source_target_pairs={{0,24},{8,0},{16,8},{24,16},{1,25},{9,1},{17,9},{25,17},{2,26},{10... | collective-permute-start | bytes 319496 | tf_op jit(solution)/shard_map/ppermute | solution.py:1031
  12.6 4.8 %collective-permute-start.2 = (f32[17,8,128]{2,1,0:T(8,128)S(1)}, f32[17,8,128]{2,1,0:T(8,128)S(1)}, u32[]{:S(2)}, u32[]{:S(2)}) collective-permute-start(f32[17,8,128]{2,1,0:T(8,128)S(1)} %get-tuple-element.46), channel_id=1, source_target_pairs={{0,4},{4,0},{1,5},{5,1},{2,6},{6,2},{3,7},{7,3},{8,12},{12,8},{9,1... | collective-permute-start | bytes 208904 | tf_op jit(solution)/shard_map/ppermute | solution.py:1031
  24.8 15.4 %copy-start.1 = (f32[4,8,16,128]{3,2,1,0:T(8,128)S(1)}, f32[4,8,16,128]{3,2,1,0:T(8,128)}, u32[]{:S(2)}) copy-start(f32[4,8,16,128]{3,2,1,0:T(8,128)} %prev.1) | copy-start | bytes 786436
  24.8 13.5 %all-to-all-start.1 = ((f32[32,4,4,128]{3,2,1,0:T(4,128)}), f32[32,4,4,128]{3,2,1,0:T(4,128)S(1)}, u32[]{:S(2)}, u32[]{:S(2)}) async-start(f32[32,4,4,128]{3,2,1,0:T(4,128)} %get-tuple-element.47), calls=%async_computation.1 | async-start | bytes 524288 | tf_op jit(solution)/shard_map/all_to_all | solution.py:1042
  27.5 12.7 %copy-start = (f32[4,8,16,128]{3,2,1,0:T(8,128)S(1)}, f32[4,8,16,128]{3,2,1,0:T(8,128)}, u32[]{:S(2)}) copy-start(f32[4,8,16,128]{3,2,1,0:T(8,128)} %old.1) | copy-start | bytes 786436
  27.5 7.7 %collective-permute-start.3 = (f32[2,4,8,128]{3,2,1,0:T(8,128)S(1)}, f32[2,4,8,128]{3,2,1,0:T(8,128)S(1)}, u32[]{:S(2)}, u32[]{:S(2)}) collective-permute-start(f32[2,4,8,128]{3,2,1,0:T(8,128)S(1)} %get-tuple-element.48.p1), channel_id=1, source_target_pairs={{0,8},{8,16},{16,24},{24,0},{1,9},{9,17},{17,25},{25,1},{2,10},{10... | collective-permute-start | bytes 98312 | tf_op jit(solution)/shard_map/ppermute | solution.py:1031
  27.7 7.5 %collective-permute-start.4 = (f32[2,4,8,128]{3,2,1,0:T(8,128)S(1)}, f32[2,4,8,128]{3,2,1,0:T(8,128)S(1)}, u32[]{:S(2)}, u32[]{:S(2)}) collective-permute-start(f32[2,4,8,128]{3,2,1,0:T(8,128)S(1)} %get-tuple-element.48.p1), channel_id=1, source_target_pairs={{0,24},{8,0},{16,8},{24,16},{1,25},{9,1},{17,9},{25,17},{2,26},{10... | collective-permute-start | bytes 98312 | tf_op jit(solution)/shard_map/ppermute | solution.py:1031
  29.3 5.9 %collective-permute-start.5 = (f32[2,4,8,128]{3,2,1,0:T(8,128)S(1)}, f32[2,4,8,128]{3,2,1,0:T(8,128)S(1)}, u32[]{:S(2)}, u32[]{:S(2)}) collective-permute-start(f32[2,4,8,128]{3,2,1,0:T(8,128)S(1)} %get-tuple-element.48.p1), channel_id=1, source_target_pairs={{0,4},{4,0},{1,5},{5,1},{2,6},{6,2},{3,7},{7,3},{8,12},{12,8},{9,1... | collective-permute-start | bytes 98312 | tf_op jit(solution)/shard_map/ppermute | solution.py:1031
  30.9 4.1 %collective-permute-start.6 = (f32[16,128]{1,0:T(8,128)S(1)}, f32[16,128]{1,0:T(8,128)S(1)}, u32[]{:S(2)}, u32[]{:S(2)}) collective-permute-start(f32[16,128]{1,0:T(8,128)S(1)} %get-tuple-element.49), channel_id=1, source_target_pairs={{0,12},{4,8},{8,20},{12,16},{16,28},{20,24},{24,4},{28,0},{1,13},{... | collective-permute-start | bytes 24584 | tf_op jit(solution)/shard_map/ppermute | solution.py:1038
  30.9 4.2 %collective-permute-start.7 = (f32[16,128]{1,0:T(8,128)S(1)}, f32[16,128]{1,0:T(8,128)S(1)}, u32[]{:S(2)}, u32[]{:S(2)}) collective-permute-start(f32[16,128]{1,0:T(8,128)S(1)} %get-tuple-element.50), channel_id=1, source_target_pairs={{0,28},{4,24},{8,4},{12,0},{16,12},{20,8},{24,20},{28,16},{1,29},{... | collective-permute-start | bytes 24584 | tf_op jit(solution)/shard_map/ppermute | solution.py:1038
  40.0 2.2 %collective-permute-start.8 = (f32[2,4,8,128]{3,2,1,0:T(8,128)S(1)}, f32[2,4,8,128]{3,2,1,0:T(8,128)S(1)}, u32[]{:S(2)}, u32[]{:S(2)}) collective-permute-start(f32[2,4,8,128]{3,2,1,0:T(8,128)S(1)} %get-tuple-element.58), channel_id=1, source_target_pairs={{0,8},{8,0},{16,24},{24,16},{1,9},{9,1},{17,25},{25,17},{2,10},{10... | collective-permute-start | bytes 98312 | tf_op jit(solution)/shard_map/ppermute | solution.py:1229
